TPU v7x, 256 devices: a whole 4x4x8 slice. The times are simulated.
256 devices in a mesh: band: 64 (over z, y, core), field: 4 (over x).
Axes of the slice: x: 4, y: 4, z: 8, core: 2. Of those that a mesh axis runs over, the one named last changes fastest.
Arguments:
- right_side: float32 [640, 2, 4, 12, 640], P('band', None, 'field'), may hold values from -40 to 40
- legendre: bfloat16 [640, 640, 640], P('band'), may hold values from -0.25 to 0.25
- wave_map: int32 [640], replicated, may hold values from 0 to 639, as said below
- obs_weight: float32 [640, 1280], P('band'), may hold values from 0.2 to 5
Outputs:
- solution: float32 [640, 2, 4, 12, 640], P('band', None, 'field')
- residual: float32 [640, 2, 4, 12, 640], P('band', None, 'field')
Inputs may be any that keep to these rules, and one draw needn't show every extreme that they name: A permutation of 0 to 639; wave_map[s] lies in the same aligned block of 20 values as 639-s.
All inputs are finite; a program needn't handle non-finite values.
Results may differ from a plain program's by a relative error of at most 0.03.
Values may be sent and summed in bfloat16 or wider, within the bound.
No kernel may reach another device: no remote copies, remote signals or barrier semaphores. Data moves between devices by JAX's collectives and lax.ppermute only.
A program may use at most 128 MiB of HBM per device.

v0:
```python
import functools
import math

import jax
import jax.numpy as jnp
from jax import lax
from jax.sharding import Mesh
from jax.sharding import PartitionSpec as P

ITERS = 3
BAND_FIELD = ("band_0", "band_1", "band_2", "field")
BAND = ("band_0", "band_1", "band_2")


def by_axis(array, axes):
    return functools.reduce(lax.psum, axes, array)


def triangle_of(own_waves, degrees):
    return (jnp.arange(degrees, dtype=jnp.int32)[None, :] >= own_waves[:, None]).astype(jnp.float32)


def fourier_of(wave_map, lon_count):
    longitude = jnp.arange(lon_count, dtype=jnp.int32)
    phase_int = wave_map[:, None] * longitude[None, :] % lon_count
    angles = phase_int.astype(jnp.float32) * (2.0 * math.pi / lon_count)
    norm_factor = 1.0 / math.sqrt(wave_map.shape[0])
    return (jnp.stack([jnp.cos(angles), -jnp.sin(angles)], axis=1) * norm_factor).astype(
        jnp.bfloat16
    )


def grid_round(spread, fourier_flat, obs_weight):
    slots, parts, items, single, lat_rows = spread.shape
    flat = spread.reshape(slots * parts, items * single * lat_rows)
    grid_vals = lax.dot_general(
        flat, fourier_flat, (((0,), (0,)), ((), ())), preferred_element_type=jnp.float32
    )
    grid_vals = (
        grid_vals.reshape(items * single, lat_rows, fourier_flat.shape[1]) * obs_weight[None, :, :]
    )
    weighted = grid_vals.astype(jnp.bfloat16).reshape(
        items * single * lat_rows, fourier_flat.shape[1]
    )
    returned = lax.dot_general(
        fourier_flat, weighted, (((1,), (1,)), ((), ())), preferred_element_type=jnp.float32
    ).astype(jnp.bfloat16)
    return returned.reshape(slots, parts, items, single, lat_rows)


def legendre_back(returned, legendre):
    return lax.dot_general(
        returned, legendre, (((4,), (2,)), ((0,), (0,))), preferred_element_type=jnp.float32
    )


def paired_sums(residual, image_vec):
    return (
        by_axis(jnp.sum(residual * residual), BAND_FIELD),
        by_axis(jnp.sum(residual * image_vec), BAND_FIELD),
    )


def on_device(right_side, legendre, wave_map, obs_weight):
    slot_count = legendre.shape[0]
    band_count = lax.axis_size(BAND)
    lat_rows = obs_weight.shape[0]
    first_slot = lax.axis_index(BAND) * slot_count
    own_waves = lax.dynamic_slice_in_dim(wave_map, first_slot, slot_count)
    triangle = triangle_of(own_waves, right_side.shape[4])
    fourier_table = fourier_of(wave_map, obs_weight.shape[1])
    fourier_flat = fourier_table.reshape(2 * fourier_table.shape[0], fourier_table.shape[2])
    triangle_five = triangle[:, None, None, None, :]
    field_count = right_side.shape[2]
    level_count = right_side.shape[3]
    merged = field_count * level_count

    def operate(vector):
        masked_bf = (vector * triangle_five).astype(jnp.bfloat16)
        coeffs = lax.dot_general(
            masked_bf, legendre, (((4,), (1,)), ((0,), (0,))), preferred_element_type=jnp.float32
        ).astype(jnp.bfloat16)
        outgoing = coeffs.reshape(slot_count, 2, merged, band_count, lat_rows)
        spread = lax.all_to_all(outgoing, BAND, split_axis=3, concat_axis=0, tiled=True)
        returned = grid_round(spread, fourier_flat, obs_weight)
        returned_home = lax.all_to_all(returned, BAND, split_axis=0, concat_axis=3, tiled=True)
        home = returned_home.reshape(slot_count, 2, field_count, level_count, band_count * lat_rows)
        adjoint = legendre_back(home, legendre)
        return vector + triangle_five * adjoint

    residual = right_side * triangle_five
    solution = jnp.zeros_like(residual)
    image_vec = operate(residual)
    norm_now, product = paired_sums(residual, image_vec)
    step_length = norm_now / product
    direction = residual
    along = image_vec
    for iteration in range(ITERS):
        solution = solution + step_length * direction
        residual = residual - step_length * along
        if iteration + 1 < ITERS:
            image_vec = operate(residual)
            norm_next, product = paired_sums(residual, image_vec)
            beta_ratio = norm_next / norm_now
            step_length = norm_next / (product - beta_ratio * norm_next / step_length)
            direction = residual + beta_ratio * direction
            along = image_vec + beta_ratio * along
            norm_now = norm_next
    return (solution, residual)


def solution(mesh):
    split = Mesh(
        mesh.devices.reshape(8, 4, 2, mesh.shape["field"]), ("band_0", "band_1", "band_2", "field")
    )
    return jax.shard_map(
        on_device,
        mesh=split,
        in_specs=(P(BAND, None, "field", None, None), P(BAND, None, None), P(), P(BAND, None)),
        out_specs=(P(BAND, None, "field", None, None), P(BAND, None, "field", None, None)),
        check_vma=False,
    )
```

profile of v0, /device:TPU:1, one launch (start us, length us, event | category | flops | bytes accessed | tf_op | source)
XLA Modules:
  0.0 736.9 jit_solution(9783474237335254011)
XLA Ops:
  1.5 4.9 fusion.49
  6.4 9.7 %reshape.240 = bf16[10,2,12,64,10]{4,3,2,1,0:T(8,128)(2,1)} reshape(bf16[10,2,12,640]{3,2,1,0:T(8,128)(2,1)S(1)} %fusion.49) | data formatting | bytes 614400 | tf_op jit(solution)/shard_map/reshape | solution.py:83
  16.1 14.1 %copy.117 = bf16[10,2,12,64,10]{2,1,4,0,3:T(2,128)(2,1)S(1)} copy(bf16[10,2,12,64,10]{4,3,2,1,0:T(8,128)(2,1)} %reshape.240) | data formatting | bytes 614400 | tf_op jit(solution)/shard_map/reshape | solution.py:83
  30.2 4.4 reshape.247
  34.6 13.5 %all-to-all-start = ((bf16[64,2,1200]{2,1,0:T(2,128)(2,1)}), bf16[64,2,1200]{2,1,0:T(2,128)(2,1)}, u32[]{:S(2)}, u32[]{:S(2)}) async-start(bf16[64,2,1200]{2,1,0:T(2,128)(2,1)} %reshape.247), calls=%async_computation | async-start | bytes 655360 | tf_op jit(solution)/shard_map/all_to_all | solution.py:84
  48.1 13.8 %fusion.17 = (f32[640,1,1280]{2,0,1:T(8,128)S(1)}, f32[640,1,1280]{2,0,1:T(8,128)S(1)}) fusion(s32[640]{0:T(1024)S(1)} %copy-done.2), kind=kLoop, calls=%fused_computation.21 | loop fusion | flops 8192000 | bytes 6556160 | tf_op jit(solution)/shard_map/cos | solution.py:28
  72.6 7.8 %reshape.248 = bf16[64,10,10,2,12]{4,3,2,1,0:T(2,128)(2,1)S(1)} reshape(bf16[64,2,1200]{2,1,0:T(2,128)(2,1)} %all-to-all-done) | data formatting | bytes 614400
  84.4 13.4 %copy.118 = bf16[64,10,2,12,1,10]{5,3,2,1,0,4:T(8,128)(2,1)} copy(bf16[64,10,2,12,1,10]{3,2,5,1,0,4:T(2,128)(2,1)} %bitcast_bitcast_fusion.2) | data formatting | bytes 614400 | tf_op jit(solution)/shard_map/all_to_all | solution.py:84
  97.8 6.4 reshape.222
  115.1 5.8 reshape.224
  120.9 12.1 %copy.123 = bf16[640,2,12,1,10]{2,1,4,3,0:T(2,128)(2,1)S(1)} copy(bf16[640,2,12,1,10]{4,2,1,0,3:T(8,128)(2,1)} %reshape.224) | data formatting | bytes 614400 | tf_op jit(solution)/shard_map/reshape | solution.py:48
  133.0 4.4 reshape.249
  137.4 24.8 %all_to_all.90 = bf16[64,2,1200]{2,1,0:T(2,128)(2,1)} all-to-all(bf16[64,2,1200]{2,1,0:T(2,128)(2,1)} %reshape.249), channel_id=1, replica_groups=mesh['band_0'=8,'band_1'=4,'band_2'=2,'field'=4] {'band_0','band_1','ban..., dimensions={0} | all-to-all | bytes 614400 | tf_op jit(solution)/shard_map/all_to_all | solution.py:86
  162.2 7.8 %reshape.250 = bf16[640,1,10,2,12]{4,3,2,1,0:T(2,128)(2,1)S(1)} reshape(bf16[64,2,1200]{2,1,0:T(2,128)(2,1)} %all_to_all.90) | data formatting | bytes 614400
  170.0 17.5 %copy.154 = bf16[64,10,2,12,1,10]{1,0,2,5,3,4:T(8,128)(2,1)} copy(bf16[64,10,2,12,1,10]{3,2,5,1,0,4:T(2,128)(2,1)S(1)} %bitcast.136) | data formatting | bytes 614400 | tf_op jit(solution)/shard_map/all_to_all | solution.py:86
  187.5 12.6 %copy.155 = bf16[10,2,12,64,1,10]{5,3,2,1,0,4:T(8,128)(2,1)} copy(bf16[10,2,12,64,1,10]{0,3,1,5,2,4:T(8,128)(2,1)} %bitcast.132) | data formatting | bytes 614400 | tf_op jit(solution)/shard_map/reshape.6
  200.1 6.7 reshape.242
  206.8 6.5 fusion.66
  213.3 12.5 %all-reduce.2 = (f32[]{:T(128)}, f32[]{:T(128)}) all-reduce(f32[]{:T(128)} %get-tuple-element.17, f32[]{:T(128)} %get-tuple-element.16), channel_id=1, replica_groups=mesh['band_0'=8,'band_1'=4,'band_2'=2,'field'=4] {'band_0'}, use_global_device_ids=true, to_apply=%region_1.2 | all-reduce | flops 2 | bytes 16 | tf_op jit(solution)/shard_map/psum | solution.py:16
  225.8 7.3 all-reduce.8
  233.1 9.4 %all-reduce.11 = (f32[]{:T(128)}, f32[]{:T(128)}) all-reduce(f32[]{:T(128)} %get-tuple-element.34, f32[]{:T(128)} %get-tuple-element.35), channel_id=1, replica_groups=mesh['band_0'=8,'band_1'=4,'band_2'=2,'field'=4] {'band_2'}, use_global_device_ids=true, to_apply=%region_3.4 | all-reduce | flops 2 | bytes 16 | tf_op jit(solution)/shard_map/psum | solution.py:16
  242.5 9.4 %all-reduce.5 = (f32[]{:T(128)}, f32[]{:T(128)}) all-reduce(f32[]{:T(128)} %get-tuple-element.40, f32[]{:T(128)} %get-tuple-element.41), channel_id=1, replica_groups=mesh['band_0'=8,'band_1'=4,'band_2'=2,'field'=4] {'field'}, use_global_device_ids=true, to_apply=%region_4.5 | all-reduce | flops 2 | bytes 16 | tf_op jit(solution)/shard_map/psum | solution.py:16
  253.3 4.7 fusion.52
  258.0 9.7 %reshape.243 = bf16[10,2,12,64,10]{4,3,2,1,0:T(8,128)(2,1)} reshape(bf16[10,2,12,640]{3,2,1,0:T(8,128)(2,1)S(1)} %fusion.52) | data formatting | bytes 614400 | tf_op jit(solution)/shard_map/reshape | solution.py:83
  267.8 14.6 %copy.128 = bf16[10,2,12,64,10]{2,1,4,0,3:T(2,128)(2,1)} copy(bf16[10,2,12,64,10]{4,3,2,1,0:T(8,128)(2,1)} %reshape.243) | data formatting | bytes 614400 | tf_op jit(solution)/shard_map/reshape | solution.py:83
  282.3 7.0 reshape.251
  289.3 22.1 %all_to_all.91 = bf16[64,2,1200]{2,1,0:T(2,128)(2,1)S(1)} all-to-all(bf16[64,2,1200]{2,1,0:T(2,128)(2,1)S(1)} %reshape.251), channel_id=1, replica_groups=mesh['band_0'=8,'band_1'=4,'band_2'=2,'field'=4] {'band_0','band_1','ban..., dimensions={0} | all-to-all | bytes 614400 | tf_op jit(solution)/shard_map/all_to_all | solution.py:84
  315.3 5.9 bitcast_bitcast_fusion.1
  321.3 13.2 %copy.129 = bf16[64,10,2,12,1,10]{5,3,2,1,0,4:T(8,128)(2,1)} copy(bf16[64,10,2,12,1,10]{3,2,5,1,0,4:T(2,128)(2,1)} %bitcast_bitcast_fusion.1) | data formatting | bytes 614400 | tf_op jit(solution)/shard_map/all_to_all | solution.py:84
  334.5 6.4 reshape.228
  350.0 5.7 reshape.230
  355.7 12.7 %copy.134 = bf16[640,2,12,1,10]{2,1,4,3,0:T(2,128)(2,1)} copy(bf16[640,2,12,1,10]{4,2,1,0,3:T(8,128)(2,1)} %reshape.230) | data formatting | bytes 614400 | tf_op jit(solution)/shard_map/reshape | solution.py:48
  368.4 7.0 reshape.253
  375.4 19.2 %all_to_all.92 = bf16[64,2,1200]{2,1,0:T(2,128)(2,1)S(1)} all-to-all(bf16[64,2,1200]{2,1,0:T(2,128)(2,1)S(1)} %reshape.253), channel_id=1, replica_groups=mesh['band_0'=8,'band_1'=4,'band_2'=2,'field'=4] {'band_0','band_1','ban..., dimensions={0} | all-to-all | bytes 614400 | tf_op jit(solution)/shard_map/all_to_all | solution.py:86
  398.5 15.4 %copy.158 = bf16[64,10,2,12,1,10]{1,0,2,5,3,4:T(8,128)(2,1)} copy(bf16[64,10,2,12,1,10]{3,2,5,1,0,4:T(2,128)(2,1)} %bitcast.138) | data formatting | bytes 614400 | tf_op jit(solution)/shard_map/all_to_all | solution.py:86
  413.9 12.6 %copy.159 = bf16[10,2,12,64,1,10]{5,3,2,1,0,4:T(8,128)(2,1)} copy(bf16[10,2,12,64,1,10]{0,3,1,5,2,4:T(8,128)(2,1)} %bitcast.133) | data formatting | bytes 614400 | tf_op jit(solution)/shard_map/reshape.12
  426.6 6.6 reshape.244
  433.2 7.5 %multiply_reduce_fusion.2 = (f32[]{:T(128)}, f32[]{:T(128)}, f32[10,2,1,12,640]{4,3,1,0,2:T(8,128)}) fusion(f32[10,2,1,12,640]{4,3,1,0,2:T(8,128)S(1)} %fusion.59, bf16[10,2,12,640]{3,2,1,0:T(8,128)(2,1)S(1)} %reshape.244, bf16[10,640,640]{2,1,0:T(8,128)(2,1)} %param.5, f32[10,640]{1,0:T(8,128)S(1)} %fusion.82), kind=kOutput, calls=%fused_computation.63 | convolution fusion | flops 197529600 | bytes 9753608 | tf_op jit(solution)/shard_map/dot_general | solution.py:52
  440.6 12.5 %all-reduce.1 = (f32[]{:T(128)}, f32[]{:T(128)}) all-reduce(f32[]{:T(128)} %get-tuple-element.15, f32[]{:T(128)} %get-tuple-element.14), channel_id=1, replica_groups=mesh['band_0'=8,'band_1'=4,'band_2'=2,'field'=4] {'band_0'}, use_global_device_ids=true, to_apply=%region_11.12 | all-reduce | flops 2 | bytes 16 | tf_op jit(solution)/shard_map/psum | solution.py:16
  453.2 7.3 all-reduce.7
  460.5 9.5 %all-reduce.10 = (f32[]{:T(128)}, f32[]{:T(128)}) all-reduce(f32[]{:T(128)} %get-tuple-element.32, f32[]{:T(128)} %get-tuple-element.33), channel_id=1, replica_groups=mesh['band_0'=8,'band_1'=4,'band_2'=2,'field'=4] {'band_2'}, use_global_device_ids=true, to_apply=%region_13.14 | all-reduce | flops 2 | bytes 16 | tf_op jit(solution)/shard_map/psum | solution.py:16
  469.9 6.7 all-reduce.4
  482.5 5.5 fusion.55
  488.0 10.4 %reshape.245 = bf16[10,2,12,64,10]{4,3,2,1,0:T(8,128)(2,1)} reshape(bf16[10,2,12,640]{3,2,1,0:T(8,128)(2,1)} %fusion.55) | data formatting | bytes 614400 | tf_op jit(solution)/shard_map/reshape | solution.py:83
  498.4 14.6 %copy.139 = bf16[10,2,12,64,10]{2,1,4,0,3:T(2,128)(2,1)} copy(bf16[10,2,12,64,10]{4,3,2,1,0:T(8,128)(2,1)} %reshape.245) | data formatting | bytes 614400 | tf_op jit(solution)/shard_map/reshape | solution.py:83
  513.0 7.6 %reshape.255 = bf16[64,2,1200]{2,1,0:T(2,128)(2,1)} reshape(bf16[64,10,10,2,12]{4,3,2,1,0:T(2,128)(2,1)} %bitcast.139) | data formatting | bytes 614400
  520.6 21.8 %all_to_all.93 = bf16[64,2,1200]{2,1,0:T(2,128)(2,1)} all-to-all(bf16[64,2,1200]{2,1,0:T(2,128)(2,1)} %reshape.255), channel_id=1, replica_groups=mesh['band_0'=8,'band_1'=4,'band_2'=2,'field'=4] {'band_0','band_1','ban..., dimensions={0} | all-to-all | bytes 614400 | tf_op jit(solution)/shard_map/all_to_all | solution.py:84
  542.4 8.6 %reshape.256 = bf16[64,10,10,2,12]{4,3,2,1,0:T(2,128)(2,1)} reshape(bf16[64,2,1200]{2,1,0:T(2,128)(2,1)} %all_to_all.93) | data formatting | bytes 614400
  551.0 5.9 bitcast_bitcast_fusion
  556.9 13.2 %copy.140 = bf16[64,10,2,12,1,10]{5,3,2,1,0,4:T(8,128)(2,1)} copy(bf16[64,10,2,12,1,10]{3,2,5,1,0,4:T(2,128)(2,1)} %bitcast_bitcast_fusion) | data formatting | bytes 614400 | tf_op jit(solution)/shard_map/all_to_all | solution.py:84
  570.1 7.1 reshape.234
  592.2 6.7 reshape.236
  598.8 12.7 %copy.145 = bf16[640,2,12,1,10]{2,1,4,3,0:T(2,128)(2,1)} copy(bf16[640,2,12,1,10]{4,2,1,0,3:T(8,128)(2,1)} %reshape.236) | data formatting | bytes 614400 | tf_op jit(solution)/shard_map/reshape | solution.py:48
  611.5 7.6 %reshape.257 = bf16[64,2,1200]{2,1,0:T(2,128)(2,1)} reshape(bf16[640,1,10,2,12]{4,3,2,1,0:T(2,128)(2,1)} %bitcast.143) | data formatting | bytes 614400
  619.1 19.6 %all_to_all.94 = bf16[64,2,1200]{2,1,0:T(2,128)(2,1)} all-to-all(bf16[64,2,1200]{2,1,0:T(2,128)(2,1)} %reshape.257), channel_id=1, replica_groups=mesh['band_0'=8,'band_1'=4,'band_2'=2,'field'=4] {'band_0','band_1','ban..., dimensions={0} | all-to-all | bytes 614400 | tf_op jit(solution)/shard_map/all_to_all | solution.py:86
  638.7 8.6 %reshape.258 = bf16[640,1,10,2,12]{4,3,2,1,0:T(2,128)(2,1)} reshape(bf16[64,2,1200]{2,1,0:T(2,128)(2,1)} %all_to_all.94) | data formatting | bytes 614400
  647.3 15.4 %copy.162 = bf16[64,10,2,12,1,10]{1,0,2,5,3,4:T(8,128)(2,1)} copy(bf16[64,10,2,12,1,10]{3,2,5,1,0,4:T(2,128)(2,1)} %bitcast.140) | data formatting | bytes 614400 | tf_op jit(solution)/shard_map/all_to_all | solution.py:86
  662.8 12.7 %copy.163 = bf16[10,2,12,64,1,10]{5,3,2,1,0,4:T(8,128)(2,1)} copy(bf16[10,2,12,64,1,10]{0,3,1,5,2,4:T(8,128)(2,1)} %bitcast.134) | data formatting | bytes 614400 | tf_op jit(solution)/shard_map/reshape.18
  675.4 7.3 reshape.246
  682.7 7.6 %multiply_reduce_fusion = (f32[]{:T(128)}, f32[]{:T(128)}, f32[10,2,1,12,640]{4,3,1,0,2:T(8,128)}) fusion(f32[10,2,1,12,640]{4,3,1,0,2:T(8,128)S(1)} %multiply_subtract_fusion.1, bf16[10,2,12,640]{3,2,1,0:T(8,128)(2,1)} %reshape.246, bf16[10,640,640]{2,1,0:T(8,128)(2,1)} %param.5, f32[10,640]{1,0:T(8,128)S(1)} %fusion.82), kind=kOutput, calls=%fused_computation.58 | convolution fusion | flops 197529600 | bytes 9753608 | tf_op jit(solution)/shard_map/dot_general | solution.py:52
  690.2 12.5 %all-reduce = (f32[]{:T(128)}, f32[]{:T(128)}) all-reduce(f32[]{:T(128)} %get-tuple-element.13, f32[]{:T(128)} %get-tuple-element.12), channel_id=1, replica_groups=mesh['band_0'=8,'band_1'=4,'band_2'=2,'field'=4] {'band_0'}, use_global_device_ids=true, to_apply=%region_21.22 | all-reduce | flops 2 | bytes 16 | tf_op jit(solution)/shard_map/psum | solution.py:16
  702.7 7.3 all-reduce.6
  710.0 9.4 %all-reduce.9 = (f32[]{:T(128)}, f32[]{:T(128)}) all-reduce(f32[]{:T(128)} %get-tuple-element.30, f32[]{:T(128)} %get-tuple-element.31), channel_id=1, replica_groups=mesh['band_0'=8,'band_1'=4,'band_2'=2,'field'=4] {'band_2'}, use_global_device_ids=true, to_apply=%region_23.24 | all-reduce | flops 2 | bytes 16 | tf_op jit(solution)/shard_map/psum | solution.py:16
  719.4 8.3 %all-reduce.3 = (f32[]{:T(128)}, f32[]{:T(128)}) all-reduce(f32[]{:T(128)} %get-tuple-element.36, f32[]{:T(128)} %get-tuple-element.37), channel_id=1, replica_groups=mesh['band_0'=8,'band_1'=4,'band_2'=2,'field'=4] {'field'}, use_global_device_ids=true, to_apply=%region_24.25 | all-reduce | flops 2 | bytes 16 | tf_op jit(solution)/shard_map/psum | solution.py:16
  (44 shorter events, 64.4 us)
Async XLA Ops:
  30.2 17.9 %copy-start.2 = (s32[640]{0:T(1024)S(1)}, s32[640]{0:T(1024)}, u32[]{:S(2)}) copy-start(s32[640]{0:T(1024)} %param.6) | copy-start | bytes 7684
  34.6 38.0 %all-to-all-start = ((bf16[64,2,1200]{2,1,0:T(2,128)(2,1)}), bf16[64,2,1200]{2,1,0:T(2,128)(2,1)}, u32[]{:S(2)}, u32[]{:S(2)}) async-start(bf16[64,2,1200]{2,1,0:T(2,128)(2,1)} %reshape.247), calls=%async_computation | async-start | bytes 655360 | tf_op jit(solution)/shard_map/all_to_all | solution.py:84
  97.8 7.5 %copy-start.3 = (f32[10,1280]{1,0:T(8,128)S(1)}, f32[10,1280]{1,0:T(8,128)}, u32[]{:S(2)}) copy-start(f32[10,1280]{1,0:T(8,128)} %param.7) | copy-start | bytes 153604
  105.3 5.7 copy-start.1
  200.1 6.7 copy-start
where the time goes:
time: 747 us; the launch traced here: 737 us
  local copies, waits for them, and re-layouts  419 us (56%)
  blocking collectives  219 us (29%)
  matrix products  55.6 us (7%)
  other arithmetic  18 us (2%)
  starting transfers between devices  13.5 us (2%)
  between operations  11.1 us (1%)
    psum x12, blocking collectives, by_axis(): return functools.reduce(lax.psum, axes, array)  112 us
    unnamed x22, local copies, waits for them, and re-layouts  81.6 us
    reshape x6, local copies, waits for them, and re-layouts, operate(): outgoing = coeffs.reshape(slot_count, 2, merged, band_count, lat_rows)  73.1 us
    all_to_all x3, blocking collectives, operate(): lax.all_to_all(returned, BAND, split_axis=0, concat_axis=3, tiled=True)  63.6 us
    another operation x6, local copies, waits for them, and re-layouts  58.5 us
    all_to_all x6, local copies, waits for them, and re-layouts, operate(): lax.all_to_all(outgoing, BAND, split_axis=3, concat_axis=0, tiled=True)  55.7 us
    reshape x6, local copies, waits for them, and re-layouts, grid_round(): return returned.reshape(slots, parts, items, single, lat_rows)  55.6 us
    all_to_all x3, local copies, waits for them, and re-layouts, operate(): lax.all_to_all(returned, BAND, split_axis=0, concat_axis=3, tiled=True)  48.3 us
  transfers between devices with their start and end apart: 1, of which 0 were waited for; matrix products, arithmetic and copies ran while one was open for 3% of the time, Pallas kernels for 0%

commit v1 on v0

v1 whole, which is shorter than its diff:
```python
import functools
import math

import jax
import jax.numpy as jnp
from jax import lax
from jax.experimental import pallas as pl
from jax.experimental.pallas import tpu as pltpu
from jax.sharding import Mesh
from jax.sharding import PartitionSpec as P

ZS, YS, CS, XS = 8, 4, 2, 4
BAND = ("z", "y", "c")
EXCHANGE = ("z", "c", "y")
GROUPS = 3
PIECE = 40
PIECES = 16
SUB = 8
LANES = 128
SPARE = GROUPS * PIECE
F32 = jnp.float32
BF16 = jnp.bfloat16


def lane_of(rows=SUB):
    return lax.broadcasted_iota(jnp.int32, (rows, LANES), 1)


def scatter_rows(value, acc_ref, slot, chunk_rows, slots):
    lane = lane_of()
    for piece in range(PIECES):
        first = piece * PIECE
        tile, offset = first // LANES, first % LANES
        out = jnp.zeros((SUB, LANES), F32)
        for group in reversed(range(GROUPS)):
            rows = slice(group * SUB, (group + 1) * SUB)
            source = value[rows, tile * LANES : (tile + 1) * LANES]
            if offset + PIECE > LANES:
                following = value[rows, (tile + 1) * LANES : (tile + 2) * LANES]
                source = jnp.where(lane >= offset, source, following)
            shift = (group * PIECE - offset) % LANES
            if shift:
                source = pltpu.roll(source, shift, 1)
            out = jnp.where(lane < (group + 1) * PIECE, source, out)
        acc_ref[pl.ds(piece * YS * chunk_rows + slot, SUB, stride=slots), :] = out


def gather_rows(held_ref, slot, chunk_rows, slots, lat_tiles):
    lane = lane_of()
    tiles = [[None] * lat_tiles for _ in range(GROUPS)]
    for piece in range(PIECES):
        first = piece * PIECE
        tile, offset = first // LANES, first % LANES
        rows = held_ref[pl.ds(piece * YS * chunk_rows + slot, SUB, stride=slots), :]
        for group in range(GROUPS):
            shift = (offset - group * PIECE) % LANES
            moved = pltpu.roll(rows, shift, 1) if shift else rows
            known = tiles[group][tile]
            tiles[group][tile] = moved if known is None else jnp.where(lane >= offset, moved, known)
            if offset + PIECE > LANES:
                tiles[group][tile + 1] = moved
    return jnp.concatenate([jnp.concatenate(row, axis=1) for row in tiles], axis=0)


def square_sum(parts):
    total = None
    for part in parts:
        for group in range(GROUPS):
            block = part[group * SUB : (group + 1) * SUB, :]
            total = block * block if total is None else total + block * block
    return total


def triangle_tile(wave, tile):
    return lane_of(GROUPS * SUB) + tile * LANES >= wave


def first_kernel(slots, chunk_rows, waves_ref, vec_ref, leg_ref, res_ref, out_ref, norm_ref, acc_ref):
    slot = pl.program_id(0)
    wave = waves_ref[slot]
    tiles = vec_ref.shape[2] // LANES
    parts = []
    for tile in range(tiles):
        cols = slice(tile * LANES, (tile + 1) * LANES)
        parts.append(jnp.where(triangle_tile(wave, tile), vec_ref[0, :, cols], 0.0))
        res_ref[0, :, cols] = parts[-1]

    @pl.when(slot == 0)
    def _():
        norm_ref[...] = jnp.zeros_like(norm_ref)

    norm_ref[...] += square_sum(parts)
    forward(jnp.concatenate(parts, axis=1), leg_ref, acc_ref, out_ref, slot, slots, chunk_rows)


def forward(vector, leg_ref, acc_ref, out_ref, slot, slots, chunk_rows):
    coeffs = jnp.dot(vector.astype(BF16), leg_ref[0], preferred_element_type=F32)
    scatter_rows(coeffs, acc_ref, slot, chunk_rows, slots)

    @pl.when(slot == slots - 1)
    def _():
        out_ref[...] = acc_ref[...].astype(BF16)


def sums_of(sum_refs, chunk_rows):
    total = sum_refs[0][...]
    for ref in sum_refs[1:]:
        total = total + ref[...]
    total = total * (1.0 / chunk_rows)
    lane = lane_of()
    norm = jnp.sum(jnp.where((lane >= SPARE) & (lane < SPARE + 3), total, 0.0), axis=(0, 1), keepdims=True)
    energy = jnp.sum(jnp.where((lane >= SPARE + 3) & (lane < SPARE + 6), total, 0.0), axis=(0, 1), keepdims=True)
    return norm, norm + energy


def image_of(vec_refs, held_ref, leg_ref, wave, slot, slots, chunk_rows):
    tiles = leg_ref.shape[2] // LANES
    home = gather_rows(held_ref, slot, chunk_rows, slots, tiles).astype(BF16)
    adjoint = lax.dot_general(home, leg_ref[0], (((1,), (1,)), ((), ())), preferred_element_type=F32)
    image = []
    for tile in range(leg_ref.shape[1] // LANES):
        cols = slice(tile * LANES, (tile + 1) * LANES)
        image.append(vec_refs[0, :, cols] + jnp.where(triangle_tile(wave, tile), adjoint[:, cols], 0.0))
    return image


def scalar_row(value):
    return jnp.broadcast_to(value, (1, LANES))


def middle_kernel(stage, slots, chunk_rows, *refs):
    waves_ref, home_ref, leg_ref, sum_a, sum_b, sum_c, sum_d, past_ref, *refs = refs
    if stage == 0:
        res_ref, new_ref, along_ref, out_ref, norm_ref, hist_ref, acc_ref, held_ref = refs
    else:
        res_ref, last_ref, new_ref, along_ref, out_ref, norm_ref, hist_ref, acc_ref, held_ref = refs
    slot = pl.program_id(0)
    wave = waves_ref[slot]

    @pl.when(slot == 0)
    def _():
        held_ref[...] = home_ref[...].astype(F32)
        norm, product = sums_of((sum_a, sum_b, sum_c, sum_d), chunk_rows)
        hist_ref[...] = jnp.zeros_like(hist_ref)
        if stage == 0:
            alpha = norm / product
            beta = jnp.zeros_like(norm)
            hist_ref[2:3, :] = scalar_row(alpha)
        else:
            beta = norm / past_ref[0:1, 0:1]
            alpha = norm / (product - beta * norm / past_ref[1:2, 0:1])
            hist_ref[2:3, :] = past_ref[2:3, :]
            hist_ref[3:4, :] = scalar_row(alpha)
        hist_ref[0:1, :] = scalar_row(norm)
        hist_ref[1:2, :] = scalar_row(alpha)
        hist_ref[4:5, :] = scalar_row(beta)
        norm_ref[...] = jnp.zeros_like(norm_ref)

    alpha = hist_ref[1:2, :]
    beta = hist_ref[4:5, :]
    image = image_of(res_ref, held_ref, leg_ref, wave, slot, slots, chunk_rows)
    parts = []
    for tile, along in enumerate(image):
        cols = slice(tile * LANES, (tile + 1) * LANES)
        if stage > 0:
            along = along + beta * last_ref[0, :, cols]
        along_ref[0, :, cols] = along
        part = res_ref[0, :, cols] - alpha * along
        new_ref[0, :, cols] = part
        parts.append(part)
    norm_ref[...] += square_sum(parts)
    forward(jnp.concatenate(parts, axis=1), leg_ref, acc_ref, out_ref, slot, slots, chunk_rows)


def last_kernel(slots, chunk_rows, *refs):
    waves_ref, home_ref, leg_ref, sum_a, sum_b, sum_c, sum_d, past_ref, *refs = refs
    res0_ref, res1_ref, res2_ref, last_ref, sol_ref, fin_ref, hist_ref, held_ref = refs
    slot = pl.program_id(0)
    wave = waves_ref[slot]

    @pl.when(slot == 0)
    def _():
        held_ref[...] = home_ref[...].astype(F32)
        norm, product = sums_of((sum_a, sum_b, sum_c, sum_d), chunk_rows)
        beta = norm / past_ref[0:1, 0:1]
        alpha = norm / (product - beta * norm / past_ref[1:2, 0:1])
        hist_ref[0:1, :] = scalar_row(alpha)
        hist_ref[1:2, :] = scalar_row(beta)

    alpha = hist_ref[0:1, :]
    beta = hist_ref[1:2, :]
    alpha0, alpha1, beta1 = past_ref[2:3, :], past_ref[3:4, :], past_ref[4:5, :]
    image = image_of(res2_ref, held_ref, leg_ref, wave, slot, slots, chunk_rows)
    for tile, along in enumerate(image):
        cols = slice(tile * LANES, (tile + 1) * LANES)
        along = along + beta * last_ref[0, :, cols]
        res2 = res2_ref[0, :, cols]
        fin_ref[0, :, cols] = res2 - alpha * along
        first = res0_ref[0, :, cols]
        second = res1_ref[0, :, cols] + beta1 * first
        third = res2 + beta * second
        sol_ref[0, :, cols] = alpha0 * first + alpha1 * second + alpha * third


def fourier_kernel(chunk_rows, slots, norm_factor, lon_count, waves_ref, out_ref):
    rows = waves_ref.shape[0]
    wave = waves_ref[...].astype(F32)
    lane = lax.broadcasted_iota(jnp.int32, (rows, LANES), 1).astype(F32)
    row = lax.broadcasted_iota(jnp.int32, (rows, LANES), 0) + pl.program_id(0) * rows
    within = row - (row // chunk_rows) * chunk_rows
    quarter = jnp.where(within >= slots, 0.25 * lon_count, 0.0)
    fine_cos, fine_sin = turn(wave * lane, lon_count)
    coarse_cos, coarse_sin = turn(wave * (lane * LANES) + quarter, lon_count)
    coarse_cos = coarse_cos * norm_factor
    coarse_sin = coarse_sin * norm_factor
    for tile in range(lon_count // LANES):
        value = coarse_cos[:, tile : tile + 1] * fine_cos - coarse_sin[:, tile : tile + 1] * fine_sin
        out_ref[:, tile * LANES : (tile + 1) * LANES] = value.astype(BF16)


def turn(phase, period):
    phase = phase - period * jnp.floor(phase * (1.0 / period) + 0.5)
    quadrant = jnp.floor(phase * (4.0 / period) + 0.5)
    angle = (phase - quadrant * (0.25 * period)) * (2.0 * math.pi / period)
    sq = angle * angle
    cosine = 1.0 + sq * (-1.0 / 2 + sq * (1.0 / 24 + sq * (-1.0 / 720 + sq * (1.0 / 40320))))
    sine = angle * (1.0 + sq * (-1.0 / 6 + sq * (1.0 / 120 + sq * (-1.0 / 5040 + sq * (1.0 / 362880)))))
    odd = jnp.abs(quadrant) == 1.0
    cos_base = jnp.where(odd, -quadrant * sine, cosine)
    sin_base = jnp.where(odd, quadrant * cosine, sine)
    back = jnp.abs(quadrant) == 2.0
    return jnp.where(back, -cos_base, cos_base), jnp.where(back, -sin_base, sin_base)


def pieces_of(value):
    high = value.astype(BF16).astype(F32)
    middle = (value - high).astype(BF16).astype(F32)
    low = (value - high - middle).astype(BF16).astype(F32)
    return high, middle, low


def grid_kernel(x_ref, table_ref, weight_ref, norm_ref, out_ref, turned_ref, wide_ref):
    count, lons = table_ref.shape
    step = 256
    turned_ref[...] = x_ref[...].astype(F32).T.astype(BF16)
    energy = jnp.zeros((SUB, step), F32)
    for first in range(0, lons, step):
        cols = slice(first, first + step)
        grid = jnp.dot(turned_ref[...], table_ref[:, cols], preferred_element_type=F32)
        weight = weight_ref[:, cols]
        weighted = []
        for group in range(GROUPS):
            rows = grid[group * PIECE : (group + 1) * PIECE]
            product = weight * rows
            weighted.append(product)
            square = product * rows
            for block in range(0, PIECE, SUB):
                energy = energy + square[block : block + SUB]
        weighted.append(jnp.zeros((LANES - SPARE, step), F32))
        wide_ref[cols, :] = jnp.concatenate(weighted, axis=0).T.astype(BF16)
    lane = lane_of(1)
    spare = jnp.zeros((1, LANES), F32)
    values = pieces_of(jnp.sum(norm_ref[...], axis=(0, 1), keepdims=True))
    values = values + pieces_of(jnp.sum(energy, axis=(0, 1), keepdims=True))
    for place, value in enumerate(values):
        spare = jnp.where(lane == SPARE + place, value, spare)
    for first in range(0, count, step):
        rows = slice(first, first + step)
        back = jnp.dot(table_ref[rows, :], wide_ref[...], preferred_element_type=F32)
        out_ref[rows, :] = jnp.where(lane >= SPARE, spare, back).astype(BF16)


def tail_kernel(x_ref, out_ref):
    total = jnp.zeros((SUB, LANES), F32)
    block = 2 * SUB
    for first in range(0, x_ref.shape[0], block):
        value = x_ref[first : first + block, :].astype(F32)
        total = total + value[:SUB] + value[SUB:]
    out_ref[...] = total


def exchange(payload, parts):
    rows = payload.shape[0]
    packed = payload.reshape(parts, rows // parts // 2, 2, LANES)
    return lax.all_to_all(packed, EXCHANGE, 0, 0, tiled=True).reshape(rows, LANES)


def whole(shape):
    return pl.BlockSpec(shape, lambda *_: (0,) * len(shape))


def on_device(right_side, legendre, wave_map, obs_weight):
    slots, degrees, lats = legendre.shape
    lon_count = obs_weight.shape[1]
    bands = ZS * YS * CS
    rows = bands * 2 * slots
    chunk_rows = 2 * slots
    band_at = lax.axis_index(BAND)
    own_waves = lax.dynamic_slice_in_dim(wave_map, band_at * slots, slots)

    vec = right_side.reshape(slots, 2, GROUPS, YS, degrees).transpose(0, 2, 3, 1, 4)
    vec = vec.reshape(slots, GROUPS * SUB, degrees)

    spread = wave_map.reshape(ZS, YS, CS, slots).transpose(0, 2, 1, 3).reshape(bands, 1, slots)
    spread = jnp.broadcast_to(spread, (bands, 2, slots)).reshape(rows, 1)
    spread = jnp.broadcast_to(spread, (rows, LANES))
    block = 128
    table = pl.pallas_call(
        functools.partial(fourier_kernel, chunk_rows, slots, 1.0 / math.sqrt(wave_map.shape[0]), lon_count),
        grid=(rows // block,),
        in_specs=[pl.BlockSpec((block, LANES), lambda i: (i, 0))],
        out_specs=pl.BlockSpec((block, lon_count), lambda i: (i, 0)),
        out_shape=jax.ShapeDtypeStruct((rows, lon_count), BF16),
        cost_estimate=pl.CostEstimate(flops=4_000_000_000, bytes_accessed=4_000_000, transcendentals=0),
        name="fourier",
    )(spread)

    near = jnp.broadcast_to(obs_weight[None], (YS * CS,) + obs_weight.shape)
    near = lax.all_to_all(near, ("y", "c"), 0, 0, tiled=True)
    near = lax.dynamic_slice_in_dim(near, lax.axis_index("c") * YS, YS)
    weight = near.reshape(PIECE, lon_count)

    slot_block = pl.BlockSpec((1, GROUPS * SUB, degrees), lambda i: (i, 0, 0))
    leg_block = pl.BlockSpec((1, degrees, lats), lambda i: (i, 0, 0))
    smem = pl.BlockSpec(memory_space=pltpu.SMEM)
    small = whole((SUB, LANES))
    payload_block = whole((rows, LANES))
    vec_shape = jax.ShapeDtypeStruct((slots, GROUPS * SUB, degrees), F32)
    payload_shape = jax.ShapeDtypeStruct((rows, LANES), BF16)
    small_shape = jax.ShapeDtypeStruct((SUB, LANES), F32)
    held = pltpu.VMEM((rows, LANES), F32)
    cost = pl.CostEstimate(flops=4_000_000_000, bytes_accessed=9_000_000, transcendentals=0)

    res, payload, norm = pl.pallas_call(
        functools.partial(first_kernel, slots, chunk_rows),
        grid=(slots,),
        in_specs=[smem, slot_block, leg_block],
        out_specs=[slot_block, payload_block, small],
        out_shape=[vec_shape, payload_shape, small_shape],
        scratch_shapes=[held],
        cost_estimate=cost,
        name="first",
    )(own_waves, vec, legendre)

    def reach(payload, norm):
        arrived = exchange(payload, bands)
        back = pl.pallas_call(
            grid_kernel,
            out_shape=payload_shape,
            scratch_shapes=[pltpu.VMEM((LANES, rows), BF16), pltpu.VMEM((lon_count, LANES), BF16)],
            cost_estimate=cost,
            name="grid",
        )(arrived, table, weight, norm)
        home = exchange(back, bands)
        sums = pl.pallas_call(
            tail_kernel,
            out_shape=small_shape,
            name="tail",
        )(home)
        others = [lax.ppermute(sums, "x", [(i, (i + k) % XS) for i in range(XS)]) for k in range(1, XS)]
        return home, [sums] + others

    past = jnp.zeros((SUB, LANES), F32)
    residuals = [res]
    along = None
    for stage in range(2):
        home, sums = reach(payload, norm)
        operands = [own_waves, home, legendre, *sums, past, residuals[-1]]
        specs = [smem, payload_block, leg_block, small, small, small, small, small, slot_block]
        if stage > 0:
            operands.append(along)
            specs.append(slot_block)
        res, along, payload, norm, past = pl.pallas_call(
            functools.partial(middle_kernel, stage, slots, chunk_rows),
            grid=(slots,),
            in_specs=specs,
            out_specs=[slot_block, slot_block, payload_block, small, small],
            out_shape=[vec_shape, vec_shape, payload_shape, small_shape, small_shape],
            scratch_shapes=[held, held],
            cost_estimate=cost,
            name=f"middle{stage}",
        )(*operands)
        residuals.append(res)
    home, sums = reach(payload, norm)
    solution, residual = pl.pallas_call(
        functools.partial(last_kernel, slots, chunk_rows),
        grid=(slots,),
        in_specs=[smem, payload_block, leg_block, small, small, small, small, small] + [slot_block] * 4,
        out_specs=[slot_block, slot_block],
        out_shape=[vec_shape, vec_shape],
        scratch_shapes=[pltpu.VMEM((SUB, LANES), F32), held],
        cost_estimate=cost,
        name="last",
    )(own_waves, home, legendre, *sums, past, *residuals, along)

    def unpack(value):
        value = value.reshape(slots, GROUPS, YS, 2, degrees).transpose(0, 3, 1, 2, 4)
        return value.reshape(right_side.shape)

    return unpack(solution), unpack(residual)


def solution(mesh):
    split = Mesh(mesh.devices.reshape(ZS, YS, CS, XS), ("z", "y", "c", "x"))
    return jax.shard_map(
        on_device,
        mesh=split,
        in_specs=(P(BAND, None, "x", None, None), P(BAND, None, None), P(), P(BAND, None)),
        out_specs=(P(BAND, None, "x", None, None), P(BAND, None, "x", None, None)),
        check_vma=False,
    )
```

time: 747 us -> 235 us (0.31)
  local copies, waits for them, and re-layouts: 419 us -> 16.1 us
  blocking collectives: 219 us -> 106 us
  Pallas kernels: 0 us -> 70.1 us
  matrix products: 55.6 us -> 0 us
  other arithmetic: 18 us -> 0 us
  waiting for transfers between devices: 0.01 us -> 12.4 us
  starting transfers between devices: 13.5 us -> 25.8 us
  between operations: 11.1 us -> 0.75 us
    reshape x18 -> x8, local copies, waits for them, and re-layouts: 152 us -> 9.27 us  [the longest x2 2.91 us: unpack(): return value.reshape(right_side.shape)]
    psum x12 -> x0, blocking collectives: 112 us -> none  [by_axis(): return functools.reduce(lax.psum, axes, array)]
    all_to_all x9 -> x0, local copies, waits for them, and re-layouts: 104 us -> none  [the longest x6 55.7 us: operate(): lax.all_to_all(outgoing, BAND, split_axis=3, concat_axis=0, tiled=True)]
    unnamed x22, local copies, waits for them, and re-layouts: 81.6 us -> 1.93 us
    pallas_call x0 -> x11, Pallas kernels: none -> 70.1 us  [the longest x2 22.9 us: on_device(): pl.pallas_call(functools.partial(middle_kernel, stage, slots, chunk_rows)...]
    another operation x6 -> x0, local copies, waits for them, and re-layouts: 58.5 us -> none
    dot_general x12 -> x0, matrix products: 55.6 us -> none  [the longest x3 21.5 us: legendre_back(): lax.dot_general(returned, legendre, (((4,), (2,)), ((0,), (0,))), preferr...]
    convert_element_type x9 -> x0, local copies, waits for them, and re-layouts: 16 us -> none  [the longest x3 9.94 us: fourier_of(): (jnp.stack([jnp.cos(angles), -jnp.sin(angles)], axis=1) * norm_factor).as...]
  transfers between devices with their start and end apart: 1 -> 11, of which waited for: 0 -> 9; matrix products, arithmetic and copies ran while one was open for 3% -> 3% of each run, Pallas kernels for 0% -> 8%
where the time goes in v1:
time: 235 us; the launch traced here: 231 us
  blocking collectives  106 us (45%)
  Pallas kernels  70.1 us (30%)
  starting transfers between devices  25.8 us (11%)
  local copies, waits for them, and re-layouts  16.1 us (7%)
  waiting for transfers between devices  12.4 us (5%)
    all_to_all x5, blocking collectives, exchange(): lax.all_to_all(packed, EXCHANGE, 0, 0, tiled=True).reshape(rows, LANES)  106 us
    pallas_call x2, Pallas kernels, on_device(): pl.pallas_call(functools.partial(middle_kernel, stage, slots, chunk_rows)...  22.9 us
    pallas_call x3, Pallas kernels, reach(): pl.pallas_call(grid_kernel, out_shape=payload_shape, scratch_shapes=[pltp...  13.6 us
    all_to_all x1, starting transfers between devices, exchange(): lax.all_to_all(packed, EXCHANGE, 0, 0, tiled=True).reshape(rows, LANES)  11.3 us
    ppermute x9, waiting for transfers between devices, reach(): lax.ppermute(sums, 'x', [(i, (i + k) % XS) for i in range(XS)])  10.2 us
    pallas_call x1, Pallas kernels, on_device(): pl.pallas_call(functools.partial(last_kernel, slots, chunk_rows), grid=(s...  10.1 us
    pallas_call x1, Pallas kernels, on_device(): pl.pallas_call(functools.partial(first_kernel, slots, chunk_rows), grid=(...  9.42 us
    pallas_call x1, Pallas kernels, on_device(): pl.pallas_call(functools.partial(fourier_kernel, chunk_rows, slots, 1.0 /...  8.88 us
  transfers between devices with their start and end apart: 11, of which 9 were waited for; matrix products, arithmetic and copies ran while one was open for 3% of the time, Pallas kernels for 8%

profile of v1, /device:TPU:1, one launch (start us, length us, event | category | flops | bytes accessed | tf_op | source)
XLA Modules:
  0.0 231.5 jit_solution(10278486333699487739)
XLA Ops:
  0.6 1.8 broadcast_in_dim.27
  2.4 6.6 %all-to-all-start.1 = ((f32[8,10,1280]{2,1,0:T(8,128)}), f32[8,10,1280]{2,1,0:T(8,128)S(1)}, u32[]{:S(2)}, u32[]{:S(2)}) async-start(f32[8,10,1280]{2,1,0:T(8,128)} %broadcast_in_dim.27), calls=%async_computation.1 | async-start | bytes 1310720 | tf_op jit(solution)/shard_map/all_to_all | solution.py:319
  9.1 1.4 copy.16
  10.4 0.0 copy-start.1
  10.5 1.2 reshape.70.vec_ref
  11.7 1.3 dynamic_slice.6.waves_ref.refs_0_
  13.0 9.4 %first.1 = (f32[10,24,640]{2,1,0:T(8,128)}, bf16[1280,128]{1,0:T(8,128)(2,1)}, f32[8,128]{1,0:T(8,128)}) custom-call(s32[10]{0:T(128)} %dynamic_slice.6.waves_ref.refs_0_, f32[10,24,640]{2,1,0:T(8,128)} %reshape.70.vec_ref, bf16[10,640,640]{2,1,0:T(8,128)(2,1)} %refs_2_.5), custom_call_target="tpu_custom_call" | custom-call | flops 4000000000 | bytes 9000000 | tf_op jit(solution)/shard_map/first/pallas_call | solution.py:334
  22.4 0.0 all-to-all-done.1
  22.4 11.3 %all-to-all-start = ((bf16[64,10,2,128]{3,2,1,0:T(2,128)(2,1)}), bf16[64,10,2,128]{3,2,1,0:T(2,128)(2,1)S(1)}, u32[]{:S(2)}, u32[]{:S(2)}) async-start(bf16[64,10,2,128]{3,2,1,0:T(2,128)(2,1)} %bitcast.32), calls=%async_computation | async-start | bytes 655360 | tf_op jit(solution)/shard_map/all_to_all | solution.py:285
  33.7 0.0 copy-done.1
  33.7 0.2 reshape.73
  34.0 0.1 broadcast_in_dim.25
  34.1 1.1 broadcast_in_dim.26.waves_ref
  35.2 8.9 %fourier.1.table_ref = bf16[1280,1280]{1,0:T(8,128)(2,1)} custom-call(s32[1280,128]{1,0:T(8,128)} %broadcast_in_dim.26.waves_ref), custom_call_target="tpu_custom_call" | custom-call | flops 4000000000 | bytes 4000000 | tf_op jit(solution)/shard_map/fourier/pallas_call | solution.py:308
  44.1 0.7 reshape.74.weight_ref
  44.8 2.2 all-to-all-done
  47.0 0.0 copy-start
  47.0 0.7 copy-done
  47.7 4.5 %grid.3 = bf16[1280,128]{1,0:T(8,128)(2,1)} custom-call(bf16[1280,128]{1,0:T(8,128)(2,1)} %bitcast.33, bf16[1280,1280]{1,0:T(8,128)(2,1)} %fourier.1.table_ref, f32[40,1280]{1,0:T(8,128)} %reshape.74.weight_ref, f32[8,128]{1,0:T(8,128)} %get-tuple-element.18.norm_ref), custom_call_target="tpu_custom_call" | custom-call | flops 4000000000 | bytes 9000000 | tf_op jit(solution)/shard_map/grid/pallas_call | solution.py:347
  52.3 21.5 %all_to_all.35 = bf16[64,10,2,128]{3,2,1,0:T(2,128)(2,1)} all-to-all(bf16[64,10,2,128]{3,2,1,0:T(2,128)(2,1)} %bitcast.38), channel_id=1, replica_groups=mesh['z'=8,'y'=4,'c'=2,'x'=4] {'z','c','y'}, dimensions={0} | all-to-all | bytes 655360 | tf_op jit(solution)/shard_map/all_to_all | solution.py:285
  73.7 1.7 tail.3.refs_3_
  75.5 2.5 %collective-permute-start.2 = (f32[8,128]{1,0:T(8,128)}, f32[8,128]{1,0:T(8,128)S(1)}, u32[]{:S(2)}, u32[]{:S(2)}) collective-permute-start(f32[8,128]{1,0:T(8,128)} %tail.3.refs_3_), channel_id=1, source_target_pairs={{0,3},{1,0},{2,1},{3,2},{4,7},{5,4},{6,5},{7,6},{8,11},{9,8},{10,9... | collective-permute-start | bytes 12296 | tf_op jit(solution)/shard_map/ppermute | solution.py:360
  77.9 0.5 collective-permute-start.1
  78.4 0.6 collective-permute-start
  79.0 0.0 collective-permute-done.2.refs_6_
  79.0 3.1 %collective-permute-done.1.refs_5_ = f32[8,128]{1,0:T(8,128)S(1)} collective-permute-done((f32[8,128]{1,0:T(8,128)}, f32[8,128]{1,0:T(8,128)S(1)}, u32[]{:S(2)}, u32[]{:S(2)}) %collective-permute-start.1) | collective-permute-done | bytes 4128 | tf_op jit(solution)/shard_map/ppermute | solution.py:360
  82.1 0.2 collective-permute-done.refs_4_
  82.3 0.6 broadcast_in_dim.28.refs_7_
  82.9 0.0 copy-done.3
  82.9 0.0 copy-done.6
  82.9 0.0 copy-done.9
  82.9 11.3 %middle0.1 = (f32[10,24,640]{2,1,0:T(8,128)}, f32[10,24,640]{2,1,0:T(8,128)}, bf16[1280,128]{1,0:T(8,128)(2,1)}, f32[8,128]{1,0:T(8,128)}, f32[8,128]{1,0:T(8,128)}) custom-call(s32[10]{0:T(128)} %dynamic_slice.6.waves_ref.refs_0_, bf16[1280,128]{1,0:T(8,128)(2,1)} %bitcast.29, bf16[10,640,640]{2,1,0:T(8,128)(2,1)} %refs_2_.5, f32[8,128]{1,0:T(8,128)} %tail.3.refs_3_, ...), custom_call_target="tpu_custom_call" | custom-call | flops 4000000000 | bytes 9000000 | tf_op jit(solution)/shard_map/middle0/pallas_call | solution.py:373
  94.2 22.2 %all_to_all.36 = bf16[64,10,2,128]{3,2,1,0:T(2,128)(2,1)} all-to-all(bf16[64,10,2,128]{3,2,1,0:T(2,128)(2,1)} %bitcast.35), channel_id=1, replica_groups=mesh['z'=8,'y'=4,'c'=2,'x'=4] {'z','c','y'}, dimensions={0} | all-to-all | bytes 655360 | tf_op jit(solution)/shard_map/all_to_all | solution.py:285
  116.4 4.5 %grid.4 = bf16[1280,128]{1,0:T(8,128)(2,1)} custom-call(bf16[1280,128]{1,0:T(8,128)(2,1)} %bitcast.39, bf16[1280,1280]{1,0:T(8,128)(2,1)} %fourier.1.table_ref, f32[40,1280]{1,0:T(8,128)} %reshape.74.weight_ref, f32[8,128]{1,0:T(8,128)} %get-tuple-element.21.norm_ref), custom_call_target="tpu_custom_call" | custom-call | flops 4000000000 | bytes 9000000 | tf_op jit(solution)/shard_map/grid/pallas_call | solution.py:347
  120.9 20.5 %all_to_all.37 = bf16[64,10,2,128]{3,2,1,0:T(2,128)(2,1)} all-to-all(bf16[64,10,2,128]{3,2,1,0:T(2,128)(2,1)} %bitcast.40), channel_id=1, replica_groups=mesh['z'=8,'y'=4,'c'=2,'x'=4] {'z','c','y'}, dimensions={0} | all-to-all | bytes 655360 | tf_op jit(solution)/shard_map/all_to_all | solution.py:285
  141.4 1.7 tail.4.refs_3_
  143.2 0.0 collective-permute-start.5
  143.2 1.2 collective-permute-start.4
  144.4 0.9 collective-permute-start.3
  145.3 0.6 collective-permute-done.5.refs_6_
  145.8 1.5 collective-permute-done.4.refs_5_
  147.4 0.9 collective-permute-done.3.refs_4_
  148.3 0.0 copy-done.4
  148.3 0.0 copy-done.7
  148.3 0.6 copy-done.10
  148.9 11.6 %middle1.1 = (f32[10,24,640]{2,1,0:T(8,128)}, f32[10,24,640]{2,1,0:T(8,128)}, bf16[1280,128]{1,0:T(8,128)(2,1)}, f32[8,128]{1,0:T(8,128)}, f32[8,128]{1,0:T(8,128)}) custom-call(s32[10]{0:T(128)} %dynamic_slice.6.waves_ref.refs_0_, bf16[1280,128]{1,0:T(8,128)(2,1)} %bitcast.31, bf16[10,640,640]{2,1,0:T(8,128)(2,1)} %refs_2_.5, f32[8,128]{1,0:T(8,128)} %tail.4.refs_3_, ...), custom_call_target="tpu_custom_call" | custom-call | flops 4000000000 | bytes 9000000 | tf_op jit(solution)/shard_map/middle1/pallas_call | solution.py:373
  160.5 21.9 %all_to_all.38 = bf16[64,10,2,128]{3,2,1,0:T(2,128)(2,1)} all-to-all(bf16[64,10,2,128]{3,2,1,0:T(2,128)(2,1)} %bitcast.34), channel_id=1, replica_groups=mesh['z'=8,'y'=4,'c'=2,'x'=4] {'z','c','y'}, dimensions={0} | all-to-all | bytes 655360 | tf_op jit(solution)/shard_map/all_to_all | solution.py:285
  182.4 4.5 %grid.5 = bf16[1280,128]{1,0:T(8,128)(2,1)} custom-call(bf16[1280,128]{1,0:T(8,128)(2,1)} %bitcast.36, bf16[1280,1280]{1,0:T(8,128)(2,1)} %fourier.1.table_ref, f32[40,1280]{1,0:T(8,128)} %reshape.74.weight_ref, f32[8,128]{1,0:T(8,128)} %get-tuple-element.26.norm_ref), custom_call_target="tpu_custom_call" | custom-call | flops 4000000000 | bytes 9000000 | tf_op jit(solution)/shard_map/grid/pallas_call | solution.py:347
  186.9 20.3 %all_to_all.39 = bf16[64,10,2,128]{3,2,1,0:T(2,128)(2,1)} all-to-all(bf16[64,10,2,128]{3,2,1,0:T(2,128)(2,1)} %bitcast.37), channel_id=1, replica_groups=mesh['z'=8,'y'=4,'c'=2,'x'=4] {'z','c','y'}, dimensions={0} | all-to-all | bytes 655360 | tf_op jit(solution)/shard_map/all_to_all | solution.py:285
  207.2 1.7 tail.5.refs_3_
  209.0 1.5 collective-permute-start.8
  210.4 0.6 collective-permute-start.7
  211.1 0.0 collective-permute-start.6
  211.1 0.6 collective-permute-done.8.refs_6_
  211.6 3.0 %collective-permute-done.7.refs_5_ = f32[8,128]{1,0:T(8,128)S(1)} collective-permute-done((f32[8,128]{1,0:T(8,128)}, f32[8,128]{1,0:T(8,128)S(1)}, u32[]{:S(2)}, u32[]{:S(2)}) %collective-permute-start.7) | collective-permute-done | bytes 4128 | tf_op jit(solution)/shard_map/ppermute | solution.py:360
  214.6 0.3 collective-permute-done.6.refs_4_
  214.9 0.0 copy-done.2
  214.9 0.3 copy-done.5
  215.2 0.3 copy-done.8
  215.5 10.1 %last.1 = (f32[10,24,640]{2,1,0:T(8,128)}, f32[10,24,640]{2,1,0:T(8,128)}) custom-call(s32[10]{0:T(128)} %dynamic_slice.6.waves_ref.refs_0_, bf16[1280,128]{1,0:T(8,128)(2,1)} %bitcast.27, bf16[10,640,640]{2,1,0:T(8,128)(2,1)} %refs_2_.5, f32[8,128]{1,0:T(8,128)} %tail.5.refs_3_, f32[8,128]{1,0:T(8,128)} %copy-done.8, f32[8,128]{1,0:T(8,128)} %copy-done.5, ...), custom_call_target="tpu_custom_call" | custom-call | flops 4000000000 | bytes 9000000 | tf_op jit(solution)/shard_map/last/pallas_call | solution.py:385
  225.7 1.4 reshape.85
  227.1 1.5 copy.17
  228.6 1.4 reshape.87
  230.0 1.5 copy.18
  (12 shorter events, 0.1 us)
Async XLA Ops:
  2.4 20.0 %all-to-all-start.1 = ((f32[8,10,1280]{2,1,0:T(8,128)}), f32[8,10,1280]{2,1,0:T(8,128)S(1)}, u32[]{:S(2)}, u32[]{:S(2)}) async-start(f32[8,10,1280]{2,1,0:T(8,128)} %broadcast_in_dim.27), calls=%async_computation.1 | async-start | bytes 1310720 | tf_op jit(solution)/shard_map/all_to_all | solution.py:319
  10.4 23.3 %copy-start.1 = (s32[640]{0:T(1024)S(1)}, s32[640]{0:T(1024)}, u32[]{:S(2)}) copy-start(s32[640]{0:T(1024)} %param.6) | copy-start | bytes 7684
  22.4 24.6 %all-to-all-start = ((bf16[64,10,2,128]{3,2,1,0:T(2,128)(2,1)}), bf16[64,10,2,128]{3,2,1,0:T(2,128)(2,1)S(1)}, u32[]{:S(2)}, u32[]{:S(2)}) async-start(bf16[64,10,2,128]{3,2,1,0:T(2,128)(2,1)} %bitcast.32), calls=%async_computation | async-start | bytes 655360 | tf_op jit(solution)/shard_map/all_to_all | solution.py:285
  47.0 0.7 copy-start
  75.5 3.6 %collective-permute-start.2 = (f32[8,128]{1,0:T(8,128)}, f32[8,128]{1,0:T(8,128)S(1)}, u32[]{:S(2)}, u32[]{:S(2)}) collective-permute-start(f32[8,128]{1,0:T(8,128)} %tail.3.refs_3_), channel_id=1, source_target_pairs={{0,3},{1,0},{2,1},{3,2},{4,7},{5,4},{6,5},{7,6},{8,11},{9,8},{10,9... | collective-permute-start | bytes 12296 | tf_op jit(solution)/shard_map/ppermute | solution.py:360
  77.9 4.2 %collective-permute-start.1 = (f32[8,128]{1,0:T(8,128)}, f32[8,128]{1,0:T(8,128)S(1)}, u32[]{:S(2)}, u32[]{:S(2)}) collective-permute-start(f32[8,128]{1,0:T(8,128)} %tail.3.refs_3_), channel_id=1, source_target_pairs={{0,2},{1,3},{2,0},{3,1},{4,6},{5,7},{6,4},{7,5},{8,10},{9,11},{10,... | collective-permute-start | bytes 12296 | tf_op jit(solution)/shard_map/ppermute | solution.py:360
  78.4 3.9 %collective-permute-start = (f32[8,128]{1,0:T(8,128)}, f32[8,128]{1,0:T(8,128)S(1)}, u32[]{:S(2)}, u32[]{:S(2)}) collective-permute-start(f32[8,128]{1,0:T(8,128)} %tail.3.refs_3_), channel_id=1, source_target_pairs={{0,1},{1,2},{2,3},{3,0},{4,5},{5,6},{6,7},{7,4},{8,9},{9,10},{10,1... | collective-permute-start | bytes 12296 | tf_op jit(solution)/shard_map/ppermute | solution.py:360
  79.0 3.9 %copy-start.3 = (f32[8,128]{1,0:T(8,128)}, f32[8,128]{1,0:T(8,128)S(1)}, u32[]{:S(2)}) copy-start(f32[8,128]{1,0:T(8,128)S(1)} %collective-permute-done.2.refs_6_) | copy-start | bytes 12292
  82.1 0.8 copy-start.6
  82.3 0.6 copy-start.9
  143.2 2.7 %collective-permute-start.5 = (f32[8,128]{1,0:T(8,128)}, f32[8,128]{1,0:T(8,128)S(1)}, u32[]{:S(2)}, u32[]{:S(2)}) collective-permute-start(f32[8,128]{1,0:T(8,128)} %tail.4.refs_3_), channel_id=1, source_target_pairs={{0,3},{1,0},{2,1},{3,2},{4,7},{5,4},{6,5},{7,6},{8,11},{9,8},{10,9... | collective-permute-start | bytes 12296 | tf_op jit(solution)/shard_map/ppermute | solution.py:360
  143.2 4.2 %collective-permute-start.4 = (f32[8,128]{1,0:T(8,128)}, f32[8,128]{1,0:T(8,128)S(1)}, u32[]{:S(2)}, u32[]{:S(2)}) collective-permute-start(f32[8,128]{1,0:T(8,128)} %tail.4.refs_3_), channel_id=1, source_target_pairs={{0,2},{1,3},{2,0},{3,1},{4,6},{5,7},{6,4},{7,5},{8,10},{9,11},{10,... | collective-permute-start | bytes 12296 | tf_op jit(solution)/shard_map/ppermute | solution.py:360
  144.4 3.9 %collective-permute-start.3 = (f32[8,128]{1,0:T(8,128)}, f32[8,128]{1,0:T(8,128)S(1)}, u32[]{:S(2)}, u32[]{:S(2)}) collective-permute-start(f32[8,128]{1,0:T(8,128)} %tail.4.refs_3_), channel_id=1, source_target_pairs={{0,1},{1,2},{2,3},{3,0},{4,5},{5,6},{6,7},{7,4},{8,9},{9,10},{10,1... | collective-permute-start | bytes 12296 | tf_op jit(solution)/shard_map/ppermute | solution.py:360
  145.8 2.5 %copy-start.4 = (f32[8,128]{1,0:T(8,128)}, f32[8,128]{1,0:T(8,128)S(1)}, u32[]{:S(2)}) copy-start(f32[8,128]{1,0:T(8,128)S(1)} %collective-permute-done.5.refs_6_) | copy-start | bytes 12292
  147.4 0.9 copy-start.7
  148.3 0.6 copy-start.10
  209.0 2.7 %collective-permute-start.8 = (f32[8,128]{1,0:T(8,128)}, f32[8,128]{1,0:T(8,128)S(1)}, u32[]{:S(2)}, u32[]{:S(2)}) collective-permute-start(f32[8,128]{1,0:T(8,128)} %tail.5.refs_3_), channel_id=1, source_target_pairs={{0,3},{1,0},{2,1},{3,2},{4,7},{5,4},{6,5},{7,6},{8,11},{9,8},{10,9... | collective-permute-start | bytes 12296 | tf_op jit(solution)/shard_map/ppermute | solution.py:360
  210.4 4.2 %collective-permute-start.7 = (f32[8,128]{1,0:T(8,128)}, f32[8,128]{1,0:T(8,128)S(1)}, u32[]{:S(2)}, u32[]{:S(2)}) collective-permute-start(f32[8,128]{1,0:T(8,128)} %tail.5.refs_3_), channel_id=1, source_target_pairs={{0,2},{1,3},{2,0},{3,1},{4,6},{5,7},{6,4},{7,5},{8,10},{9,11},{10,... | collective-permute-start | bytes 12296 | tf_op jit(solution)/shard_map/ppermute | solution.py:360
  211.1 3.9 %collective-permute-start.6 = (f32[8,128]{1,0:T(8,128)}, f32[8,128]{1,0:T(8,128)S(1)}, u32[]{:S(2)}, u32[]{:S(2)}) collective-permute-start(f32[8,128]{1,0:T(8,128)} %tail.5.refs_3_), channel_id=1, source_target_pairs={{0,1},{1,2},{2,3},{3,0},{4,5},{5,6},{6,7},{7,4},{8,9},{9,10},{10,1... | collective-permute-start | bytes 12296 | tf_op jit(solution)/shard_map/ppermute | solution.py:360
  211.6 3.3 %copy-start.2 = (f32[8,128]{1,0:T(8,128)}, f32[8,128]{1,0:T(8,128)S(1)}, u32[]{:S(2)}) copy-start(f32[8,128]{1,0:T(8,128)S(1)} %collective-permute-done.8.refs_6_) | copy-start | bytes 12292
  214.6 0.6 copy-start.5
  214.9 0.6 copy-start.8

commit v2 on v1

--- a/solution.py
+++ b/solution.py
@@ -312,6 +312,7 @@
         out_specs=pl.BlockSpec((block, lon_count), lambda i: (i, 0)),
         out_shape=jax.ShapeDtypeStruct((rows, lon_count), BF16),
         cost_estimate=pl.CostEstimate(flops=4_000_000_000, bytes_accessed=4_000_000, transcendentals=0),
+        compiler_params=pltpu.CompilerParams(vmem_limit_bytes=16 * 1024 * 1024),
         name="fourier",
     )(spread)
 
@@ -339,6 +340,7 @@
         out_shape=[vec_shape, payload_shape, small_shape],
         scratch_shapes=[held],
         cost_estimate=cost,
+        compiler_params=pltpu.CompilerParams(vmem_limit_bytes=16 * 1024 * 1024),
         name="first",
     )(own_waves, vec, legendre)
 
@@ -349,13 +351,15 @@
             out_shape=payload_shape,
             scratch_shapes=[pltpu.VMEM((LANES, rows), BF16), pltpu.VMEM((lon_count, LANES), BF16)],
             cost_estimate=cost,
-            name="grid",
+            compiler_params=pltpu.CompilerParams(vmem_limit_bytes=16 * 1024 * 1024),
+        name="grid",
         )(arrived, table, weight, norm)
         home = exchange(back, bands)
         sums = pl.pallas_call(
             tail_kernel,
             out_shape=small_shape,
-            name="tail",
+            compiler_params=pltpu.CompilerParams(vmem_limit_bytes=16 * 1024 * 1024),
+        name="tail",
         )(home)
         others = [lax.ppermute(sums, "x", [(i, (i + k) % XS) for i in range(XS)]) for k in range(1, XS)]
         return home, [sums] + others
@@ -378,6 +382,7 @@
             out_shape=[vec_shape, vec_shape, payload_shape, small_shape, small_shape],
             scratch_shapes=[held, held],
             cost_estimate=cost,
+            compiler_params=pltpu.CompilerParams(vmem_limit_bytes=16 * 1024 * 1024),
             name=f"middle{stage}",
         )(*operands)
         residuals.append(res)
@@ -390,6 +395,7 @@
         out_shape=[vec_shape, vec_shape],
         scratch_shapes=[pltpu.VMEM((SUB, LANES), F32), held],
         cost_estimate=cost,
+        compiler_params=pltpu.CompilerParams(vmem_limit_bytes=16 * 1024 * 1024),
         name="last",
     )(own_waves, home, legendre, *sums, past, *residuals, along)
 

time: 235 us -> 198 us (0.84)
  Pallas kernels: 70.1 us -> 36.6 us
  blocking collectives: 106 us -> 98.5 us
  local copies, waits for them, and re-layouts: 16.1 us -> 18.9 us
    unnamed x22 -> x16, local copies, waits for them, and re-layouts: 1.93 us -> 10.3 us
    pallas_call x2, Pallas kernels: 22.9 us -> 14.7 us  [on_device(): pl.pallas_call(functools.partial(middle_kernel, stage, slots, chunk_rows)...]
    pallas_call x3, Pallas kernels: 13.6 us -> 5.53 us  [reach(): pl.pallas_call(grid_kernel, out_shape=payload_shape, scratch_shapes=[pltp...]
    all_to_all x5, blocking collectives: 106 us -> 98.5 us  [exchange(): lax.all_to_all(packed, EXCHANGE, 0, 0, tiled=True).reshape(rows, LANES)]
    pallas_call x1, Pallas kernels: 10.1 us -> 4.95 us  [on_device(): pl.pallas_call(functools.partial(last_kernel, slots, chunk_rows), grid=(s...]
    pallas_call x3, Pallas kernels: 5.19 us -> 0.51 us  [reach(): pl.pallas_call(tail_kernel, out_shape=small_shape, compiler_params=pltpu....]
    pallas_call x1, Pallas kernels: 9.42 us -> 4.94 us  [on_device(): pl.pallas_call(functools.partial(first_kernel, slots, chunk_rows), grid=(...]
    pallas_call x1, Pallas kernels: 8.88 us -> 5.97 us  [on_device(): pl.pallas_call(functools.partial(fourier_kernel, chunk_rows, slots, 1.0 /...]
  transfers between devices with their start and end apart: 11 -> 11, of which waited for: 9 -> 9; matrix products, arithmetic and copies ran while one was open for 3% -> 2% of each run, Pallas kernels for 8% -> 6%
where the time goes in v2:
time: 198 us; the launch traced here: 195 us
  blocking collectives  98.5 us (50%)
  Pallas kernels  36.6 us (18%)
  starting transfers between devices  26 us (13%)
  local copies, waits for them, and re-layouts  18.9 us (10%)
  waiting for transfers between devices  14.6 us (7%)
    all_to_all x5, blocking collectives, exchange(): lax.all_to_all(packed, EXCHANGE, 0, 0, tiled=True).reshape(rows, LANES)  98.5 us
    pallas_call x2, Pallas kernels, on_device(): pl.pallas_call(functools.partial(middle_kernel, stage, slots, chunk_rows)...  14.7 us
    all_to_all x1, starting transfers between devices, exchange(): lax.all_to_all(packed, EXCHANGE, 0, 0, tiled=True).reshape(rows, LANES)  11.3 us
    unnamed x16, local copies, waits for them, and re-layouts  10.3 us
    ppermute x9, waiting for transfers between devices, reach(): lax.ppermute(sums, 'x', [(i, (i + k) % XS) for i in range(XS)])  9.6 us
    ppermute x9, starting transfers between devices, reach(): lax.ppermute(sums, 'x', [(i, (i + k) % XS) for i in range(XS)])  8.06 us
    all_to_all x1, starting transfers between devices, on_device(): near = lax.all_to_all(near, ('y', 'c'), 0, 0, tiled=True)  6.64 us
    pallas_call x1, Pallas kernels, on_device(): pl.pallas_call(functools.partial(fourier_kernel, chunk_rows, slots, 1.0 /...  5.97 us
  transfers between devices with their start and end apart: 11, of which 9 were waited for; matrix products, arithmetic and copies ran while one was open for 2% of the time, Pallas kernels for 6%

profile of v2, /device:TPU:1, one launch (start us, length us, event | category | flops | bytes accessed | tf_op | source)
XLA Modules:
  0.0 195.4 jit_solution(14716235953740566616)
XLA Ops:
  0.6 1.8 broadcast_in_dim.27
  2.4 6.6 %all-to-all-start.1 = ((f32[8,10,1280]{2,1,0:T(8,128)}), f32[8,10,1280]{2,1,0:T(8,128)S(1)}, u32[]{:S(2)}, u32[]{:S(2)}) async-start(f32[8,10,1280]{2,1,0:T(8,128)} %broadcast_in_dim.27), calls=%async_computation.1 | async-start | bytes 1310720 | tf_op jit(solution)/shard_map/all_to_all | solution.py:320
  9.1 1.4 copy.16
  10.4 0.0 copy-start.5
  10.5 0.4 reshape.70.vec_ref
  10.9 0.8 dynamic_slice.6.waves_ref.refs_0_
  11.7 0.0 copy-start
  11.7 3.3 %copy-done = bf16[10,640,640]{2,1,0:T(8,128)(2,1)S(1)} copy-done((bf16[10,640,640]{2,1,0:T(8,128)(2,1)S(1)}, bf16[10,640,640]{2,1,0:T(8,128)(2,1)}, u32[]{:S(2)}) %copy-start) | copy-done | bytes 8192024
  15.0 4.9 %first.1 = (f32[10,24,640]{2,1,0:T(8,128)S(1)}, bf16[1280,128]{1,0:T(8,128)(2,1)}, f32[8,128]{1,0:T(8,128)S(1)}) custom-call(s32[10]{0:T(128)S(1)} %dynamic_slice.6.waves_ref.refs_0_, f32[10,24,640]{2,1,0:T(8,128)S(1)} %reshape.70.vec_ref, bf16[10,640,640]{2,1,0:T(8,128)(2,1)S(1)} %copy-done), custom_call_target="tpu_custom_call" | custom-call | flops 4000000000 | bytes 9000000 | tf_op jit(solution)/shard_map/first/pallas_call | solution.py:335
  19.9 0.0 all-to-all-done.1
  19.9 11.3 %all-to-all-start = ((bf16[64,10,2,128]{3,2,1,0:T(2,128)(2,1)}), bf16[64,10,2,128]{3,2,1,0:T(2,128)(2,1)S(1)}, u32[]{:S(2)}, u32[]{:S(2)}) async-start(bf16[64,10,2,128]{3,2,1,0:T(2,128)(2,1)} %bitcast.2), calls=%async_computation | async-start | bytes 655360 | tf_op jit(solution)/shard_map/all_to_all | solution.py:285
  31.3 0.0 copy-done.5
  31.3 0.2 reshape.73
  31.5 0.1 broadcast_in_dim.25
  31.6 0.2 broadcast_in_dim.26.waves_ref
  31.8 6.0 %fourier.1.table_ref = bf16[1280,1280]{1,0:T(8,128)(2,1)S(1)} custom-call(s32[1280,128]{1,0:T(8,128)S(1)} %broadcast_in_dim.26.waves_ref), custom_call_target="tpu_custom_call" | custom-call | flops 4000000000 | bytes 4000000 | tf_op jit(solution)/shard_map/fourier/pallas_call | solution.py:308
  37.8 0.0 copy-start.2
  37.8 1.7 copy-done.2
  39.6 5.0 %all-to-all-done = bf16[64,10,2,128]{3,2,1,0:T(2,128)(2,1)S(1)} async-done(((bf16[64,10,2,128]{3,2,1,0:T(2,128)(2,1)}), bf16[64,10,2,128]{3,2,1,0:T(2,128)(2,1)S(1)}, u32[]{:S(2)}, u32[]{:S(2)}) %all-to-all-start) | async-done | bytes 327712 | tf_op jit(solution)/shard_map/all_to_all | solution.py:285
  44.5 0.0 copy-start.3
  44.5 1.9 copy-done.3
  46.5 0.0 copy-start.4
  46.5 1.8 grid.3
  48.3 19.0 %all_to_all.35 = bf16[64,10,2,128]{3,2,1,0:T(2,128)(2,1)S(1)} all-to-all(bf16[64,10,2,128]{3,2,1,0:T(2,128)(2,1)S(1)} %bitcast.34), channel_id=1, replica_groups=mesh['z'=8,'y'=4,'c'=2,'x'=4] {'z','c','y'}, dimensions={0} | all-to-all | bytes 655360 | tf_op jit(solution)/shard_map/all_to_all | solution.py:285
  67.3 0.2 tail.3.refs_3_
  67.5 2.6 %collective-permute-start.2 = (f32[8,128]{1,0:T(8,128)S(1)}, f32[8,128]{1,0:T(8,128)S(1)}, u32[]{:S(2)}, u32[]{:S(2)}) collective-permute-start(f32[8,128]{1,0:T(8,128)S(1)} %tail.3.refs_3_), channel_id=1, source_target_pairs={{0,3},{1,0},{2,1},{3,2},{4,7},{5,4},{6,5},{7,6},{8,11},{9,8},{10,9... | collective-permute-start | bytes 12296 | tf_op jit(solution)/shard_map/ppermute | solution.py:364
  70.0 0.5 collective-permute-start.1
  70.5 0.6 collective-permute-start
  71.1 0.0 collective-permute-done.2.refs_6_
  71.1 2.8 %collective-permute-done.1.refs_5_ = f32[8,128]{1,0:T(8,128)S(1)} collective-permute-done((f32[8,128]{1,0:T(8,128)S(1)}, f32[8,128]{1,0:T(8,128)S(1)}, u32[]{:S(2)}, u32[]{:S(2)}) %collective-permute-start.1) | collective-permute-done | bytes 4128 | tf_op jit(solution)/shard_map/ppermute | solution.py:364
  74.0 0.2 collective-permute-done.refs_4_
  74.2 0.0 copy-start.1
  74.2 3.3 %copy-done.1 = bf16[10,640,640]{2,1,0:T(8,128)(2,1)S(1)} copy-done((bf16[10,640,640]{2,1,0:T(8,128)(2,1)S(1)}, bf16[10,640,640]{2,1,0:T(8,128)(2,1)}, u32[]{:S(2)}) %copy-start.1) | copy-done | bytes 8192024
  77.5 7.3 %middle0.1 = (f32[10,24,640]{2,1,0:T(8,128)S(1)}, f32[10,24,640]{2,1,0:T(8,128)S(1)}, bf16[1280,128]{1,0:T(8,128)(2,1)S(1)}, f32[8,128]{1,0:T(8,128)S(1)}, f32[8,128]{1,0:T(8,128)S(1)}) custom-call(s32[10]{0:T(128)S(1)} %dynamic_slice.6.waves_ref.refs_0_, bf16[1280,128]{1,0:T(8,128)(2,1)S(1)} %bitcast.26, bf16[10,640,640]{2,1,0:T(8,128)(2,1)S(1)} %copy-done.1, ...), custom_call_target="tpu_custom_call" | custom-call | flops 4000000000 | bytes 9000000 | tf_op jit(solution)/shard_map/middle0/pallas_call | solution.py:377
  84.8 0.0 slice-start
  84.9 21.0 %all_to_all.36 = bf16[64,10,2,128]{3,2,1,0:T(2,128)(2,1)S(1)} all-to-all(bf16[64,10,2,128]{3,2,1,0:T(2,128)(2,1)S(1)} %bitcast.31), channel_id=1, replica_groups=mesh['z'=8,'y'=4,'c'=2,'x'=4] {'z','c','y'}, dimensions={0} | all-to-all | bytes 655360 | tf_op jit(solution)/shard_map/all_to_all | solution.py:285
  105.8 0.0 copy-done.4
  105.8 1.9 grid.4
  107.7 19.0 %all_to_all.37 = bf16[64,10,2,128]{3,2,1,0:T(2,128)(2,1)S(1)} all-to-all(bf16[64,10,2,128]{3,2,1,0:T(2,128)(2,1)S(1)} %bitcast.36), channel_id=1, replica_groups=mesh['z'=8,'y'=4,'c'=2,'x'=4] {'z','c','y'}, dimensions={0} | all-to-all | bytes 655360 | tf_op jit(solution)/shard_map/all_to_all | solution.py:285
  126.7 0.2 tail.4.refs_3_
  126.9 0.1 collective-permute-start.5
  127.0 1.3 collective-permute-start.4
  128.3 0.8 collective-permute-start.3
  129.1 0.3 collective-permute-done.5.refs_6_
  129.4 1.6 collective-permute-done.4.refs_5_
  131.0 1.0 collective-permute-done.3.refs_4_
  132.0 0.0 slice-done
  132.0 0.0 slice-done.1
  132.0 7.4 %middle1.1 = (f32[10,24,640]{2,1,0:T(8,128)S(1)}, f32[10,24,640]{2,1,0:T(8,128)S(1)}, bf16[1280,128]{1,0:T(8,128)(2,1)S(1)}, f32[8,128]{1,0:T(8,128)S(1)}, f32[8,128]{1,0:T(8,128)S(1)}) custom-call(s32[10]{0:T(128)S(1)} %dynamic_slice.6.waves_ref.refs_0_, bf16[1280,128]{1,0:T(8,128)(2,1)S(1)} %bitcast.28, bf16[10,640,640]{2,1,0:T(8,128)(2,1)S(1)} %bitcast.38, ...), custom_call_target="tpu_custom_call" | custom-call | flops 4000000000 | bytes 9000000 | tf_op jit(solution)/shard_map/middle1/pallas_call | solution.py:377
  139.4 20.6 %all_to_all.38 = bf16[64,10,2,128]{3,2,1,0:T(2,128)(2,1)S(1)} all-to-all(bf16[64,10,2,128]{3,2,1,0:T(2,128)(2,1)S(1)} %bitcast.30), channel_id=1, replica_groups=mesh['z'=8,'y'=4,'c'=2,'x'=4] {'z','c','y'}, dimensions={0} | all-to-all | bytes 655360 | tf_op jit(solution)/shard_map/all_to_all | solution.py:285
  160.0 1.9 grid.5
  161.8 19.0 %all_to_all.39 = bf16[64,10,2,128]{3,2,1,0:T(2,128)(2,1)S(1)} all-to-all(bf16[64,10,2,128]{3,2,1,0:T(2,128)(2,1)S(1)} %bitcast.33), channel_id=1, replica_groups=mesh['z'=8,'y'=4,'c'=2,'x'=4] {'z','c','y'}, dimensions={0} | all-to-all | bytes 655360 | tf_op jit(solution)/shard_map/all_to_all | solution.py:285
  180.8 0.2 tail.5.refs_3_
  181.0 1.5 collective-permute-start.8
  182.5 0.7 collective-permute-start.7
  183.2 0.0 collective-permute-start.6
  183.2 0.3 collective-permute-done.8.refs_6_
  183.5 3.0 %collective-permute-done.7.refs_5_ = f32[8,128]{1,0:T(8,128)S(1)} collective-permute-done((f32[8,128]{1,0:T(8,128)S(1)}, f32[8,128]{1,0:T(8,128)S(1)}, u32[]{:S(2)}, u32[]{:S(2)}) %collective-permute-start.7) | collective-permute-done | bytes 4128 | tf_op jit(solution)/shard_map/ppermute | solution.py:364
  186.5 0.4 collective-permute-done.6.refs_4_
  186.8 4.9 %last.1 = (f32[10,24,640]{2,1,0:T(8,128)S(1)}, f32[10,24,640]{2,1,0:T(8,128)S(1)}) custom-call(s32[10]{0:T(128)S(1)} %dynamic_slice.6.waves_ref.refs_0_, bf16[1280,128]{1,0:T(8,128)(2,1)S(1)} %bitcast.24, bf16[10,640,640]{2,1,0:T(8,128)(2,1)S(1)} %bitcast.38, f32[8,128]{1,0:T(8,128)S(1)} %tail.5.refs_3_, f32[8,128]{1,0:T(8,128)S(1)} %collective-permute-done.6.refs_4_, ...), custom_call_target="tpu_custom_call" | custom-call | flops 4000000000 | bytes 9000000 | tf_op jit(solution)/shard_map/last/pallas_call | solution.py:390
  191.8 0.4 reshape.85
  192.2 1.5 copy.17
  193.6 0.4 reshape.87
  194.0 1.5 copy.18
  (7 shorter events, 0.1 us)
Async XLA Ops:
  2.4 17.5 %all-to-all-start.1 = ((f32[8,10,1280]{2,1,0:T(8,128)}), f32[8,10,1280]{2,1,0:T(8,128)S(1)}, u32[]{:S(2)}, u32[]{:S(2)}) async-start(f32[8,10,1280]{2,1,0:T(8,128)} %broadcast_in_dim.27), calls=%async_computation.1 | async-start | bytes 1310720 | tf_op jit(solution)/shard_map/all_to_all | solution.py:320
  10.4 20.8 %copy-start.5 = (s32[640]{0:T(1024)S(1)}, s32[640]{0:T(1024)}, u32[]{:S(2)}) copy-start(s32[640]{0:T(1024)} %param.6) | copy-start | bytes 7684
  11.7 3.3 %copy-start = (bf16[10,640,640]{2,1,0:T(8,128)(2,1)S(1)}, bf16[10,640,640]{2,1,0:T(8,128)(2,1)}, u32[]{:S(2)}) copy-start(bf16[10,640,640]{2,1,0:T(8,128)(2,1)} %refs_2_.5) | copy-start | bytes 24576004
  19.9 24.6 %all-to-all-start = ((bf16[64,10,2,128]{3,2,1,0:T(2,128)(2,1)}), bf16[64,10,2,128]{3,2,1,0:T(2,128)(2,1)S(1)}, u32[]{:S(2)}, u32[]{:S(2)}) async-start(bf16[64,10,2,128]{3,2,1,0:T(2,128)(2,1)} %bitcast.2), calls=%async_computation | async-start | bytes 655360 | tf_op jit(solution)/shard_map/all_to_all | solution.py:285
  37.8 1.7 copy-start.2
  44.5 1.9 copy-start.3
  46.5 59.4 %copy-start.4 = (bf16[1280,1280]{1,0:T(8,128)(2,1)S(1)}, bf16[1280,1280]{1,0:T(8,128)(2,1)}, u32[]{:S(2)}) copy-start(bf16[1280,1280]{1,0:T(8,128)(2,1)} %copy-done.2) | copy-start | bytes 9830404
  67.5 3.7 %collective-permute-start.2 = (f32[8,128]{1,0:T(8,128)S(1)}, f32[8,128]{1,0:T(8,128)S(1)}, u32[]{:S(2)}, u32[]{:S(2)}) collective-permute-start(f32[8,128]{1,0:T(8,128)S(1)} %tail.3.refs_3_), channel_id=1, source_target_pairs={{0,3},{1,0},{2,1},{3,2},{4,7},{5,4},{6,5},{7,6},{8,11},{9,8},{10,9... | collective-permute-start | bytes 12296 | tf_op jit(solution)/shard_map/ppermute | solution.py:364
  70.0 4.0 %collective-permute-start.1 = (f32[8,128]{1,0:T(8,128)S(1)}, f32[8,128]{1,0:T(8,128)S(1)}, u32[]{:S(2)}, u32[]{:S(2)}) collective-permute-start(f32[8,128]{1,0:T(8,128)S(1)} %tail.3.refs_3_), channel_id=1, source_target_pairs={{0,2},{1,3},{2,0},{3,1},{4,6},{5,7},{6,4},{7,5},{8,10},{9,11},{10,... | collective-permute-start | bytes 12296 | tf_op jit(solution)/shard_map/ppermute | solution.py:364
  70.5 3.7 %collective-permute-start = (f32[8,128]{1,0:T(8,128)S(1)}, f32[8,128]{1,0:T(8,128)S(1)}, u32[]{:S(2)}, u32[]{:S(2)}) collective-permute-start(f32[8,128]{1,0:T(8,128)S(1)} %tail.3.refs_3_), channel_id=1, source_target_pairs={{0,1},{1,2},{2,3},{3,0},{4,5},{5,6},{6,7},{7,4},{8,9},{9,10},{10,1... | collective-permute-start | bytes 12296 | tf_op jit(solution)/shard_map/ppermute | solution.py:364
  74.2 3.3 %copy-start.1 = (bf16[10,640,640]{2,1,0:T(8,128)(2,1)S(1)}, bf16[10,640,640]{2,1,0:T(8,128)(2,1)}, u32[]{:S(2)}) copy-start(bf16[10,640,640]{2,1,0:T(8,128)(2,1)} %refs_2_.5) | copy-start | bytes 24576004
  84.8 47.1 %slice-start = ((s8[8192000]{0:T(1024)(128)(4,1)}), s8[4194304]{0:T(1024)(128)(4,1)S(1)}, s32[]{:S(2)}) async-start(s8[8192000]{0:T(1024)(128)(4,1)} %bitcast.37), calls=%async_computation.7 | async-start | bytes 8388608
  105.8 26.1 %slice-start.1 = ((s8[8192000]{0:T(1024)(128)(4,1)}), s8[3997696]{0:T(1024)(128)(4,1)S(1)}, s32[]{:S(2)}) async-start(s8[8192000]{0:T(1024)(128)(4,1)} %bitcast.37), calls=%async_computation.8 | async-start | bytes 7995392
  126.9 2.5 %collective-permute-start.5 = (f32[8,128]{1,0:T(8,128)S(1)}, f32[8,128]{1,0:T(8,128)S(1)}, u32[]{:S(2)}, u32[]{:S(2)}) collective-permute-start(f32[8,128]{1,0:T(8,128)S(1)} %tail.4.refs_3_), channel_id=1, source_target_pairs={{0,3},{1,0},{2,1},{3,2},{4,7},{5,4},{6,5},{7,6},{8,11},{9,8},{10,9... | collective-permute-start | bytes 12296 | tf_op jit(solution)/shard_map/ppermute | solution.py:364
  127.0 4.0 %collective-permute-start.4 = (f32[8,128]{1,0:T(8,128)S(1)}, f32[8,128]{1,0:T(8,128)S(1)}, u32[]{:S(2)}, u32[]{:S(2)}) collective-permute-start(f32[8,128]{1,0:T(8,128)S(1)} %tail.4.refs_3_), channel_id=1, source_target_pairs={{0,2},{1,3},{2,0},{3,1},{4,6},{5,7},{6,4},{7,5},{8,10},{9,11},{10,... | collective-permute-start | bytes 12296 | tf_op jit(solution)/shard_map/ppermute | solution.py:364
  128.3 3.7 %collective-permute-start.3 = (f32[8,128]{1,0:T(8,128)S(1)}, f32[8,128]{1,0:T(8,128)S(1)}, u32[]{:S(2)}, u32[]{:S(2)}) collective-permute-start(f32[8,128]{1,0:T(8,128)S(1)} %tail.4.refs_3_), channel_id=1, source_target_pairs={{0,1},{1,2},{2,3},{3,0},{4,5},{5,6},{6,7},{7,4},{8,9},{9,10},{10,1... | collective-permute-start | bytes 12296 | tf_op jit(solution)/shard_map/ppermute | solution.py:364
  181.0 2.5 %collective-permute-start.8 = (f32[8,128]{1,0:T(8,128)S(1)}, f32[8,128]{1,0:T(8,128)S(1)}, u32[]{:S(2)}, u32[]{:S(2)}) collective-permute-start(f32[8,128]{1,0:T(8,128)S(1)} %tail.5.refs_3_), channel_id=1, source_target_pairs={{0,3},{1,0},{2,1},{3,2},{4,7},{5,4},{6,5},{7,6},{8,11},{9,8},{10,9... | collective-permute-start | bytes 12296 | tf_op jit(solution)/shard_map/ppermute | solution.py:364
  182.5 4.0 %collective-permute-start.7 = (f32[8,128]{1,0:T(8,128)S(1)}, f32[8,128]{1,0:T(8,128)S(1)}, u32[]{:S(2)}, u32[]{:S(2)}) collective-permute-start(f32[8,128]{1,0:T(8,128)S(1)} %tail.5.refs_3_), channel_id=1, source_target_pairs={{0,2},{1,3},{2,0},{3,1},{4,6},{5,7},{6,4},{7,5},{8,10},{9,11},{10,... | collective-permute-start | bytes 12296 | tf_op jit(solution)/shard_map/ppermute | solution.py:364
  183.2 3.7 %collective-permute-start.6 = (f32[8,128]{1,0:T(8,128)S(1)}, f32[8,128]{1,0:T(8,128)S(1)}, u32[]{:S(2)}, u32[]{:S(2)}) collective-permute-start(f32[8,128]{1,0:T(8,128)S(1)} %tail.5.refs_3_), channel_id=1, source_target_pairs={{0,1},{1,2},{2,3},{3,0},{4,5},{5,6},{6,7},{7,4},{8,9},{9,10},{10,1... | collective-permute-start | bytes 12296 | tf_op jit(solution)/shard_map/ppermute | solution.py:364

commit v3 on v1

v3 whole, which is shorter than its diff:
```python
import functools
import math

import jax
import jax.numpy as jnp
from jax import lax
from jax.experimental import pallas as pl
from jax.experimental.pallas import tpu as pltpu
from jax.sharding import Mesh
from jax.sharding import PartitionSpec as P

ZS, YS, CS, XS = 8, 4, 2, 4
BAND = ("z", "y", "c")
GROUPS = 3
SHARES = 4
PIECE = 40
PIECES = 16
SUB = 8
LANES = 128
SPARE = GROUPS * PIECE
F32 = jnp.float32
BF16 = jnp.bfloat16
UNROLL = 2


def lane_of(rows=SUB):
    return lax.broadcasted_iota(jnp.int32, (rows, LANES), 1)


def scatter_rows(value, acc_ref, slot, chunk_rows, slots):
    lane = lane_of()
    for piece in range(PIECES):
        first = piece * PIECE
        tile, offset = first // LANES, first % LANES
        out = jnp.zeros((SUB, LANES), F32)
        for group in reversed(range(GROUPS)):
            rows = slice(group * SUB, (group + 1) * SUB)
            source = value[rows, tile * LANES : (tile + 1) * LANES]
            if offset + PIECE > LANES:
                following = value[rows, (tile + 1) * LANES : (tile + 2) * LANES]
                source = jnp.where(lane >= offset, source, following)
            shift = (group * PIECE - offset) % LANES
            if shift:
                source = pltpu.roll(source, shift, 1)
            out = jnp.where(lane < (group + 1) * PIECE, source, out)
        acc_ref[pl.ds(piece * SHARES * chunk_rows + slot, SUB, stride=slots), :] = out


def gather_rows(held_ref, slot, chunk_rows, slots, lat_tiles):
    lane = lane_of()
    tiles = [[None] * lat_tiles for _ in range(GROUPS)]
    for piece in range(PIECES):
        first = piece * PIECE
        tile, offset = first // LANES, first % LANES
        rows = held_ref[pl.ds(piece * SHARES * chunk_rows + slot, SUB, stride=slots), :]
        for group in range(GROUPS):
            shift = (offset - group * PIECE) % LANES
            moved = pltpu.roll(rows, shift, 1) if shift else rows
            known = tiles[group][tile]
            tiles[group][tile] = moved if known is None else jnp.where(lane >= offset, moved, known)
            if offset + PIECE > LANES:
                tiles[group][tile + 1] = moved
    return jnp.concatenate([jnp.concatenate(row, axis=1) for row in tiles], axis=0)


def square_sum(parts):
    total = None
    for part in parts:
        for group in range(GROUPS):
            block = part[group * SUB : (group + 1) * SUB, :]
            total = block * block if total is None else total + block * block
    return total


def triangle_tile(wave, tile):
    return lane_of(GROUPS * SUB) + tile * LANES >= wave


def band_index():
    return (lax.axis_index("z") * YS + lax.axis_index("y")) * CS + lax.axis_index("c")


def wave_of(waves_ref, slots, slot):
    return waves_ref[band_index() * slots + slot]


def flat_rows(slot, group, tile, part, tiles):
    first = ((slot * 2 + part) * GROUPS + group) * SHARES * tiles + tile
    return pl.ds(first, SHARES, stride=tiles)


def first_kernel(slots, chunk_rows, waves_ref, vec_ref, leg_ref, res_ref, out_ref, norm_ref, acc_ref, turn_ref):
    tiles = leg_ref.shape[1] // LANES
    norm_ref[...] = jnp.zeros_like(norm_ref)

    def step(slot, carry):
        wave = wave_of(waves_ref, slots, slot)
        parts = []
        for tile in range(tiles):
            cols = slice(tile * LANES, (tile + 1) * LANES)
            for group in range(GROUPS):
                for part in range(2):
                    rows = vec_ref[flat_rows(slot, group, tile, part, tiles), :]
                    turn_ref[pl.ds(group * SUB + part, SHARES, stride=2), :] = rows
            parts.append(jnp.where(triangle_tile(wave, tile), turn_ref[...], 0.0))
            res_ref[slot, :, cols] = parts[-1]
        norm_ref[...] += square_sum(parts)
        forward(jnp.concatenate(parts, axis=1), leg_ref, acc_ref, slot, slots, chunk_rows)
        return carry

    lax.fori_loop(0, slots, step, 0, unroll=UNROLL)
    out_ref[...] = acc_ref[...].astype(BF16)


def forward(vector, leg_ref, acc_ref, slot, slots, chunk_rows):
    coeffs = jnp.dot(vector.astype(BF16), leg_ref[slot], preferred_element_type=F32)
    scatter_rows(coeffs, acc_ref, slot, chunk_rows, slots)


def sums_of(sum_refs, chunk_rows):
    total = sum_refs[0][...]
    for ref in sum_refs[1:]:
        total = total + ref[...]
    total = total * (1.0 / chunk_rows)
    lane = lane_of()
    norm = jnp.sum(jnp.where((lane >= SPARE) & (lane < SPARE + 3), total, 0.0), axis=(0, 1), keepdims=True)
    energy = jnp.sum(jnp.where((lane >= SPARE + 3) & (lane < SPARE + 6), total, 0.0), axis=(0, 1), keepdims=True)
    return norm, norm + energy


def back_kernel(slots, chunk_rows, waves_ref, home_ref, leg_ref, adj_ref, held_ref):
    held_ref[...] = home_ref[...].astype(F32)
    tiles = leg_ref.shape[2] // LANES

    def step(slot, carry):
        wave = wave_of(waves_ref, slots, slot)
        home = gather_rows(held_ref, slot, chunk_rows, slots, tiles).astype(BF16)
        adjoint = lax.dot_general(home, leg_ref[slot], (((1,), (1,)), ((), ())), preferred_element_type=F32)
        for tile in range(leg_ref.shape[1] // LANES):
            cols = slice(tile * LANES, (tile + 1) * LANES)
            adj_ref[slot, :, cols] = jnp.where(triangle_tile(wave, tile), adjoint[:, cols], 0.0)
        return carry

    lax.fori_loop(0, slots, step, 0, unroll=UNROLL)


def scalar_row(value):
    return jnp.broadcast_to(value, (1, LANES))


def middle_kernel(stage, slots, chunk_rows, *refs):
    if stage == 0:
        sum_a, sum_b, sum_c, sum_d, leg_ref, adj_ref, res_ref, *refs = refs
    else:
        sum_a, sum_b, sum_c, sum_d, leg_ref, adj_ref, res_ref, last_ref, past_ref, *refs = refs
    new_ref, along_ref, out_ref, norm_ref, hist_ref, acc_ref = refs
    norm, product = sums_of((sum_a, sum_b, sum_c, sum_d), chunk_rows)
    hist_ref[...] = jnp.zeros_like(hist_ref)
    if stage == 0:
        alpha = norm / product
        beta = jnp.zeros_like(norm)
        hist_ref[2:3, :] = scalar_row(alpha)
    else:
        beta = norm / past_ref[0:1, 0:1]
        alpha = norm / (product - beta * norm / past_ref[1:2, 0:1])
        hist_ref[2:3, :] = past_ref[2:3, :]
        hist_ref[3:4, :] = scalar_row(alpha)
    hist_ref[0:1, :] = scalar_row(norm)
    hist_ref[1:2, :] = scalar_row(alpha)
    hist_ref[4:5, :] = scalar_row(beta)
    norm_ref[...] = jnp.zeros_like(norm_ref)

    def step(slot, carry):
        alpha = hist_ref[1:2, :]
        beta = hist_ref[4:5, :]
        parts = []
        for tile in range(leg_ref.shape[1] // LANES):
            cols = slice(tile * LANES, (tile + 1) * LANES)
            res = res_ref[slot, :, cols]
            along = res + adj_ref[slot, :, cols]
            if stage > 0:
                along = along + beta * last_ref[slot, :, cols]
            along_ref[slot, :, cols] = along
            part = res - alpha * along
            new_ref[slot, :, cols] = part
            parts.append(part)
        norm_ref[...] += square_sum(parts)
        forward(jnp.concatenate(parts, axis=1), leg_ref, acc_ref, slot, slots, chunk_rows)
        return carry

    lax.fori_loop(0, slots, step, 0, unroll=UNROLL)
    out_ref[...] = acc_ref[...].astype(BF16)


def last_kernel(slots, chunk_rows, *refs):
    sum_a, sum_b, sum_c, sum_d, adj_ref, res0_ref, res1_ref, res2_ref, last_ref, past_ref, *refs = refs
    sol_ref, fin_ref, turn_ref = refs
    norm, product = sums_of((sum_a, sum_b, sum_c, sum_d), chunk_rows)
    beta = norm / past_ref[0:1, 0:1]
    alpha = scalar_row(norm / (product - beta * norm / past_ref[1:2, 0:1]))
    beta = scalar_row(beta)
    alpha0, alpha1, beta1 = past_ref[2:3, :], past_ref[3:4, :], past_ref[4:5, :]
    tiles = adj_ref.shape[2] // LANES
    height = GROUPS * SUB

    def step(slot, carry):
        for tile in range(tiles):
            cols = slice(tile * LANES, (tile + 1) * LANES)
            res2 = res2_ref[slot, :, cols]
            along = res2 + adj_ref[slot, :, cols] + beta * last_ref[slot, :, cols]
            first = res0_ref[slot, :, cols]
            second = res1_ref[slot, :, cols] + beta1 * first
            third = res2 + beta * second
            turn_ref[(2 * tile) * height : (2 * tile + 1) * height, :] = res2 - alpha * along
            turn_ref[(2 * tile + 1) * height : (2 * tile + 2) * height, :] = (
                alpha0 * first + alpha1 * second + alpha * third
            )
            for group in range(GROUPS):
                for part in range(2):
                    rows = flat_rows(slot, group, tile, part, tiles)
                    at = group * SUB + part
                    fin_ref[rows, :] = turn_ref[pl.ds((2 * tile) * height + at, SHARES, stride=2), :]
                    sol_ref[rows, :] = turn_ref[pl.ds((2 * tile + 1) * height + at, SHARES, stride=2), :]
        return carry

    lax.fori_loop(0, slots, step, 0)


def fourier_kernel(chunk_rows, slots, norm_factor, waves_ref, out_ref):
    rows = 32
    lon_count = out_ref.shape[1]
    lane = lax.broadcasted_iota(jnp.int32, (rows, LANES), 1).astype(F32)
    local = lax.broadcasted_iota(jnp.int32, (rows, LANES), 0)

    def step(index, carry):
        at = pl.multiple_of(index * rows, rows)
        wave = waves_ref[pl.ds(at, rows), :].astype(F32)
        row = (local + at).astype(F32)
        within = row - chunk_rows * jnp.floor((row + 0.5) * (1.0 / chunk_rows))
        quarter = jnp.where(within > slots - 0.5, 0.25 * lon_count, 0.0)
        cosine, sine = turn(wave * lane + quarter, lon_count)
        cosine = cosine * norm_factor
        sine = sine * norm_factor
        step_cos, step_sin = turn(wave * float(LANES), lon_count)
        for tile in range(lon_count // LANES):
            out_ref[pl.ds(at, rows), tile * LANES : (tile + 1) * LANES] = cosine.astype(BF16)
            cosine, sine = cosine * step_cos - sine * step_sin, sine * step_cos + cosine * step_sin
        return carry

    lax.fori_loop(0, waves_ref.shape[0] // rows, step, 0)


def weight_kernel(*refs):
    *near_refs, out_ref, held_ref = refs
    height = near_refs[0].shape[0]
    for turn_at, near_ref in enumerate(near_refs):
        held_ref[turn_at, :height, :] = near_ref[...]
    share = lax.rem(band_index(), SHARES)
    for place in range(SHARES):
        out_ref[place * height : (place + 1) * height, :] = held_ref[jnp.bitwise_xor(share, place), :height, :]


def turn(phase, period):
    phase = phase - period * jnp.floor(phase * (1.0 / period) + 0.5)
    quadrant = jnp.floor(phase * (4.0 / period) + 0.5)
    angle = (phase - quadrant * (0.25 * period)) * (2.0 * math.pi / period)
    sq = angle * angle
    cosine = 1.0 + sq * (-1.0 / 2 + sq * (1.0 / 24 + sq * (-1.0 / 720 + sq * (1.0 / 40320))))
    sine = angle * (1.0 + sq * (-1.0 / 6 + sq * (1.0 / 120 + sq * (-1.0 / 5040 + sq * (1.0 / 362880)))))
    odd = jnp.abs(quadrant) == 1.0
    cos_base = jnp.where(odd, -quadrant * sine, cosine)
    sin_base = jnp.where(odd, quadrant * cosine, sine)
    back = jnp.abs(quadrant) == 2.0
    return jnp.where(back, -cos_base, cos_base), jnp.where(back, -sin_base, sin_base)


def pieces_of(value):
    high = value.astype(BF16).astype(F32)
    middle = (value - high).astype(BF16).astype(F32)
    low = (value - high - middle).astype(BF16).astype(F32)
    return high, middle, low


def grid_kernel(x_ref, table_ref, weight_ref, norm_ref, out_ref, turned_ref, wide_ref):
    count, lons = table_ref.shape
    step = 256
    turned_ref[...] = x_ref[...].astype(F32).T.astype(BF16)
    energy = jnp.zeros((SUB, step), F32)
    for first in range(0, lons, step):
        cols = slice(first, first + step)
        grid = jnp.dot(turned_ref[...], table_ref[:, cols], preferred_element_type=F32)
        weight = weight_ref[:, cols]
        weighted = []
        for group in range(GROUPS):
            rows = grid[group * PIECE : (group + 1) * PIECE]
            product = weight * rows
            weighted.append(product)
            square = product * rows
            for block in range(0, PIECE, SUB):
                energy = energy + square[block : block + SUB]
        weighted.append(jnp.zeros((LANES - SPARE, step), F32))
        wide_ref[cols, :] = jnp.concatenate(weighted, axis=0).T.astype(BF16)
    lane = lane_of(1)
    spare = jnp.zeros((1, LANES), F32)
    values = pieces_of(jnp.sum(norm_ref[...], axis=(0, 1), keepdims=True))
    values = values + pieces_of(jnp.sum(energy, axis=(0, 1), keepdims=True))
    for place, value in enumerate(values):
        spare = jnp.where(lane == SPARE + place, value, spare)
    for first in range(0, count, step):
        rows = slice(first, first + step)
        back = jnp.dot(table_ref[rows, :], wide_ref[...], preferred_element_type=F32)
        out_ref[rows, :] = jnp.where(lane >= SPARE, spare, back).astype(BF16)


def tail_kernel(x_ref, out_ref):
    total = jnp.zeros((SUB, LANES), F32)
    block = 2 * SUB
    for first in range(0, x_ref.shape[0], block):
        value = x_ref[first : first + block, :].astype(F32)
        total = total + value[:SUB] + value[SUB:]
    out_ref[...] = total


def exchange(payload, parts):
    rows = payload.shape[0]
    packed = payload.reshape(parts, rows // parts // 2, 2, LANES)
    return lax.all_to_all(packed, BAND, 0, 0, tiled=True).reshape(rows, LANES)


def call(kernel, name, outs, ins, scratch=(), vmem=24, flops=2_000_000_000):
    return pl.pallas_call(
        kernel,
        in_specs=ins,
        out_specs=[pl.BlockSpec(memory_space=pltpu.VMEM)] * len(outs),
        out_shape=outs,
        scratch_shapes=scratch,
        compiler_params=pltpu.CompilerParams(vmem_limit_bytes=vmem * 1024 * 1024),
        cost_estimate=pl.CostEstimate(flops=flops, bytes_accessed=1_000_000, transcendentals=0),
        name=name,
    )


def on_device(right_side, legendre, wave_map, obs_weight):
    slots, degrees, lats = legendre.shape
    lon_count = obs_weight.shape[1]
    bands = ZS * YS * CS
    rows = bands * 2 * slots
    chunk_rows = 2 * slots
    smem = pl.BlockSpec(memory_space=pltpu.SMEM)
    vmem = pl.BlockSpec(memory_space=pltpu.VMEM)
    flat = right_side.reshape(-1, LANES)
    spread = jnp.broadcast_to(wave_map.reshape(bands, 1, slots), (bands, 2, slots)).reshape(rows, 1)
    spread = jnp.broadcast_to(spread, (rows, LANES))
    flat, spread = lax.optimization_barrier((flat, spread))

    vec_shape = jax.ShapeDtypeStruct((slots, GROUPS * SUB, degrees), F32)
    payload_shape = jax.ShapeDtypeStruct((rows, LANES), BF16)
    small_shape = jax.ShapeDtypeStruct((SUB, LANES), F32)
    flat_shape = jax.ShapeDtypeStruct(flat.shape, F32)
    held = pltpu.VMEM((rows, LANES), F32)

    (table,) = call(
        functools.partial(fourier_kernel, chunk_rows, slots, 1.0 / math.sqrt(wave_map.shape[0])),
        "fourier",
        [jax.ShapeDtypeStruct((rows, lon_count), BF16)],
        [vmem],
        flops=4_000_000_000,
    )(spread)
    flat, table = lax.optimization_barrier((flat, table))

    res, payload, norm = call(
        functools.partial(first_kernel, slots, chunk_rows),
        "first",
        [vec_shape, payload_shape, small_shape],
        [smem, vmem, vmem],
        [held, pltpu.VMEM((GROUPS * SUB, LANES), F32)],
    )(wave_map, flat, legendre)

    near = [obs_weight]
    for turn_at in range(1, SHARES):
        pairs = [(at, at ^ turn_at) for at in range(YS * CS)]
        near.append(lax.ppermute(obs_weight, ("y", "c"), pairs))
    (weight,) = call(
        weight_kernel,
        "weight",
        [jax.ShapeDtypeStruct((PIECE, lon_count), F32)],
        [vmem] * SHARES,
        [pltpu.VMEM((SHARES, 2 * SUB, lon_count), F32)],
    )(*near)
    payload, table, weight = lax.optimization_barrier((payload, table, weight))

    def reach(payload, norm):
        arrived = exchange(payload, bands)
        (back,) = call(
            grid_kernel,
            "grid",
            [payload_shape],
            [vmem] * 4,
            [pltpu.VMEM((LANES, rows), BF16), pltpu.VMEM((lon_count, LANES), BF16)],
        )(arrived, table, weight, norm)
        home = exchange(back, bands)
        (sums,) = call(tail_kernel, "tail", [small_shape], [vmem])(home)
        others = [lax.ppermute(sums, "x", [(i, (i + k) % XS) for i in range(XS)]) for k in range(1, XS)]
        (adjoint,) = call(
            functools.partial(back_kernel, slots, chunk_rows),
            "back",
            [vec_shape],
            [smem, vmem, vmem],
            [held],
            flops=8_000_000_000,
        )(wave_map, home, legendre)
        return adjoint, [sums] + others

    residuals = [res]
    carried = []
    for stage in range(2):
        adjoint, sums = reach(payload, norm)
        operands = [*sums, legendre, adjoint, residuals[-1], *carried]
        res, along, payload, norm, past = call(
            functools.partial(middle_kernel, stage, slots, chunk_rows),
            f"middle{stage}",
            [vec_shape, vec_shape, payload_shape, small_shape, small_shape],
            [vmem] * len(operands),
            [held],
        )(*operands)
        residuals.append(res)
        carried = [along, past]
    adjoint, sums = reach(payload, norm)
    solution, residual = call(
        functools.partial(last_kernel, slots, chunk_rows),
        "last",
        [flat_shape, flat_shape],
        [vmem] * 10,
        [pltpu.VMEM((2 * GROUPS * SUB * (degrees // LANES), LANES), F32)],
    )(*sums, adjoint, *residuals, along, past)
    return solution.reshape(right_side.shape), residual.reshape(right_side.shape)


def solution(mesh):
    split = Mesh(mesh.devices.reshape(ZS, YS, CS, XS), ("z", "y", "c", "x"))
    return jax.shard_map(
        on_device,
        mesh=split,
        in_specs=(P(BAND, None, "x", None, None), P(BAND, None, None), P(), P(BAND, None)),
        out_specs=(P(BAND, None, "x", None, None), P(BAND, None, "x", None, None)),
        check_vma=False,
    )
```

time: 235 us -> 170 us (0.72); the launches traced: 231 us -> 170 us
  Pallas kernels: 70.1 us -> 30.6 us
  blocking collectives: 106 us -> 122 us
  local copies, waits for them, and re-layouts: 16.1 us -> 1.23 us
  waiting for transfers between devices: 12.4 us -> 0.26 us
  starting transfers between devices: 25.8 us -> 14.5 us
    pallas_call x11 -> x15, Pallas kernels: 70.1 us -> 30.6 us  [the longest x3 11.1 us: reach(): call(functools.partial(back_kernel, slots, chunk_rows), 'back', [vec_shap...]
    all_to_all x2 -> x0, starting transfers between devices: 18 us -> none  [the longest x1 11.3 us: exchange(): lax.all_to_all(packed, EXCHANGE, 0, 0, tiled=True).reshape(rows, LANES)]
    all_to_all x5 -> x6, blocking collectives: 106 us -> 122 us  [exchange(): return lax.all_to_all(packed, BAND, 0, 0, tiled=True).reshape(rows, LANES)]
    ppermute x9, waiting for transfers between devices: 10.2 us -> 0.25 us  [reach(): lax.ppermute(sums, 'x', [(i, (i + k) % XS) for i in range(XS)])]
    reshape x8 -> x0, local copies, waits for them, and re-layouts: 9.27 us -> none  [the longest x2 2.91 us: unpack(): return value.reshape(right_side.shape)]
    ppermute x0 -> x3, starting transfers between devices: none -> 4.92 us  [on_device(): near.append(lax.ppermute(obs_weight, ('y', 'c'), pairs))]
  transfers between devices with their start and end apart: 11 -> 12, of which waited for: 9 -> 1; matrix products, arithmetic and copies ran while one was open for 3% -> 1% of each run, Pallas kernels for 8% -> 10%
where the time goes in v3:
time: 170 us
  blocking collectives  122 us (72%)
  Pallas kernels  30.6 us (18%)
  starting transfers between devices  14.5 us (9%)
    all_to_all x6, blocking collectives, exchange(): return lax.all_to_all(packed, BAND, 0, 0, tiled=True).reshape(rows, LANES)  122 us
    pallas_call x3, Pallas kernels, reach(): call(functools.partial(back_kernel, slots, chunk_rows), 'back', [vec_shap...  11.1 us
    ppermute x9, starting transfers between devices, reach(): lax.ppermute(sums, 'x', [(i, (i + k) % XS) for i in range(XS)])  9.54 us
    pallas_call x3, Pallas kernels, reach(): call(grid_kernel, 'grid', [payload_shape], [vmem] * 4, [pltpu.VMEM((LANES...  5.48 us
    ppermute x3, starting transfers between devices, on_device(): near.append(lax.ppermute(obs_weight, ('y', 'c'), pairs))  4.92 us
    pallas_call x2, Pallas kernels, on_device(): call(functools.partial(middle_kernel, stage, slots, chunk_rows), f'middle...  4.91 us
    pallas_call x1, Pallas kernels, on_device(): call(functools.partial(fourier_kernel, chunk_rows, slots, 1.0 / math.sqrt...  3.54 us
  transfers between devices with their start and end apart: 12, of which 1 were waited for; matrix products, arithmetic and copies ran while one was open for 1% of the time, Pallas kernels for 10%

profile of v3, /device:TPU:1, one launch (start us, length us, event | category | flops | bytes accessed | tf_op | source)
XLA Modules:
  0.0 169.7 jit_solution(12979122639941000297)
XLA Ops:
  0.6 0.0 copy-start.1
  0.6 0.0 copy-start
  0.6 2.2 %collective-permute-start.1 = (f32[10,1280]{1,0:T(8,128)}, f32[10,1280]{1,0:T(8,128)S(1)}, u32[]{:S(2)}, u32[]{:S(2)}) collective-permute-start(f32[10,1280]{1,0:T(8,128)} %refs_0_.1), channel_id=1, source_target_pairs={{0,8},{4,12},{8,0},{12,4},{16,24},{20,28},{24,16},{28,20},{1,9},{5... | collective-permute-start | bytes 153608 | tf_op jit(solution)/shard_map/ppermute | solution.py:382
  2.9 1.2 collective-permute-start
  4.0 1.5 collective-permute-start.2
  5.6 0.8 broadcast_in_dim.14
  6.4 0.1 broadcast_in_dim.16
  6.6 0.0 slice-start
  6.6 0.2 broadcast_in_dim.17.waves_ref
  6.8 0.0 slice-start.1
  6.8 0.0 copy-start.2
  6.8 3.5 %fourier.1.table_ref = bf16[1280,1280]{1,0:T(8,128)(2,1)S(1)} custom-call(s32[1280,128]{1,0:T(8,128)S(1)} %broadcast_in_dim.17.waves_ref), custom_call_target="tpu_custom_call" | custom-call | flops 4000000000 | bytes 1000000 | tf_op jit(solution)/shard_map/fourier/pallas_call | solution.py:362
  10.4 0.0 copy-done.1
  10.4 0.0 copy-done
  10.4 0.0 slice-done
  10.4 0.0 slice-done.1
  10.4 3.0 %first.1 = (f32[10,24,640]{2,1,0:T(8,128)S(1)}, bf16[1280,128]{1,0:T(8,128)(2,1)S(1)}, f32[8,128]{1,0:T(8,128)S(1)}) custom-call(s32[640]{0:T(1024)S(1)} %copy-done.1, f32[1200,128]{1,0:T(8,128)S(1)} %bitcast.17, bf16[10,640,640]{2,1,0:T(8,128)(2,1)S(1)} %bitcast.16), custom_call_target="tpu_custom_call" | custom-call | flops 2000000000 | bytes 1000000 | tf_op jit(solution)/shard_map/first/pallas_call | solution.py:371
  13.4 0.0 collective-permute-done.1.refs_2_
  13.4 0.0 collective-permute-done.refs_1_
  13.4 0.0 collective-permute-done.2.refs_3_
  13.4 0.0 copy-done.2
  13.5 0.1 weight.1.weight_ref
  13.5 24.5 %all_to_all.30 = bf16[64,10,2,128]{3,2,1,0:T(2,128)(2,1)S(1)} all-to-all(bf16[64,10,2,128]{3,2,1,0:T(2,128)(2,1)S(1)} %bitcast.18), channel_id=1, replica_groups=mesh['z'=8,'y'=4,'c'=2,'x'=4] {'z','y','c'}, dimensions={0} | all-to-all | bytes 655360 | tf_op jit(solution)/shard_map/all_to_all | solution.py:327
  38.0 1.8 %grid.3 = bf16[1280,128]{1,0:T(8,128)(2,1)S(1)} custom-call(bf16[1280,128]{1,0:T(8,128)(2,1)S(1)} %bitcast.29, bf16[1280,1280]{1,0:T(8,128)(2,1)S(1)} %fourier.1.table_ref, f32[40,1280]{1,0:T(8,128)S(1)} %weight.1.weight_ref, f32[8,128]{1,0:T(8,128)S(1)} %get-tuple-element.32.norm_ref), custom_call_target="tpu_custom_call" | custom-call | flops 2000000000 | bytes 1000000 | tf_op jit(solution)/shard_map/grid/pallas_call | solution.py:394
  39.8 19.0 %all_to_all.31 = bf16[64,10,2,128]{3,2,1,0:T(2,128)(2,1)S(1)} all-to-all(bf16[64,10,2,128]{3,2,1,0:T(2,128)(2,1)S(1)} %bitcast.30), channel_id=1, replica_groups=mesh['z'=8,'y'=4,'c'=2,'x'=4] {'z','y','c'}, dimensions={0} | all-to-all | bytes 655360 | tf_op jit(solution)/shard_map/all_to_all | solution.py:327
  58.8 0.2 tail.3.refs_0_
  59.0 2.6 %collective-permute-start.5 = (f32[8,128]{1,0:T(8,128)S(1)}, f32[8,128]{1,0:T(8,128)S(1)}, u32[]{:S(2)}, u32[]{:S(2)}) collective-permute-start(f32[8,128]{1,0:T(8,128)S(1)} %tail.3.refs_0_), channel_id=1, source_target_pairs={{0,3},{1,0},{2,1},{3,2},{4,7},{5,4},{6,5},{7,6},{8,11},{9,8},{10,9... | collective-permute-start | bytes 12296 | tf_op jit(solution)/shard_map/ppermute | solution.py:403
  61.6 0.5 collective-permute-start.4
  62.1 0.6 collective-permute-start.3
  62.7 3.7 %back.3.refs_5_ = f32[10,24,640]{2,1,0:T(8,128)S(1)} custom-call(s32[640]{0:T(1024)S(1)} %copy-done.1, bf16[1280,128]{1,0:T(8,128)(2,1)S(1)} %bitcast.20, bf16[10,640,640]{2,1,0:T(8,128)(2,1)S(1)} %bitcast.16), custom_call_target="tpu_custom_call" | custom-call | flops 8000000000 | bytes 1000000 | tf_op jit(solution)/shard_map/back/pallas_call | solution.py:404
  66.4 0.0 collective-permute-done.5.refs_3_
  66.4 0.0 collective-permute-done.4.refs_2_
  66.4 0.0 collective-permute-done.3.refs_1_
  66.5 2.4 %middle0.1 = (f32[10,24,640]{2,1,0:T(8,128)S(1)}, f32[10,24,640]{2,1,0:T(8,128)S(1)}, bf16[1280,128]{1,0:T(8,128)(2,1)S(1)}, f32[8,128]{1,0:T(8,128)S(1)}, f32[8,128]{1,0:T(8,128)S(1)}) custom-call(f32[8,128]{1,0:T(8,128)S(1)} %tail.3.refs_0_, f32[8,128]{1,0:T(8,128)S(1)} %collective-permute-done.3.refs_1_, f32[8,128]{1,0:T(8,128)S(1)} %collective-permute-done.4.refs_2_, ...), custom_call_target="tpu_custom_call" | custom-call | flops 2000000000 | bytes 1000000 | tf_op jit(solution)/shard_map/middle0/pallas_call | solution.py:419
  68.9 20.0 %all_to_all.32 = bf16[64,10,2,128]{3,2,1,0:T(2,128)(2,1)S(1)} all-to-all(bf16[64,10,2,128]{3,2,1,0:T(2,128)(2,1)S(1)} %bitcast.26), channel_id=1, replica_groups=mesh['z'=8,'y'=4,'c'=2,'x'=4] {'z','y','c'}, dimensions={0} | all-to-all | bytes 655360 | tf_op jit(solution)/shard_map/all_to_all | solution.py:327
  88.9 1.8 %grid.4 = bf16[1280,128]{1,0:T(8,128)(2,1)S(1)} custom-call(bf16[1280,128]{1,0:T(8,128)(2,1)S(1)} %bitcast.31, bf16[1280,1280]{1,0:T(8,128)(2,1)S(1)} %fourier.1.table_ref, f32[40,1280]{1,0:T(8,128)S(1)} %weight.1.weight_ref, f32[8,128]{1,0:T(8,128)S(1)} %get-tuple-element.35.norm_ref), custom_call_target="tpu_custom_call" | custom-call | flops 2000000000 | bytes 1000000 | tf_op jit(solution)/shard_map/grid/pallas_call | solution.py:394
  90.8 19.2 %all_to_all.33 = bf16[64,10,2,128]{3,2,1,0:T(2,128)(2,1)S(1)} all-to-all(bf16[64,10,2,128]{3,2,1,0:T(2,128)(2,1)S(1)} %bitcast.32), channel_id=1, replica_groups=mesh['z'=8,'y'=4,'c'=2,'x'=4] {'z','y','c'}, dimensions={0} | all-to-all | bytes 655360 | tf_op jit(solution)/shard_map/all_to_all | solution.py:327
  110.0 0.2 tail.4.refs_0_
  110.1 2.0 %collective-permute-start.8 = (f32[8,128]{1,0:T(8,128)S(1)}, f32[8,128]{1,0:T(8,128)S(1)}, u32[]{:S(2)}, u32[]{:S(2)}) collective-permute-start(f32[8,128]{1,0:T(8,128)S(1)} %tail.4.refs_0_), channel_id=1, source_target_pairs={{0,3},{1,0},{2,1},{3,2},{4,7},{5,4},{6,5},{7,6},{8,11},{9,8},{10,9... | collective-permute-start | bytes 12296 | tf_op jit(solution)/shard_map/ppermute | solution.py:403
  112.1 1.2 collective-permute-start.7
  113.3 0.0 collective-permute-start.6
  113.3 3.7 %back.4.refs_5_ = f32[10,24,640]{2,1,0:T(8,128)S(1)} custom-call(s32[640]{0:T(1024)S(1)} %copy-done.1, bf16[1280,128]{1,0:T(8,128)(2,1)S(1)} %bitcast.22, bf16[10,640,640]{2,1,0:T(8,128)(2,1)S(1)} %bitcast.16), custom_call_target="tpu_custom_call" | custom-call | flops 8000000000 | bytes 1000000 | tf_op jit(solution)/shard_map/back/pallas_call | solution.py:404
  117.0 0.0 collective-permute-done.8.refs_3_
  117.1 0.0 collective-permute-done.7.refs_2_
  117.1 0.1 collective-permute-done.6.refs_1_
  117.2 2.5 %middle1.1 = (f32[10,24,640]{2,1,0:T(8,128)S(1)}, f32[10,24,640]{2,1,0:T(8,128)S(1)}, bf16[1280,128]{1,0:T(8,128)(2,1)S(1)}, f32[8,128]{1,0:T(8,128)S(1)}, f32[8,128]{1,0:T(8,128)S(1)}) custom-call(f32[8,128]{1,0:T(8,128)S(1)} %tail.4.refs_0_, f32[8,128]{1,0:T(8,128)S(1)} %collective-permute-done.6.refs_1_, f32[8,128]{1,0:T(8,128)S(1)} %collective-permute-done.7.refs_2_, ...), custom_call_target="tpu_custom_call" | custom-call | flops 2000000000 | bytes 1000000 | tf_op jit(solution)/shard_map/middle1/pallas_call | solution.py:419
  119.7 20.5 %all_to_all.34 = bf16[64,10,2,128]{3,2,1,0:T(2,128)(2,1)S(1)} all-to-all(bf16[64,10,2,128]{3,2,1,0:T(2,128)(2,1)S(1)} %bitcast.25), channel_id=1, replica_groups=mesh['z'=8,'y'=4,'c'=2,'x'=4] {'z','y','c'}, dimensions={0} | all-to-all | bytes 655360 | tf_op jit(solution)/shard_map/all_to_all | solution.py:327
  140.3 1.8 %grid.5 = bf16[1280,128]{1,0:T(8,128)(2,1)S(1)} custom-call(bf16[1280,128]{1,0:T(8,128)(2,1)S(1)} %bitcast.27, bf16[1280,1280]{1,0:T(8,128)(2,1)S(1)} %fourier.1.table_ref, f32[40,1280]{1,0:T(8,128)S(1)} %weight.1.weight_ref, f32[8,128]{1,0:T(8,128)S(1)} %get-tuple-element.40.norm_ref), custom_call_target="tpu_custom_call" | custom-call | flops 2000000000 | bytes 1000000 | tf_op jit(solution)/shard_map/grid/pallas_call | solution.py:394
  142.1 19.0 %all_to_all.35 = bf16[64,10,2,128]{3,2,1,0:T(2,128)(2,1)S(1)} all-to-all(bf16[64,10,2,128]{3,2,1,0:T(2,128)(2,1)S(1)} %bitcast.28), channel_id=1, replica_groups=mesh['z'=8,'y'=4,'c'=2,'x'=4] {'z','y','c'}, dimensions={0} | all-to-all | bytes 655360 | tf_op jit(solution)/shard_map/all_to_all | solution.py:327
  161.1 0.2 tail.5.refs_0_
  161.3 2.0 %collective-permute-start.11 = (f32[8,128]{1,0:T(8,128)S(1)}, f32[8,128]{1,0:T(8,128)S(1)}, u32[]{:S(2)}, u32[]{:S(2)}) collective-permute-start(f32[8,128]{1,0:T(8,128)S(1)} %tail.5.refs_0_), channel_id=1, source_target_pairs={{0,3},{1,0},{2,1},{3,2},{4,7},{5,4},{6,5},{7,6},{8,11},{9,8},{10,9... | collective-permute-start | bytes 12296 | tf_op jit(solution)/shard_map/ppermute | solution.py:403
  163.3 0.5 collective-permute-start.10
  163.8 0.2 collective-permute-start.9
  163.9 3.7 %back.5.refs_4_ = f32[10,24,640]{2,1,0:T(8,128)S(1)} custom-call(s32[640]{0:T(1024)S(1)} %copy-done.1, bf16[1280,128]{1,0:T(8,128)(2,1)S(1)} %bitcast.24, bf16[10,640,640]{2,1,0:T(8,128)(2,1)S(1)} %bitcast.16), custom_call_target="tpu_custom_call" | custom-call | flops 8000000000 | bytes 1000000 | tf_op jit(solution)/shard_map/back/pallas_call | solution.py:404
  167.6 0.0 collective-permute-done.11.refs_3_
  167.7 0.0 collective-permute-done.10.refs_2_
  167.7 0.0 collective-permute-done.9.refs_1_
  167.7 2.0 %last.1 = (f32[1200,128]{1,0:T(8,128)}, f32[1200,128]{1,0:T(8,128)}) custom-call(f32[8,128]{1,0:T(8,128)S(1)} %tail.5.refs_0_, f32[8,128]{1,0:T(8,128)S(1)} %collective-permute-done.9.refs_1_, f32[8,128]{1,0:T(8,128)S(1)} %collective-permute-done.10.refs_2_, f32[8,128]{1,0:T(8,128)S(1)} %collective-permute-done.11.refs_3_, f32[10,24,640]{2,1,0:T(8,128)S(1)} %back.5.refs_4_, ...), custom_call_target="tpu_custom_call" | custom-call | flops 2000000000 | bytes 1000000 | tf_op jit(solution)/shard_map/last/pallas_call | solution.py:429
  (2 shorter events, 0.0 us)
Async XLA Ops:
  0.6 9.8 %copy-start.1 = (s32[640]{0:T(1024)S(1)}, s32[640]{0:T(1024)}, u32[]{:S(2)}) copy-start(s32[640]{0:T(1024)} %waves_ref.7) | copy-start | bytes 7684
  0.6 9.8 %copy-start = (f32[10,2,1,12,640]{4,2,3,1,0:T(1,128)S(1)}, f32[10,2,1,12,640]{4,2,3,1,0:T(1,128)}, u32[]{:S(2)}) copy-start(f32[10,2,1,12,640]{4,2,3,1,0:T(1,128)} %param.4) | copy-start | bytes 1843204
  0.6 12.8 %collective-permute-start.1 = (f32[10,1280]{1,0:T(8,128)}, f32[10,1280]{1,0:T(8,128)S(1)}, u32[]{:S(2)}, u32[]{:S(2)}) collective-permute-start(f32[10,1280]{1,0:T(8,128)} %refs_0_.1), channel_id=1, source_target_pairs={{0,8},{4,12},{8,0},{12,4},{16,24},{20,28},{24,16},{28,20},{1,9},{5... | collective-permute-start | bytes 153608 | tf_op jit(solution)/shard_map/ppermute | solution.py:382
  2.9 10.6 %collective-permute-start = (f32[10,1280]{1,0:T(8,128)}, f32[10,1280]{1,0:T(8,128)S(1)}, u32[]{:S(2)}, u32[]{:S(2)}) collective-permute-start(f32[10,1280]{1,0:T(8,128)} %refs_0_.1), channel_id=1, source_target_pairs={{0,4},{4,0},{8,12},{12,8},{16,20},{20,16},{24,28},{28,24},{1,5},{5... | collective-permute-start | bytes 153608 | tf_op jit(solution)/shard_map/ppermute | solution.py:382
  4.0 9.4 %collective-permute-start.2 = (f32[10,1280]{1,0:T(8,128)}, f32[10,1280]{1,0:T(8,128)S(1)}, u32[]{:S(2)}, u32[]{:S(2)}) collective-permute-start(f32[10,1280]{1,0:T(8,128)} %refs_0_.1), channel_id=1, source_target_pairs={{0,12},{4,8},{8,4},{12,0},{16,28},{20,24},{24,20},{28,16},{1,13},{... | collective-permute-start | bytes 153608 | tf_op jit(solution)/shard_map/ppermute | solution.py:382
  6.6 3.8 %slice-start = ((s8[8192000]{0:T(1024)(128)(4,1)}), s8[4194304]{0:T(1024)(128)(4,1)S(1)}, s32[]{:S(2)}) async-start(s8[8192000]{0:T(1024)(128)(4,1)} %bitcast.15), calls=%async_computation.6 | async-start | bytes 8388608
  6.8 3.6 %slice-start.1 = ((s8[8192000]{0:T(1024)(128)(4,1)}), s8[3997696]{0:T(1024)(128)(4,1)S(1)}, s32[]{:S(2)}) async-start(s8[8192000]{0:T(1024)(128)(4,1)} %bitcast.15), calls=%async_computation.7 | async-start | bytes 7995392
  6.8 6.6 %copy-start.2 = (f32[10,1280]{1,0:T(8,128)S(1)}, f32[10,1280]{1,0:T(8,128)}, u32[]{:S(2)}) copy-start(f32[10,1280]{1,0:T(8,128)} %refs_0_.1) | copy-start | bytes 153604
  59.0 7.4 %collective-permute-start.5 = (f32[8,128]{1,0:T(8,128)S(1)}, f32[8,128]{1,0:T(8,128)S(1)}, u32[]{:S(2)}, u32[]{:S(2)}) collective-permute-start(f32[8,128]{1,0:T(8,128)S(1)} %tail.3.refs_0_), channel_id=1, source_target_pairs={{0,3},{1,0},{2,1},{3,2},{4,7},{5,4},{6,5},{7,6},{8,11},{9,8},{10,9... | collective-permute-start | bytes 12296 | tf_op jit(solution)/shard_map/ppermute | solution.py:403
  61.6 4.9 %collective-permute-start.4 = (f32[8,128]{1,0:T(8,128)S(1)}, f32[8,128]{1,0:T(8,128)S(1)}, u32[]{:S(2)}, u32[]{:S(2)}) collective-permute-start(f32[8,128]{1,0:T(8,128)S(1)} %tail.3.refs_0_), channel_id=1, source_target_pairs={{0,2},{1,3},{2,0},{3,1},{4,6},{5,7},{6,4},{7,5},{8,10},{9,11},{10,... | collective-permute-start | bytes 12296 | tf_op jit(solution)/shard_map/ppermute | solution.py:403
  62.1 4.4 %collective-permute-start.3 = (f32[8,128]{1,0:T(8,128)S(1)}, f32[8,128]{1,0:T(8,128)S(1)}, u32[]{:S(2)}, u32[]{:S(2)}) collective-permute-start(f32[8,128]{1,0:T(8,128)S(1)} %tail.3.refs_0_), channel_id=1, source_target_pairs={{0,1},{1,2},{2,3},{3,0},{4,5},{5,6},{6,7},{7,4},{8,9},{9,10},{10,1... | collective-permute-start | bytes 12296 | tf_op jit(solution)/shard_map/ppermute | solution.py:403
  110.1 6.9 %collective-permute-start.8 = (f32[8,128]{1,0:T(8,128)S(1)}, f32[8,128]{1,0:T(8,128)S(1)}, u32[]{:S(2)}, u32[]{:S(2)}) collective-permute-start(f32[8,128]{1,0:T(8,128)S(1)} %tail.4.refs_0_), channel_id=1, source_target_pairs={{0,3},{1,0},{2,1},{3,2},{4,7},{5,4},{6,5},{7,6},{8,11},{9,8},{10,9... | collective-permute-start | bytes 12296 | tf_op jit(solution)/shard_map/ppermute | solution.py:403
  112.1 5.0 %collective-permute-start.7 = (f32[8,128]{1,0:T(8,128)S(1)}, f32[8,128]{1,0:T(8,128)S(1)}, u32[]{:S(2)}, u32[]{:S(2)}) collective-permute-start(f32[8,128]{1,0:T(8,128)S(1)} %tail.4.refs_0_), channel_id=1, source_target_pairs={{0,2},{1,3},{2,0},{3,1},{4,6},{5,7},{6,4},{7,5},{8,10},{9,11},{10,... | collective-permute-start | bytes 12296 | tf_op jit(solution)/shard_map/ppermute | solution.py:403
  113.3 3.9 %collective-permute-start.6 = (f32[8,128]{1,0:T(8,128)S(1)}, f32[8,128]{1,0:T(8,128)S(1)}, u32[]{:S(2)}, u32[]{:S(2)}) collective-permute-start(f32[8,128]{1,0:T(8,128)S(1)} %tail.4.refs_0_), channel_id=1, source_target_pairs={{0,1},{1,2},{2,3},{3,0},{4,5},{5,6},{6,7},{7,4},{8,9},{9,10},{10,1... | collective-permute-start | bytes 12296 | tf_op jit(solution)/shard_map/ppermute | solution.py:403
  161.3 6.4 %collective-permute-start.11 = (f32[8,128]{1,0:T(8,128)S(1)}, f32[8,128]{1,0:T(8,128)S(1)}, u32[]{:S(2)}, u32[]{:S(2)}) collective-permute-start(f32[8,128]{1,0:T(8,128)S(1)} %tail.5.refs_0_), channel_id=1, source_target_pairs={{0,3},{1,0},{2,1},{3,2},{4,7},{5,4},{6,5},{7,6},{8,11},{9,8},{10,9... | collective-permute-start | bytes 12296 | tf_op jit(solution)/shard_map/ppermute | solution.py:403
  163.3 4.4 %collective-permute-start.10 = (f32[8,128]{1,0:T(8,128)S(1)}, f32[8,128]{1,0:T(8,128)S(1)}, u32[]{:S(2)}, u32[]{:S(2)}) collective-permute-start(f32[8,128]{1,0:T(8,128)S(1)} %tail.5.refs_0_), channel_id=1, source_target_pairs={{0,2},{1,3},{2,0},{3,1},{4,6},{5,7},{6,4},{7,5},{8,10},{9,11},{10,... | collective-permute-start | bytes 12296 | tf_op jit(solution)/shard_map/ppermute | solution.py:403
  163.8 3.9 %collective-permute-start.9 = (f32[8,128]{1,0:T(8,128)S(1)}, f32[8,128]{1,0:T(8,128)S(1)}, u32[]{:S(2)}, u32[]{:S(2)}) collective-permute-start(f32[8,128]{1,0:T(8,128)S(1)} %tail.5.refs_0_), channel_id=1, source_target_pairs={{0,1},{1,2},{2,3},{3,0},{4,5},{5,6},{6,7},{7,4},{8,9},{9,10},{10,1... | collective-permute-start | bytes 12296 | tf_op jit(solution)/shard_map/ppermute | solution.py:403

commit v4 on v3

--- a/solution.py
+++ b/solution.py
@@ -20,7 +20,7 @@
 SPARE = GROUPS * PIECE
 F32 = jnp.float32
 BF16 = jnp.bfloat16
-UNROLL = 2
+UNROLL = 10
 
 
 def lane_of(rows=SUB):
@@ -239,12 +239,13 @@
         within = row - chunk_rows * jnp.floor((row + 0.5) * (1.0 / chunk_rows))
         quarter = jnp.where(within > slots - 0.5, 0.25 * lon_count, 0.0)
         cosine, sine = turn(wave * lane + quarter, lon_count)
-        cosine = cosine * norm_factor
-        sine = sine * norm_factor
         step_cos, step_sin = turn(wave * float(LANES), lon_count)
+        before = (cosine * step_cos + sine * step_sin) * norm_factor
+        now = cosine * norm_factor
+        twice = step_cos + step_cos
         for tile in range(lon_count // LANES):
-            out_ref[pl.ds(at, rows), tile * LANES : (tile + 1) * LANES] = cosine.astype(BF16)
-            cosine, sine = cosine * step_cos - sine * step_sin, sine * step_cos + cosine * step_sin
+            out_ref[pl.ds(at, rows), tile * LANES : (tile + 1) * LANES] = now.astype(BF16)
+            before, now = now, twice * now - before
         return carry
 
     lax.fori_loop(0, waves_ref.shape[0] // rows, step, 0)

time: 170 us -> 166 us (0.976)
  Pallas kernels: 30.6 us -> 26.4 us
  transfers between devices with their start and end apart: 12 -> 12, of which waited for: 1 -> 3; matrix products, arithmetic and copies ran while one was open for 1% -> 1% of each run, Pallas kernels for 10% -> 9%
where the time goes in v4:
time: 166 us
  blocking collectives  123 us (74%)
  Pallas kernels  26.4 us (16%)
  starting transfers between devices  13.6 us (8%)
    all_to_all x6, blocking collectives, exchange(): return lax.all_to_all(packed, BAND, 0, 0, tiled=True).reshape(rows, LANES)  123 us
    pallas_call x3, Pallas kernels, reach(): call(functools.partial(back_kernel, slots, chunk_rows), 'back', [vec_shap...  9.53 us
    ppermute x9, starting transfers between devices, reach(): lax.ppermute(sums, 'x', [(i, (i + k) % XS) for i in range(XS)])  8.71 us
    pallas_call x3, Pallas kernels, reach(): call(grid_kernel, 'grid', [payload_shape], [vmem] * 4, [pltpu.VMEM((LANES...  5.47 us
    ppermute x3, starting transfers between devices, on_device(): near.append(lax.ppermute(obs_weight, ('y', 'c'), pairs))  4.92 us
    pallas_call x1, Pallas kernels, on_device(): call(functools.partial(fourier_kernel, chunk_rows, slots, 1.0 / math.sqrt...  3.33 us
    pallas_call x2, Pallas kernels, on_device(): call(functools.partial(middle_kernel, stage, slots, chunk_rows), f'middle...  3.32 us
  transfers between devices with their start and end apart: 12, of which 3 were waited for; matrix products, arithmetic and copies ran while one was open for 1% of the time, Pallas kernels for 9%

profile of v4, /device:TPU:1, one launch (start us, length us, event | category | flops | bytes accessed | tf_op | source)
XLA Modules:
  0.0 166.0 jit_solution(7682797749376844862)
XLA Ops:
  0.6 0.0 copy-start.1
  0.6 0.0 copy-start
  0.6 2.2 %collective-permute-start.1 = (f32[10,1280]{1,0:T(8,128)}, f32[10,1280]{1,0:T(8,128)S(1)}, u32[]{:S(2)}, u32[]{:S(2)}) collective-permute-start(f32[10,1280]{1,0:T(8,128)} %refs_0_.1), channel_id=1, source_target_pairs={{0,8},{4,12},{8,0},{12,4},{16,24},{20,28},{24,16},{28,20},{1,9},{5... | collective-permute-start | bytes 153608 | tf_op jit(solution)/shard_map/ppermute | solution.py:383
  2.9 1.2 collective-permute-start
  4.0 1.5 collective-permute-start.2
  5.6 0.8 broadcast_in_dim.14
  6.4 0.1 broadcast_in_dim.16
  6.6 0.0 slice-start
  6.6 0.2 broadcast_in_dim.17.waves_ref
  6.8 0.0 slice-start.1
  6.8 0.0 copy-start.2
  6.8 3.3 %fourier.1.table_ref = bf16[1280,1280]{1,0:T(8,128)(2,1)S(1)} custom-call(s32[1280,128]{1,0:T(8,128)S(1)} %broadcast_in_dim.17.waves_ref), custom_call_target="tpu_custom_call" | custom-call | flops 4000000000 | bytes 1000000 | tf_op jit(solution)/shard_map/fourier/pallas_call | solution.py:363
  10.2 0.0 copy-done.1
  10.2 0.0 copy-done
  10.2 0.0 slice-done
  10.2 0.0 slice-done.1
  10.2 2.2 %first.1 = (f32[10,24,640]{2,1,0:T(8,128)S(1)}, bf16[1280,128]{1,0:T(8,128)(2,1)S(1)}, f32[8,128]{1,0:T(8,128)S(1)}) custom-call(s32[640]{0:T(1024)S(1)} %copy-done.1, f32[1200,128]{1,0:T(8,128)S(1)} %bitcast.17, bf16[10,640,640]{2,1,0:T(8,128)(2,1)S(1)} %bitcast.16), custom_call_target="tpu_custom_call" | custom-call | flops 2000000000 | bytes 1000000 | tf_op jit(solution)/shard_map/first/pallas_call | solution.py:372
  12.4 0.0 collective-permute-done.1.refs_2_
  12.4 0.0 collective-permute-done.refs_1_
  12.4 0.0 collective-permute-done.2.refs_3_
  12.4 0.0 copy-done.2
  12.4 0.1 weight.1.weight_ref
  12.5 24.5 %all_to_all.30 = bf16[64,10,2,128]{3,2,1,0:T(2,128)(2,1)S(1)} all-to-all(bf16[64,10,2,128]{3,2,1,0:T(2,128)(2,1)S(1)} %bitcast.18), channel_id=1, replica_groups=mesh['z'=8,'y'=4,'c'=2,'x'=4] {'z','y','c'}, dimensions={0} | all-to-all | bytes 655360 | tf_op jit(solution)/shard_map/all_to_all | solution.py:328
  37.0 1.8 %grid.3 = bf16[1280,128]{1,0:T(8,128)(2,1)S(1)} custom-call(bf16[1280,128]{1,0:T(8,128)(2,1)S(1)} %bitcast.29, bf16[1280,1280]{1,0:T(8,128)(2,1)S(1)} %fourier.1.table_ref, f32[40,1280]{1,0:T(8,128)S(1)} %weight.1.weight_ref, f32[8,128]{1,0:T(8,128)S(1)} %get-tuple-element.32.norm_ref), custom_call_target="tpu_custom_call" | custom-call | flops 2000000000 | bytes 1000000 | tf_op jit(solution)/shard_map/grid/pallas_call | solution.py:395
  38.8 19.0 %all_to_all.31 = bf16[64,10,2,128]{3,2,1,0:T(2,128)(2,1)S(1)} all-to-all(bf16[64,10,2,128]{3,2,1,0:T(2,128)(2,1)S(1)} %bitcast.30), channel_id=1, replica_groups=mesh['z'=8,'y'=4,'c'=2,'x'=4] {'z','y','c'}, dimensions={0} | all-to-all | bytes 655360 | tf_op jit(solution)/shard_map/all_to_all | solution.py:328
  57.8 0.2 tail.3.refs_0_
  58.0 2.6 %collective-permute-start.5 = (f32[8,128]{1,0:T(8,128)S(1)}, f32[8,128]{1,0:T(8,128)S(1)}, u32[]{:S(2)}, u32[]{:S(2)}) collective-permute-start(f32[8,128]{1,0:T(8,128)S(1)} %tail.3.refs_0_), channel_id=1, source_target_pairs={{0,3},{1,0},{2,1},{3,2},{4,7},{5,4},{6,5},{7,6},{8,11},{9,8},{10,9... | collective-permute-start | bytes 12296 | tf_op jit(solution)/shard_map/ppermute | solution.py:404
  60.6 0.5 collective-permute-start.4
  61.1 0.6 collective-permute-start.3
  61.7 3.2 %back.3.refs_5_ = f32[10,24,640]{2,1,0:T(8,128)S(1)} custom-call(s32[640]{0:T(1024)S(1)} %copy-done.1, bf16[1280,128]{1,0:T(8,128)(2,1)S(1)} %bitcast.20, bf16[10,640,640]{2,1,0:T(8,128)(2,1)S(1)} %bitcast.16), custom_call_target="tpu_custom_call" | custom-call | flops 8000000000 | bytes 1000000 | tf_op jit(solution)/shard_map/back/pallas_call | solution.py:405
  64.9 0.0 collective-permute-done.5.refs_3_
  64.9 0.0 collective-permute-done.4.refs_2_
  64.9 0.0 collective-permute-done.3.refs_1_
  64.9 1.6 middle0.1
  66.5 20.8 %all_to_all.32 = bf16[64,10,2,128]{3,2,1,0:T(2,128)(2,1)S(1)} all-to-all(bf16[64,10,2,128]{3,2,1,0:T(2,128)(2,1)S(1)} %bitcast.26), channel_id=1, replica_groups=mesh['z'=8,'y'=4,'c'=2,'x'=4] {'z','y','c'}, dimensions={0} | all-to-all | bytes 655360 | tf_op jit(solution)/shard_map/all_to_all | solution.py:328
  87.3 1.8 %grid.4 = bf16[1280,128]{1,0:T(8,128)(2,1)S(1)} custom-call(bf16[1280,128]{1,0:T(8,128)(2,1)S(1)} %bitcast.31, bf16[1280,1280]{1,0:T(8,128)(2,1)S(1)} %fourier.1.table_ref, f32[40,1280]{1,0:T(8,128)S(1)} %weight.1.weight_ref, f32[8,128]{1,0:T(8,128)S(1)} %get-tuple-element.35.norm_ref), custom_call_target="tpu_custom_call" | custom-call | flops 2000000000 | bytes 1000000 | tf_op jit(solution)/shard_map/grid/pallas_call | solution.py:395
  89.1 19.0 %all_to_all.33 = bf16[64,10,2,128]{3,2,1,0:T(2,128)(2,1)S(1)} all-to-all(bf16[64,10,2,128]{3,2,1,0:T(2,128)(2,1)S(1)} %bitcast.32), channel_id=1, replica_groups=mesh['z'=8,'y'=4,'c'=2,'x'=4] {'z','y','c'}, dimensions={0} | all-to-all | bytes 655360 | tf_op jit(solution)/shard_map/all_to_all | solution.py:328
  108.2 0.2 tail.4.refs_0_
  108.3 1.4 collective-permute-start.8
  109.8 1.2 collective-permute-start.7
  111.0 0.0 collective-permute-start.6
  111.0 3.2 %back.4.refs_5_ = f32[10,24,640]{2,1,0:T(8,128)S(1)} custom-call(s32[640]{0:T(1024)S(1)} %copy-done.1, bf16[1280,128]{1,0:T(8,128)(2,1)S(1)} %bitcast.22, bf16[10,640,640]{2,1,0:T(8,128)(2,1)S(1)} %bitcast.16), custom_call_target="tpu_custom_call" | custom-call | flops 8000000000 | bytes 1000000 | tf_op jit(solution)/shard_map/back/pallas_call | solution.py:405
  114.2 0.0 collective-permute-done.8.refs_3_
  114.2 0.0 collective-permute-done.7.refs_2_
  114.2 0.7 collective-permute-done.6.refs_1_
  114.9 1.7 %middle1.1 = (f32[10,24,640]{2,1,0:T(8,128)S(1)}, f32[10,24,640]{2,1,0:T(8,128)S(1)}, bf16[1280,128]{1,0:T(8,128)(2,1)S(1)}, f32[8,128]{1,0:T(8,128)S(1)}, f32[8,128]{1,0:T(8,128)S(1)}) custom-call(f32[8,128]{1,0:T(8,128)S(1)} %tail.4.refs_0_, f32[8,128]{1,0:T(8,128)S(1)} %collective-permute-done.6.refs_1_, f32[8,128]{1,0:T(8,128)S(1)} %collective-permute-done.7.refs_2_, ...), custom_call_target="tpu_custom_call" | custom-call | flops 2000000000 | bytes 1000000 | tf_op jit(solution)/shard_map/middle1/pallas_call | solution.py:420
  116.6 20.5 %all_to_all.34 = bf16[64,10,2,128]{3,2,1,0:T(2,128)(2,1)S(1)} all-to-all(bf16[64,10,2,128]{3,2,1,0:T(2,128)(2,1)S(1)} %bitcast.25), channel_id=1, replica_groups=mesh['z'=8,'y'=4,'c'=2,'x'=4] {'z','y','c'}, dimensions={0} | all-to-all | bytes 655360 | tf_op jit(solution)/shard_map/all_to_all | solution.py:328
  137.1 1.8 %grid.5 = bf16[1280,128]{1,0:T(8,128)(2,1)S(1)} custom-call(bf16[1280,128]{1,0:T(8,128)(2,1)S(1)} %bitcast.27, bf16[1280,1280]{1,0:T(8,128)(2,1)S(1)} %fourier.1.table_ref, f32[40,1280]{1,0:T(8,128)S(1)} %weight.1.weight_ref, f32[8,128]{1,0:T(8,128)S(1)} %get-tuple-element.40.norm_ref), custom_call_target="tpu_custom_call" | custom-call | flops 2000000000 | bytes 1000000 | tf_op jit(solution)/shard_map/grid/pallas_call | solution.py:395
  139.0 19.0 %all_to_all.35 = bf16[64,10,2,128]{3,2,1,0:T(2,128)(2,1)S(1)} all-to-all(bf16[64,10,2,128]{3,2,1,0:T(2,128)(2,1)S(1)} %bitcast.28), channel_id=1, replica_groups=mesh['z'=8,'y'=4,'c'=2,'x'=4] {'z','y','c'}, dimensions={0} | all-to-all | bytes 655360 | tf_op jit(solution)/shard_map/all_to_all | solution.py:328
  158.0 0.2 tail.5.refs_0_
  158.2 1.7 %collective-permute-start.11 = (f32[8,128]{1,0:T(8,128)S(1)}, f32[8,128]{1,0:T(8,128)S(1)}, u32[]{:S(2)}, u32[]{:S(2)}) collective-permute-start(f32[8,128]{1,0:T(8,128)S(1)} %tail.5.refs_0_), channel_id=1, source_target_pairs={{0,3},{1,0},{2,1},{3,2},{4,7},{5,4},{6,5},{7,6},{8,11},{9,8},{10,9... | collective-permute-start | bytes 12296 | tf_op jit(solution)/shard_map/ppermute | solution.py:404
  159.8 0.5 collective-permute-start.10
  160.4 0.2 collective-permute-start.9
  160.5 3.2 %back.5.refs_4_ = f32[10,24,640]{2,1,0:T(8,128)S(1)} custom-call(s32[640]{0:T(1024)S(1)} %copy-done.1, bf16[1280,128]{1,0:T(8,128)(2,1)S(1)} %bitcast.24, bf16[10,640,640]{2,1,0:T(8,128)(2,1)S(1)} %bitcast.16), custom_call_target="tpu_custom_call" | custom-call | flops 8000000000 | bytes 1000000 | tf_op jit(solution)/shard_map/back/pallas_call | solution.py:405
  163.7 0.0 collective-permute-done.11.refs_3_
  163.7 0.1 collective-permute-done.10.refs_2_
  163.8 0.2 collective-permute-done.9.refs_1_
  164.0 2.0 %last.1 = (f32[1200,128]{1,0:T(8,128)}, f32[1200,128]{1,0:T(8,128)}) custom-call(f32[8,128]{1,0:T(8,128)S(1)} %tail.5.refs_0_, f32[8,128]{1,0:T(8,128)S(1)} %collective-permute-done.9.refs_1_, f32[8,128]{1,0:T(8,128)S(1)} %collective-permute-done.10.refs_2_, f32[8,128]{1,0:T(8,128)S(1)} %collective-permute-done.11.refs_3_, f32[10,24,640]{2,1,0:T(8,128)S(1)} %back.5.refs_4_, ...), custom_call_target="tpu_custom_call" | custom-call | flops 2000000000 | bytes 1000000 | tf_op jit(solution)/shard_map/last/pallas_call | solution.py:430
  (2 shorter events, 0.0 us)
Async XLA Ops:
  0.6 9.5 %copy-start.1 = (s32[640]{0:T(1024)S(1)}, s32[640]{0:T(1024)}, u32[]{:S(2)}) copy-start(s32[640]{0:T(1024)} %waves_ref.7) | copy-start | bytes 7684
  0.6 9.5 %copy-start = (f32[10,2,1,12,640]{4,2,3,1,0:T(1,128)S(1)}, f32[10,2,1,12,640]{4,2,3,1,0:T(1,128)}, u32[]{:S(2)}) copy-start(f32[10,2,1,12,640]{4,2,3,1,0:T(1,128)} %param.4) | copy-start | bytes 1843204
  0.6 11.7 %collective-permute-start.1 = (f32[10,1280]{1,0:T(8,128)}, f32[10,1280]{1,0:T(8,128)S(1)}, u32[]{:S(2)}, u32[]{:S(2)}) collective-permute-start(f32[10,1280]{1,0:T(8,128)} %refs_0_.1), channel_id=1, source_target_pairs={{0,8},{4,12},{8,0},{12,4},{16,24},{20,28},{24,16},{28,20},{1,9},{5... | collective-permute-start | bytes 153608 | tf_op jit(solution)/shard_map/ppermute | solution.py:383
  2.9 9.6 %collective-permute-start = (f32[10,1280]{1,0:T(8,128)}, f32[10,1280]{1,0:T(8,128)S(1)}, u32[]{:S(2)}, u32[]{:S(2)}) collective-permute-start(f32[10,1280]{1,0:T(8,128)} %refs_0_.1), channel_id=1, source_target_pairs={{0,4},{4,0},{8,12},{12,8},{16,20},{20,16},{24,28},{28,24},{1,5},{5... | collective-permute-start | bytes 153608 | tf_op jit(solution)/shard_map/ppermute | solution.py:383
  4.0 8.4 %collective-permute-start.2 = (f32[10,1280]{1,0:T(8,128)}, f32[10,1280]{1,0:T(8,128)S(1)}, u32[]{:S(2)}, u32[]{:S(2)}) collective-permute-start(f32[10,1280]{1,0:T(8,128)} %refs_0_.1), channel_id=1, source_target_pairs={{0,12},{4,8},{8,4},{12,0},{16,28},{20,24},{24,20},{28,16},{1,13},{... | collective-permute-start | bytes 153608 | tf_op jit(solution)/shard_map/ppermute | solution.py:383
  6.6 3.6 %slice-start = ((s8[8192000]{0:T(1024)(128)(4,1)}), s8[4194304]{0:T(1024)(128)(4,1)S(1)}, s32[]{:S(2)}) async-start(s8[8192000]{0:T(1024)(128)(4,1)} %bitcast.15), calls=%async_computation.6 | async-start | bytes 8388608
  6.8 3.4 %slice-start.1 = ((s8[8192000]{0:T(1024)(128)(4,1)}), s8[3997696]{0:T(1024)(128)(4,1)S(1)}, s32[]{:S(2)}) async-start(s8[8192000]{0:T(1024)(128)(4,1)} %bitcast.15), calls=%async_computation.7 | async-start | bytes 7995392
  6.8 5.6 %copy-start.2 = (f32[10,1280]{1,0:T(8,128)S(1)}, f32[10,1280]{1,0:T(8,128)}, u32[]{:S(2)}) copy-start(f32[10,1280]{1,0:T(8,128)} %refs_0_.1) | copy-start | bytes 153604
  58.0 6.9 %collective-permute-start.5 = (f32[8,128]{1,0:T(8,128)S(1)}, f32[8,128]{1,0:T(8,128)S(1)}, u32[]{:S(2)}, u32[]{:S(2)}) collective-permute-start(f32[8,128]{1,0:T(8,128)S(1)} %tail.3.refs_0_), channel_id=1, source_target_pairs={{0,3},{1,0},{2,1},{3,2},{4,7},{5,4},{6,5},{7,6},{8,11},{9,8},{10,9... | collective-permute-start | bytes 12296 | tf_op jit(solution)/shard_map/ppermute | solution.py:404
  60.6 4.3 %collective-permute-start.4 = (f32[8,128]{1,0:T(8,128)S(1)}, f32[8,128]{1,0:T(8,128)S(1)}, u32[]{:S(2)}, u32[]{:S(2)}) collective-permute-start(f32[8,128]{1,0:T(8,128)S(1)} %tail.3.refs_0_), channel_id=1, source_target_pairs={{0,2},{1,3},{2,0},{3,1},{4,6},{5,7},{6,4},{7,5},{8,10},{9,11},{10,... | collective-permute-start | bytes 12296 | tf_op jit(solution)/shard_map/ppermute | solution.py:404
  61.1 3.8 %collective-permute-start.3 = (f32[8,128]{1,0:T(8,128)S(1)}, f32[8,128]{1,0:T(8,128)S(1)}, u32[]{:S(2)}, u32[]{:S(2)}) collective-permute-start(f32[8,128]{1,0:T(8,128)S(1)} %tail.3.refs_0_), channel_id=1, source_target_pairs={{0,1},{1,2},{2,3},{3,0},{4,5},{5,6},{6,7},{7,4},{8,9},{9,10},{10,1... | collective-permute-start | bytes 12296 | tf_op jit(solution)/shard_map/ppermute | solution.py:404
  108.3 5.9 %collective-permute-start.8 = (f32[8,128]{1,0:T(8,128)S(1)}, f32[8,128]{1,0:T(8,128)S(1)}, u32[]{:S(2)}, u32[]{:S(2)}) collective-permute-start(f32[8,128]{1,0:T(8,128)S(1)} %tail.4.refs_0_), channel_id=1, source_target_pairs={{0,3},{1,0},{2,1},{3,2},{4,7},{5,4},{6,5},{7,6},{8,11},{9,8},{10,9... | collective-permute-start | bytes 12296 | tf_op jit(solution)/shard_map/ppermute | solution.py:404
  109.8 4.5 %collective-permute-start.7 = (f32[8,128]{1,0:T(8,128)S(1)}, f32[8,128]{1,0:T(8,128)S(1)}, u32[]{:S(2)}, u32[]{:S(2)}) collective-permute-start(f32[8,128]{1,0:T(8,128)S(1)} %tail.4.refs_0_), channel_id=1, source_target_pairs={{0,2},{1,3},{2,0},{3,1},{4,6},{5,7},{6,4},{7,5},{8,10},{9,11},{10,... | collective-permute-start | bytes 12296 | tf_op jit(solution)/shard_map/ppermute | solution.py:404
  111.0 3.9 %collective-permute-start.6 = (f32[8,128]{1,0:T(8,128)S(1)}, f32[8,128]{1,0:T(8,128)S(1)}, u32[]{:S(2)}, u32[]{:S(2)}) collective-permute-start(f32[8,128]{1,0:T(8,128)S(1)} %tail.4.refs_0_), channel_id=1, source_target_pairs={{0,1},{1,2},{2,3},{3,0},{4,5},{5,6},{6,7},{7,4},{8,9},{9,10},{10,1... | collective-permute-start | bytes 12296 | tf_op jit(solution)/shard_map/ppermute | solution.py:404
  158.2 5.6 %collective-permute-start.11 = (f32[8,128]{1,0:T(8,128)S(1)}, f32[8,128]{1,0:T(8,128)S(1)}, u32[]{:S(2)}, u32[]{:S(2)}) collective-permute-start(f32[8,128]{1,0:T(8,128)S(1)} %tail.5.refs_0_), channel_id=1, source_target_pairs={{0,3},{1,0},{2,1},{3,2},{4,7},{5,4},{6,5},{7,6},{8,11},{9,8},{10,9... | collective-permute-start | bytes 12296 | tf_op jit(solution)/shard_map/ppermute | solution.py:404
  159.8 4.0 %collective-permute-start.10 = (f32[8,128]{1,0:T(8,128)S(1)}, f32[8,128]{1,0:T(8,128)S(1)}, u32[]{:S(2)}, u32[]{:S(2)}) collective-permute-start(f32[8,128]{1,0:T(8,128)S(1)} %tail.5.refs_0_), channel_id=1, source_target_pairs={{0,2},{1,3},{2,0},{3,1},{4,6},{5,7},{6,4},{7,5},{8,10},{9,11},{10,... | collective-permute-start | bytes 12296 | tf_op jit(solution)/shard_map/ppermute | solution.py:404
  160.4 3.7 %collective-permute-start.9 = (f32[8,128]{1,0:T(8,128)S(1)}, f32[8,128]{1,0:T(8,128)S(1)}, u32[]{:S(2)}, u32[]{:S(2)}) collective-permute-start(f32[8,128]{1,0:T(8,128)S(1)} %tail.5.refs_0_), channel_id=1, source_target_pairs={{0,1},{1,2},{2,3},{3,0},{4,5},{5,6},{6,7},{7,4},{8,9},{9,10},{10,1... | collective-permute-start | bytes 12296 | tf_op jit(solution)/shard_map/ppermute | solution.py:404

commit v5 on v4

--- a/solution.py
+++ b/solution.py
@@ -194,7 +194,7 @@
 
 def last_kernel(slots, chunk_rows, *refs):
     sum_a, sum_b, sum_c, sum_d, adj_ref, res0_ref, res1_ref, res2_ref, last_ref, past_ref, *refs = refs
-    sol_ref, fin_ref, turn_ref = refs
+    sol_hbm, fin_hbm, turn_ref, sol_ref, fin_ref, sol_sems, fin_sems = refs
     norm, product = sums_of((sum_a, sum_b, sum_c, sum_d), chunk_rows)
     beta = norm / past_ref[0:1, 0:1]
     alpha = scalar_row(norm / (product - beta * norm / past_ref[1:2, 0:1]))
@@ -203,7 +203,17 @@
     tiles = adj_ref.shape[2] // LANES
     height = GROUPS * SUB
 
-    def step(slot, carry):
+    rows_each = sol_hbm.shape[0] // slots
+    copies = []
+
+    def send(slot):
+        rows = pl.ds(slot * rows_each, rows_each)
+        copies.append(pltpu.make_async_copy(sol_ref.at[rows], sol_hbm.at[rows], sol_sems.at[slot]))
+        copies.append(pltpu.make_async_copy(fin_ref.at[rows], fin_hbm.at[rows], fin_sems.at[slot]))
+        copies[-2].start()
+        copies[-1].start()
+
+    for slot in range(slots):
         for tile in range(tiles):
             cols = slice(tile * LANES, (tile + 1) * LANES)
             res2 = res2_ref[slot, :, cols]
@@ -221,9 +231,11 @@
                     at = group * SUB + part
                     fin_ref[rows, :] = turn_ref[pl.ds((2 * tile) * height + at, SHARES, stride=2), :]
                     sol_ref[rows, :] = turn_ref[pl.ds((2 * tile + 1) * height + at, SHARES, stride=2), :]
-        return carry
-
-    lax.fori_loop(0, slots, step, 0)
+        if slot > 0:
+            send(slot - 1)
+    send(slots - 1)
+    for copy in copies:
+        copy.wait()
 
 
 def fourier_kernel(chunk_rows, slots, norm_factor, waves_ref, out_ref):
@@ -285,7 +297,7 @@
 def grid_kernel(x_ref, table_ref, weight_ref, norm_ref, out_ref, turned_ref, wide_ref):
     count, lons = table_ref.shape
     step = 256
-    turned_ref[...] = x_ref[...].astype(F32).T.astype(BF16)
+    turned_ref[...] = x_ref[...].T
     energy = jnp.zeros((SUB, step), F32)
     for first in range(0, lons, step):
         cols = slice(first, first + step)
@@ -300,7 +312,7 @@
             for block in range(0, PIECE, SUB):
                 energy = energy + square[block : block + SUB]
         weighted.append(jnp.zeros((LANES - SPARE, step), F32))
-        wide_ref[cols, :] = jnp.concatenate(weighted, axis=0).T.astype(BF16)
+        wide_ref[:, cols] = jnp.concatenate(weighted, axis=0).astype(BF16)
     lane = lane_of(1)
     spare = jnp.zeros((1, LANES), F32)
     values = pieces_of(jnp.sum(norm_ref[...], axis=(0, 1), keepdims=True))
@@ -309,7 +321,9 @@
         spare = jnp.where(lane == SPARE + place, value, spare)
     for first in range(0, count, step):
         rows = slice(first, first + step)
-        back = jnp.dot(table_ref[rows, :], wide_ref[...], preferred_element_type=F32)
+        back = lax.dot_general(
+            table_ref[rows, :], wide_ref[...], (((1,), (1,)), ((), ())), preferred_element_type=F32
+        )
         out_ref[rows, :] = jnp.where(lane >= SPARE, spare, back).astype(BF16)
 
 
@@ -328,11 +342,11 @@
     return lax.all_to_all(packed, BAND, 0, 0, tiled=True).reshape(rows, LANES)
 
 
-def call(kernel, name, outs, ins, scratch=(), vmem=24, flops=2_000_000_000):
+def call(kernel, name, outs, ins, scratch=(), vmem=24, flops=2_000_000_000, place=pltpu.VMEM):
     return pl.pallas_call(
         kernel,
         in_specs=ins,
-        out_specs=[pl.BlockSpec(memory_space=pltpu.VMEM)] * len(outs),
+        out_specs=[pl.BlockSpec(memory_space=place)] * len(outs),
         out_shape=outs,
         scratch_shapes=scratch,
         compiler_params=pltpu.CompilerParams(vmem_limit_bytes=vmem * 1024 * 1024),
@@ -397,7 +411,7 @@
             "grid",
             [payload_shape],
             [vmem] * 4,
-            [pltpu.VMEM((LANES, rows), BF16), pltpu.VMEM((lon_count, LANES), BF16)],
+            [pltpu.VMEM((LANES, rows), BF16), pltpu.VMEM((LANES, lon_count), BF16)],
         )(arrived, table, weight, norm)
         home = exchange(back, bands)
         (sums,) = call(tail_kernel, "tail", [small_shape], [vmem])(home)
@@ -432,7 +446,14 @@
         "last",
         [flat_shape, flat_shape],
         [vmem] * 10,
-        [pltpu.VMEM((2 * GROUPS * SUB * (degrees // LANES), LANES), F32)],
+        [
+            pltpu.VMEM((2 * GROUPS * SUB * (degrees // LANES), LANES), F32),
+            pltpu.VMEM(flat.shape, F32),
+            pltpu.VMEM(flat.shape, F32),
+            pltpu.SemaphoreType.DMA((slots,)),
+            pltpu.SemaphoreType.DMA((slots,)),
+        ],
+        place=pltpu.HBM,
     )(*sums, adjoint, *residuals, along, past)
     return solution.reshape(right_side.shape), residual.reshape(right_side.shape)
 

time: 166 us -> 165 us (level)
  transfers between devices with their start and end apart: 12 -> 12, of which waited for: 3 -> 2; matrix products, arithmetic and copies ran while one was open for 1% -> 1% of each run, Pallas kernels for 9% -> 9%
where the time goes in v5:
time: 165 us
  blocking collectives  123 us (75%)
  Pallas kernels  25.2 us (15%)
  starting transfers between devices  13.7 us (8%)
    all_to_all x6, blocking collectives, exchange(): return lax.all_to_all(packed, BAND, 0, 0, tiled=True).reshape(rows, LANES)  123 us
    pallas_call x3, Pallas kernels, reach(): call(functools.partial(back_kernel, slots, chunk_rows), 'back', [vec_shap...  9.53 us
    ppermute x9, starting transfers between devices, reach(): lax.ppermute(sums, 'x', [(i, (i + k) % XS) for i in range(XS)])  8.73 us
    ppermute x3, starting transfers between devices, on_device(): near.append(lax.ppermute(obs_weight, ('y', 'c'), pairs))  4.92 us
    pallas_call x3, Pallas kernels, reach(): call(grid_kernel, 'grid', [payload_shape], [vmem] * 4, [pltpu.VMEM((LANES...  4.78 us
    pallas_call x1, Pallas kernels, on_device(): call(functools.partial(fourier_kernel, chunk_rows, slots, 1.0 / math.sqrt...  3.33 us
    pallas_call x2, Pallas kernels, on_device(): call(functools.partial(middle_kernel, stage, slots, chunk_rows), f'middle...  3.32 us
  transfers between devices with their start and end apart: 12, of which 2 were waited for; matrix products, arithmetic and copies ran while one was open for 1% of the time, Pallas kernels for 9%

profile of v5, /device:TPU:1, one launch (start us, length us, event | category | flops | bytes accessed | tf_op | source)
XLA Modules:
  0.0 164.6 jit_solution(3108683992704053511)
XLA Ops:
  0.6 0.0 copy-start.1
  0.6 0.0 copy-start
  0.6 2.2 %collective-permute-start.1 = (f32[10,1280]{1,0:T(8,128)}, f32[10,1280]{1,0:T(8,128)S(1)}, u32[]{:S(2)}, u32[]{:S(2)}) collective-permute-start(f32[10,1280]{1,0:T(8,128)} %refs_0_.1), channel_id=1, source_target_pairs={{0,8},{4,12},{8,0},{12,4},{16,24},{20,28},{24,16},{28,20},{1,9},{5... | collective-permute-start | bytes 153608 | tf_op jit(solution)/shard_map/ppermute | solution.py:397
  2.9 1.2 collective-permute-start
  4.0 1.5 collective-permute-start.2
  5.6 0.8 broadcast_in_dim.14
  6.4 0.1 broadcast_in_dim.16
  6.6 0.0 slice-start
  6.6 0.2 broadcast_in_dim.17.waves_ref
  6.8 0.0 slice-start.1
  6.8 0.0 copy-start.2
  6.8 3.3 %fourier.1.table_ref = bf16[1280,1280]{1,0:T(8,128)(2,1)S(1)} custom-call(s32[1280,128]{1,0:T(8,128)S(1)} %broadcast_in_dim.17.waves_ref), custom_call_target="tpu_custom_call" | custom-call | flops 4000000000 | bytes 1000000 | tf_op jit(solution)/shard_map/fourier/pallas_call | solution.py:377
  10.2 0.0 copy-done.1
  10.2 0.0 copy-done
  10.2 0.0 slice-done
  10.2 0.0 slice-done.1
  10.2 2.2 %first.1 = (f32[10,24,640]{2,1,0:T(8,128)S(1)}, bf16[1280,128]{1,0:T(8,128)(2,1)S(1)}, f32[8,128]{1,0:T(8,128)S(1)}) custom-call(s32[640]{0:T(1024)S(1)} %copy-done.1, f32[1200,128]{1,0:T(8,128)S(1)} %bitcast.17, bf16[10,640,640]{2,1,0:T(8,128)(2,1)S(1)} %bitcast.16), custom_call_target="tpu_custom_call" | custom-call | flops 2000000000 | bytes 1000000 | tf_op jit(solution)/shard_map/first/pallas_call | solution.py:386
  12.4 0.0 collective-permute-done.1.refs_2_
  12.4 0.0 collective-permute-done.refs_1_
  12.4 0.0 collective-permute-done.2.refs_3_
  12.4 0.0 copy-done.2
  12.4 0.1 weight.1.weight_ref
  12.5 24.5 %all_to_all.30 = bf16[64,10,2,128]{3,2,1,0:T(2,128)(2,1)S(1)} all-to-all(bf16[64,10,2,128]{3,2,1,0:T(2,128)(2,1)S(1)} %bitcast.18), channel_id=1, replica_groups=mesh['z'=8,'y'=4,'c'=2,'x'=4] {'z','y','c'}, dimensions={0} | all-to-all | bytes 655360 | tf_op jit(solution)/shard_map/all_to_all | solution.py:342
  37.0 1.6 grid.3
  38.6 19.0 %all_to_all.31 = bf16[64,10,2,128]{3,2,1,0:T(2,128)(2,1)S(1)} all-to-all(bf16[64,10,2,128]{3,2,1,0:T(2,128)(2,1)S(1)} %bitcast.30), channel_id=1, replica_groups=mesh['z'=8,'y'=4,'c'=2,'x'=4] {'z','y','c'}, dimensions={0} | all-to-all | bytes 655360 | tf_op jit(solution)/shard_map/all_to_all | solution.py:342
  57.6 0.2 tail.3.refs_0_
  57.8 2.6 %collective-permute-start.5 = (f32[8,128]{1,0:T(8,128)S(1)}, f32[8,128]{1,0:T(8,128)S(1)}, u32[]{:S(2)}, u32[]{:S(2)}) collective-permute-start(f32[8,128]{1,0:T(8,128)S(1)} %tail.3.refs_0_), channel_id=1, source_target_pairs={{0,3},{1,0},{2,1},{3,2},{4,7},{5,4},{6,5},{7,6},{8,11},{9,8},{10,9... | collective-permute-start | bytes 12296 | tf_op jit(solution)/shard_map/ppermute | solution.py:418
  60.3 0.5 collective-permute-start.4
  60.8 0.6 collective-permute-start.3
  61.5 3.2 %back.3.refs_5_ = f32[10,24,640]{2,1,0:T(8,128)S(1)} custom-call(s32[640]{0:T(1024)S(1)} %copy-done.1, bf16[1280,128]{1,0:T(8,128)(2,1)S(1)} %bitcast.20, bf16[10,640,640]{2,1,0:T(8,128)(2,1)S(1)} %bitcast.16), custom_call_target="tpu_custom_call" | custom-call | flops 8000000000 | bytes 1000000 | tf_op jit(solution)/shard_map/back/pallas_call | solution.py:419
  64.6 0.0 collective-permute-done.5.refs_3_
  64.7 0.0 collective-permute-done.4.refs_2_
  64.7 0.0 collective-permute-done.3.refs_1_
  64.7 1.6 middle0.1
  66.3 20.6 %all_to_all.32 = bf16[64,10,2,128]{3,2,1,0:T(2,128)(2,1)S(1)} all-to-all(bf16[64,10,2,128]{3,2,1,0:T(2,128)(2,1)S(1)} %bitcast.26), channel_id=1, replica_groups=mesh['z'=8,'y'=4,'c'=2,'x'=4] {'z','y','c'}, dimensions={0} | all-to-all | bytes 655360 | tf_op jit(solution)/shard_map/all_to_all | solution.py:342
  86.9 1.6 grid.4
  88.5 19.0 %all_to_all.33 = bf16[64,10,2,128]{3,2,1,0:T(2,128)(2,1)S(1)} all-to-all(bf16[64,10,2,128]{3,2,1,0:T(2,128)(2,1)S(1)} %bitcast.32), channel_id=1, replica_groups=mesh['z'=8,'y'=4,'c'=2,'x'=4] {'z','y','c'}, dimensions={0} | all-to-all | bytes 655360 | tf_op jit(solution)/shard_map/all_to_all | solution.py:342
  107.5 0.2 tail.4.refs_0_
  107.7 1.5 collective-permute-start.8
  109.1 1.2 collective-permute-start.7
  110.4 0.0 collective-permute-start.6
  110.4 3.2 %back.4.refs_5_ = f32[10,24,640]{2,1,0:T(8,128)S(1)} custom-call(s32[640]{0:T(1024)S(1)} %copy-done.1, bf16[1280,128]{1,0:T(8,128)(2,1)S(1)} %bitcast.22, bf16[10,640,640]{2,1,0:T(8,128)(2,1)S(1)} %bitcast.16), custom_call_target="tpu_custom_call" | custom-call | flops 8000000000 | bytes 1000000 | tf_op jit(solution)/shard_map/back/pallas_call | solution.py:419
  113.6 0.0 collective-permute-done.8.refs_3_
  113.6 0.0 collective-permute-done.7.refs_2_
  113.6 0.7 collective-permute-done.6.refs_1_
  114.3 1.7 %middle1.1 = (f32[10,24,640]{2,1,0:T(8,128)S(1)}, f32[10,24,640]{2,1,0:T(8,128)S(1)}, bf16[1280,128]{1,0:T(8,128)(2,1)S(1)}, f32[8,128]{1,0:T(8,128)S(1)}, f32[8,128]{1,0:T(8,128)S(1)}) custom-call(f32[8,128]{1,0:T(8,128)S(1)} %tail.4.refs_0_, f32[8,128]{1,0:T(8,128)S(1)} %collective-permute-done.6.refs_1_, f32[8,128]{1,0:T(8,128)S(1)} %collective-permute-done.7.refs_2_, ...), custom_call_target="tpu_custom_call" | custom-call | flops 2000000000 | bytes 1000000 | tf_op jit(solution)/shard_map/middle1/pallas_call | solution.py:434
  116.0 20.5 %all_to_all.34 = bf16[64,10,2,128]{3,2,1,0:T(2,128)(2,1)S(1)} all-to-all(bf16[64,10,2,128]{3,2,1,0:T(2,128)(2,1)S(1)} %bitcast.25), channel_id=1, replica_groups=mesh['z'=8,'y'=4,'c'=2,'x'=4] {'z','y','c'}, dimensions={0} | all-to-all | bytes 655360 | tf_op jit(solution)/shard_map/all_to_all | solution.py:342
  136.5 1.6 grid.5
  138.1 19.0 %all_to_all.35 = bf16[64,10,2,128]{3,2,1,0:T(2,128)(2,1)S(1)} all-to-all(bf16[64,10,2,128]{3,2,1,0:T(2,128)(2,1)S(1)} %bitcast.28), channel_id=1, replica_groups=mesh['z'=8,'y'=4,'c'=2,'x'=4] {'z','y','c'}, dimensions={0} | all-to-all | bytes 655360 | tf_op jit(solution)/shard_map/all_to_all | solution.py:342
  157.1 0.2 tail.5.refs_0_
  157.3 1.5 collective-permute-start.11
  158.8 0.5 collective-permute-start.10
  159.3 0.4 collective-permute-start.9
  159.7 3.2 %back.5.refs_4_ = f32[10,24,640]{2,1,0:T(8,128)S(1)} custom-call(s32[640]{0:T(1024)S(1)} %copy-done.1, bf16[1280,128]{1,0:T(8,128)(2,1)S(1)} %bitcast.24, bf16[10,640,640]{2,1,0:T(8,128)(2,1)S(1)} %bitcast.16), custom_call_target="tpu_custom_call" | custom-call | flops 8000000000 | bytes 1000000 | tf_op jit(solution)/shard_map/back/pallas_call | solution.py:419
  162.8 0.0 collective-permute-done.11.refs_3_
  162.9 0.0 collective-permute-done.10.refs_2_
  162.9 0.1 collective-permute-done.9.refs_1_
  162.9 1.5 last.1
  (2 shorter events, 0.0 us)
Async XLA Ops:
  0.6 9.5 %copy-start.1 = (s32[640]{0:T(1024)S(1)}, s32[640]{0:T(1024)}, u32[]{:S(2)}) copy-start(s32[640]{0:T(1024)} %waves_ref.7) | copy-start | bytes 7684
  0.6 9.5 %copy-start = (f32[10,2,1,12,640]{4,2,3,1,0:T(1,128)S(1)}, f32[10,2,1,12,640]{4,2,3,1,0:T(1,128)}, u32[]{:S(2)}) copy-start(f32[10,2,1,12,640]{4,2,3,1,0:T(1,128)} %param.4) | copy-start | bytes 1843204
  0.6 11.7 %collective-permute-start.1 = (f32[10,1280]{1,0:T(8,128)}, f32[10,1280]{1,0:T(8,128)S(1)}, u32[]{:S(2)}, u32[]{:S(2)}) collective-permute-start(f32[10,1280]{1,0:T(8,128)} %refs_0_.1), channel_id=1, source_target_pairs={{0,8},{4,12},{8,0},{12,4},{16,24},{20,28},{24,16},{28,20},{1,9},{5... | collective-permute-start | bytes 153608 | tf_op jit(solution)/shard_map/ppermute | solution.py:397
  2.9 9.6 %collective-permute-start = (f32[10,1280]{1,0:T(8,128)}, f32[10,1280]{1,0:T(8,128)S(1)}, u32[]{:S(2)}, u32[]{:S(2)}) collective-permute-start(f32[10,1280]{1,0:T(8,128)} %refs_0_.1), channel_id=1, source_target_pairs={{0,4},{4,0},{8,12},{12,8},{16,20},{20,16},{24,28},{28,24},{1,5},{5... | collective-permute-start | bytes 153608 | tf_op jit(solution)/shard_map/ppermute | solution.py:397
  4.0 8.4 %collective-permute-start.2 = (f32[10,1280]{1,0:T(8,128)}, f32[10,1280]{1,0:T(8,128)S(1)}, u32[]{:S(2)}, u32[]{:S(2)}) collective-permute-start(f32[10,1280]{1,0:T(8,128)} %refs_0_.1), channel_id=1, source_target_pairs={{0,12},{4,8},{8,4},{12,0},{16,28},{20,24},{24,20},{28,16},{1,13},{... | collective-permute-start | bytes 153608 | tf_op jit(solution)/shard_map/ppermute | solution.py:397
  6.6 3.6 %slice-start = ((s8[8192000]{0:T(1024)(128)(4,1)}), s8[4194304]{0:T(1024)(128)(4,1)S(1)}, s32[]{:S(2)}) async-start(s8[8192000]{0:T(1024)(128)(4,1)} %bitcast.15), calls=%async_computation.6 | async-start | bytes 8388608
  6.8 3.4 %slice-start.1 = ((s8[8192000]{0:T(1024)(128)(4,1)}), s8[3997696]{0:T(1024)(128)(4,1)S(1)}, s32[]{:S(2)}) async-start(s8[8192000]{0:T(1024)(128)(4,1)} %bitcast.15), calls=%async_computation.7 | async-start | bytes 7995392
  6.8 5.6 %copy-start.2 = (f32[10,1280]{1,0:T(8,128)S(1)}, f32[10,1280]{1,0:T(8,128)}, u32[]{:S(2)}) copy-start(f32[10,1280]{1,0:T(8,128)} %refs_0_.1) | copy-start | bytes 153604
  57.8 6.9 %collective-permute-start.5 = (f32[8,128]{1,0:T(8,128)S(1)}, f32[8,128]{1,0:T(8,128)S(1)}, u32[]{:S(2)}, u32[]{:S(2)}) collective-permute-start(f32[8,128]{1,0:T(8,128)S(1)} %tail.3.refs_0_), channel_id=1, source_target_pairs={{0,3},{1,0},{2,1},{3,2},{4,7},{5,4},{6,5},{7,6},{8,11},{9,8},{10,9... | collective-permute-start | bytes 12296 | tf_op jit(solution)/shard_map/ppermute | solution.py:418
  60.3 4.3 %collective-permute-start.4 = (f32[8,128]{1,0:T(8,128)S(1)}, f32[8,128]{1,0:T(8,128)S(1)}, u32[]{:S(2)}, u32[]{:S(2)}) collective-permute-start(f32[8,128]{1,0:T(8,128)S(1)} %tail.3.refs_0_), channel_id=1, source_target_pairs={{0,2},{1,3},{2,0},{3,1},{4,6},{5,7},{6,4},{7,5},{8,10},{9,11},{10,... | collective-permute-start | bytes 12296 | tf_op jit(solution)/shard_map/ppermute | solution.py:418
  60.8 3.8 %collective-permute-start.3 = (f32[8,128]{1,0:T(8,128)S(1)}, f32[8,128]{1,0:T(8,128)S(1)}, u32[]{:S(2)}, u32[]{:S(2)}) collective-permute-start(f32[8,128]{1,0:T(8,128)S(1)} %tail.3.refs_0_), channel_id=1, source_target_pairs={{0,1},{1,2},{2,3},{3,0},{4,5},{5,6},{6,7},{7,4},{8,9},{9,10},{10,1... | collective-permute-start | bytes 12296 | tf_op jit(solution)/shard_map/ppermute | solution.py:418
  107.7 5.9 %collective-permute-start.8 = (f32[8,128]{1,0:T(8,128)S(1)}, f32[8,128]{1,0:T(8,128)S(1)}, u32[]{:S(2)}, u32[]{:S(2)}) collective-permute-start(f32[8,128]{1,0:T(8,128)S(1)} %tail.4.refs_0_), channel_id=1, source_target_pairs={{0,3},{1,0},{2,1},{3,2},{4,7},{5,4},{6,5},{7,6},{8,11},{9,8},{10,9... | collective-permute-start | bytes 12296 | tf_op jit(solution)/shard_map/ppermute | solution.py:418
  109.1 4.5 %collective-permute-start.7 = (f32[8,128]{1,0:T(8,128)S(1)}, f32[8,128]{1,0:T(8,128)S(1)}, u32[]{:S(2)}, u32[]{:S(2)}) collective-permute-start(f32[8,128]{1,0:T(8,128)S(1)} %tail.4.refs_0_), channel_id=1, source_target_pairs={{0,2},{1,3},{2,0},{3,1},{4,6},{5,7},{6,4},{7,5},{8,10},{9,11},{10,... | collective-permute-start | bytes 12296 | tf_op jit(solution)/shard_map/ppermute | solution.py:418
  110.4 3.9 %collective-permute-start.6 = (f32[8,128]{1,0:T(8,128)S(1)}, f32[8,128]{1,0:T(8,128)S(1)}, u32[]{:S(2)}, u32[]{:S(2)}) collective-permute-start(f32[8,128]{1,0:T(8,128)S(1)} %tail.4.refs_0_), channel_id=1, source_target_pairs={{0,1},{1,2},{2,3},{3,0},{4,5},{5,6},{6,7},{7,4},{8,9},{9,10},{10,1... | collective-permute-start | bytes 12296 | tf_op jit(solution)/shard_map/ppermute | solution.py:418
  157.3 5.6 %collective-permute-start.11 = (f32[8,128]{1,0:T(8,128)S(1)}, f32[8,128]{1,0:T(8,128)S(1)}, u32[]{:S(2)}, u32[]{:S(2)}) collective-permute-start(f32[8,128]{1,0:T(8,128)S(1)} %tail.5.refs_0_), channel_id=1, source_target_pairs={{0,3},{1,0},{2,1},{3,2},{4,7},{5,4},{6,5},{7,6},{8,11},{9,8},{10,9... | collective-permute-start | bytes 12296 | tf_op jit(solution)/shard_map/ppermute | solution.py:418
  158.8 4.1 %collective-permute-start.10 = (f32[8,128]{1,0:T(8,128)S(1)}, f32[8,128]{1,0:T(8,128)S(1)}, u32[]{:S(2)}, u32[]{:S(2)}) collective-permute-start(f32[8,128]{1,0:T(8,128)S(1)} %tail.5.refs_0_), channel_id=1, source_target_pairs={{0,2},{1,3},{2,0},{3,1},{4,6},{5,7},{6,4},{7,5},{8,10},{9,11},{10,... | collective-permute-start | bytes 12296 | tf_op jit(solution)/shard_map/ppermute | solution.py:418
  159.3 3.7 %collective-permute-start.9 = (f32[8,128]{1,0:T(8,128)S(1)}, f32[8,128]{1,0:T(8,128)S(1)}, u32[]{:S(2)}, u32[]{:S(2)}) collective-permute-start(f32[8,128]{1,0:T(8,128)S(1)} %tail.5.refs_0_), channel_id=1, source_target_pairs={{0,1},{1,2},{2,3},{3,0},{4,5},{5,6},{6,7},{7,4},{8,9},{9,10},{10,1... | collective-permute-start | bytes 12296 | tf_op jit(solution)/shard_map/ppermute | solution.py:418

commit v6 on v5

--- a/solution.py
+++ b/solution.py
@@ -238,15 +238,27 @@
         copy.wait()
 
 
-def fourier_kernel(chunk_rows, slots, norm_factor, waves_ref, out_ref):
+def fourier_kernel(chunk_rows, slots, norm_factor, map_ref, out_ref, column_ref, waves_ref):
     rows = 32
     lon_count = out_ref.shape[1]
+    blocks = map_ref.shape[0]
+    compact = jnp.concatenate([map_ref[...].astype(F32), jnp.zeros((SUB - blocks, LANES), F32)], axis=0)
+    columns = jnp.concatenate([compact, jnp.zeros((LANES - SUB, LANES), F32)], axis=0).T
+    for block in range(blocks):
+        column_ref[block * LANES : (block + 1) * LANES, :] = jnp.broadcast_to(
+            columns[:, block : block + 1], (LANES, LANES)
+        )
+    for band in range(waves_ref.shape[0] // chunk_rows):
+        wave = column_ref[band * slots : (band + 1) * slots, :]
+        for part in range(2):
+            at = band * chunk_rows + part * slots
+            waves_ref[at : at + slots, :] = wave
     lane = lax.broadcasted_iota(jnp.int32, (rows, LANES), 1).astype(F32)
     local = lax.broadcasted_iota(jnp.int32, (rows, LANES), 0)
 
     def step(index, carry):
         at = pl.multiple_of(index * rows, rows)
-        wave = waves_ref[pl.ds(at, rows), :].astype(F32)
+        wave = waves_ref[pl.ds(at, rows), :]
         row = (local + at).astype(F32)
         within = row - chunk_rows * jnp.floor((row + 0.5) * (1.0 / chunk_rows))
         quarter = jnp.where(within > slots - 0.5, 0.25 * lon_count, 0.0)
@@ -364,10 +376,6 @@
     smem = pl.BlockSpec(memory_space=pltpu.SMEM)
     vmem = pl.BlockSpec(memory_space=pltpu.VMEM)
     flat = right_side.reshape(-1, LANES)
-    spread = jnp.broadcast_to(wave_map.reshape(bands, 1, slots), (bands, 2, slots)).reshape(rows, 1)
-    spread = jnp.broadcast_to(spread, (rows, LANES))
-    flat, spread = lax.optimization_barrier((flat, spread))
-
     vec_shape = jax.ShapeDtypeStruct((slots, GROUPS * SUB, degrees), F32)
     payload_shape = jax.ShapeDtypeStruct((rows, LANES), BF16)
     small_shape = jax.ShapeDtypeStruct((SUB, LANES), F32)
@@ -379,8 +387,9 @@
         "fourier",
         [jax.ShapeDtypeStruct((rows, lon_count), BF16)],
         [vmem],
+        [pltpu.VMEM((wave_map.shape[0], LANES), F32), pltpu.VMEM((rows, LANES), F32)],
         flops=4_000_000_000,
-    )(spread)
+    )(wave_map.reshape(-1, LANES))
     flat, table = lax.optimization_barrier((flat, table))
 
     res, payload, norm = call(
@@ -415,7 +424,7 @@
         )(arrived, table, weight, norm)
         home = exchange(back, bands)
         (sums,) = call(tail_kernel, "tail", [small_shape], [vmem])(home)
-        others = [lax.ppermute(sums, "x", [(i, (i + k) % XS) for i in range(XS)]) for k in range(1, XS)]
+        others = [lax.ppermute(sums, "x", [(i, i ^ k) for i in range(XS)]) for k in range(1, XS)]
         (adjoint,) = call(
             functools.partial(back_kernel, slots, chunk_rows),
             "back",

time: 165 us -> 165 us (level)
  transfers between devices with their start and end apart: 12 -> 12, of which waited for: 2 -> 0; matrix products, arithmetic and copies ran while one was open for 1% -> 0% of each run, Pallas kernels for 9% -> 9%
where the time goes in v6:
time: 165 us; the launch traced here: 164 us
  blocking collectives  122 us (74%)
  Pallas kernels  25.6 us (16%)
  starting transfers between devices  14.9 us (9%)
    all_to_all x6, blocking collectives, exchange(): return lax.all_to_all(packed, BAND, 0, 0, tiled=True).reshape(rows, LANES)  122 us
    ppermute x9, starting transfers between devices, reach(): lax.ppermute(sums, 'x', [(i, i ^ k) for i in range(XS)])  10 us
    pallas_call x3, Pallas kernels, reach(): call(functools.partial(back_kernel, slots, chunk_rows), 'back', [vec_shap...  9.53 us
    ppermute x3, starting transfers between devices, on_device(): near.append(lax.ppermute(obs_weight, ('y', 'c'), pairs))  4.92 us
    pallas_call x3, Pallas kernels, reach(): call(grid_kernel, 'grid', [payload_shape], [vmem] * 4, [pltpu.VMEM((LANES...  4.79 us
    pallas_call x1, Pallas kernels, on_device(): call(functools.partial(fourier_kernel, chunk_rows, slots, 1.0 / math.sqrt...  3.66 us
    pallas_call x2, Pallas kernels, on_device(): call(functools.partial(middle_kernel, stage, slots, chunk_rows), f'middle...  3.33 us
  transfers between devices with their start and end apart: 12, of which 0 were waited for; matrix products, arithmetic and copies ran while one was open for 0% of the time, Pallas kernels for 9%

profile of v6, /device:TPU:1, one launch (start us, length us, event | category | flops | bytes accessed | tf_op | source)
XLA Modules:
  0.0 164.2 jit_solution(13293518824798764705)
XLA Ops:
  0.6 0.0 copy-start
  0.6 0.0 slice-start
  0.7 2.2 %collective-permute-start.1 = (f32[10,1280]{1,0:T(8,128)}, f32[10,1280]{1,0:T(8,128)S(1)}, u32[]{:S(2)}, u32[]{:S(2)}) collective-permute-start(f32[10,1280]{1,0:T(8,128)} %refs_0_.1), channel_id=1, source_target_pairs={{0,8},{4,12},{8,0},{12,4},{16,24},{20,28},{24,16},{28,20},{1,9},{5... | collective-permute-start | bytes 153608 | tf_op jit(solution)/shard_map/ppermute | solution.py:406
  2.9 1.2 collective-permute-start
  4.0 1.5 collective-permute-start.2
  5.6 0.0 copy-start.1
  5.6 0.7 copy-done.1
  6.3 0.0 slice-start.1
  6.3 0.0 copy-start.3
  6.3 3.7 %fourier.1.table_ref = bf16[1280,1280]{1,0:T(8,128)(2,1)S(1)} custom-call(s32[5,128]{1,0:T(8,128)S(1)} %bitcast.34), custom_call_target="tpu_custom_call" | custom-call | flops 4000000000 | bytes 1000000 | tf_op jit(solution)/shard_map/fourier/pallas_call | solution.py:385
  9.9 0.0 copy-done
  9.9 0.0 slice-done
  9.9 0.0 slice-done.1
  10.0 2.2 %first.1 = (f32[10,24,640]{2,1,0:T(8,128)S(1)}, bf16[1280,128]{1,0:T(8,128)(2,1)S(1)}, f32[8,128]{1,0:T(8,128)S(1)}) custom-call(s32[640]{0:T(1024)S(1)} %copy-done.1, f32[1200,128]{1,0:T(8,128)S(1)} %bitcast.18, bf16[10,640,640]{2,1,0:T(8,128)(2,1)S(1)} %bitcast.17), custom_call_target="tpu_custom_call" | custom-call | flops 2000000000 | bytes 1000000 | tf_op jit(solution)/shard_map/first/pallas_call | solution.py:395
  12.1 0.0 collective-permute-done.1.refs_2_
  12.2 0.0 collective-permute-done.refs_1_
  12.2 0.0 collective-permute-done.2.refs_3_
  12.2 0.0 copy-done.3
  12.2 0.1 weight.1.weight_ref
  12.3 0.0 copy-start.2
  12.3 24.5 %all_to_all.30 = bf16[64,10,2,128]{3,2,1,0:T(2,128)(2,1)S(1)} all-to-all(bf16[64,10,2,128]{3,2,1,0:T(2,128)(2,1)S(1)} %bitcast.19), channel_id=1, replica_groups=mesh['z'=8,'y'=4,'c'=2,'x'=4] {'z','y','c'}, dimensions={0} | all-to-all | bytes 655360 | tf_op jit(solution)/shard_map/all_to_all | solution.py:354
  36.7 1.6 grid.3
  38.3 19.0 %all_to_all.31 = bf16[64,10,2,128]{3,2,1,0:T(2,128)(2,1)S(1)} all-to-all(bf16[64,10,2,128]{3,2,1,0:T(2,128)(2,1)S(1)} %bitcast.31), channel_id=1, replica_groups=mesh['z'=8,'y'=4,'c'=2,'x'=4] {'z','y','c'}, dimensions={0} | all-to-all | bytes 655360 | tf_op jit(solution)/shard_map/all_to_all | solution.py:354
  57.4 0.2 tail.3.refs_0_
  57.5 2.6 %collective-permute-start.5 = (f32[8,128]{1,0:T(8,128)S(1)}, f32[8,128]{1,0:T(8,128)S(1)}, u32[]{:S(2)}, u32[]{:S(2)}) collective-permute-start(f32[8,128]{1,0:T(8,128)S(1)} %tail.3.refs_0_), channel_id=1, source_target_pairs={{0,3},{1,2},{2,1},{3,0},{4,7},{5,6},{6,5},{7,4},{8,11},{9,10},{10,... | collective-permute-start | bytes 12296 | tf_op jit(solution)/shard_map/ppermute | solution.py:427
  60.1 0.5 collective-permute-start.4
  60.6 0.3 collective-permute-start.3
  60.9 0.0 copy-done.2
  60.9 3.2 %back.3.refs_5_ = f32[10,24,640]{2,1,0:T(8,128)S(1)} custom-call(s32[640]{0:T(1024)S(1)} %copy-done.2, bf16[1280,128]{1,0:T(8,128)(2,1)S(1)} %bitcast.21, bf16[10,640,640]{2,1,0:T(8,128)(2,1)S(1)} %bitcast.17), custom_call_target="tpu_custom_call" | custom-call | flops 8000000000 | bytes 1000000 | tf_op jit(solution)/shard_map/back/pallas_call | solution.py:428
  64.1 0.0 collective-permute-done.5.refs_3_
  64.1 0.0 collective-permute-done.4.refs_2_
  64.1 0.0 collective-permute-done.3.refs_1_
  64.1 1.6 middle0.1
  65.7 20.4 %all_to_all.32 = bf16[64,10,2,128]{3,2,1,0:T(2,128)(2,1)S(1)} all-to-all(bf16[64,10,2,128]{3,2,1,0:T(2,128)(2,1)S(1)} %bitcast.27), channel_id=1, replica_groups=mesh['z'=8,'y'=4,'c'=2,'x'=4] {'z','y','c'}, dimensions={0} | all-to-all | bytes 655360 | tf_op jit(solution)/shard_map/all_to_all | solution.py:354
  86.1 1.6 grid.4
  87.7 19.0 %all_to_all.33 = bf16[64,10,2,128]{3,2,1,0:T(2,128)(2,1)S(1)} all-to-all(bf16[64,10,2,128]{3,2,1,0:T(2,128)(2,1)S(1)} %bitcast.33), channel_id=1, replica_groups=mesh['z'=8,'y'=4,'c'=2,'x'=4] {'z','y','c'}, dimensions={0} | all-to-all | bytes 655360 | tf_op jit(solution)/shard_map/all_to_all | solution.py:354
  106.8 0.2 tail.4.refs_0_
  107.0 2.0 %collective-permute-start.8 = (f32[8,128]{1,0:T(8,128)S(1)}, f32[8,128]{1,0:T(8,128)S(1)}, u32[]{:S(2)}, u32[]{:S(2)}) collective-permute-start(f32[8,128]{1,0:T(8,128)S(1)} %tail.4.refs_0_), channel_id=1, source_target_pairs={{0,3},{1,2},{2,1},{3,0},{4,7},{5,6},{6,5},{7,4},{8,11},{9,10},{10,... | collective-permute-start | bytes 12296 | tf_op jit(solution)/shard_map/ppermute | solution.py:427
  109.0 0.5 collective-permute-start.7
  109.5 0.8 collective-permute-start.6
  110.3 3.2 %back.4.refs_5_ = f32[10,24,640]{2,1,0:T(8,128)S(1)} custom-call(s32[640]{0:T(1024)S(1)} %copy-done.2, bf16[1280,128]{1,0:T(8,128)(2,1)S(1)} %bitcast.23, bf16[10,640,640]{2,1,0:T(8,128)(2,1)S(1)} %bitcast.17), custom_call_target="tpu_custom_call" | custom-call | flops 8000000000 | bytes 1000000 | tf_op jit(solution)/shard_map/back/pallas_call | solution.py:428
  113.5 0.0 collective-permute-done.8.refs_3_
  113.5 0.0 collective-permute-done.7.refs_2_
  113.5 0.0 collective-permute-done.6.refs_1_
  113.5 1.7 %middle1.1 = (f32[10,24,640]{2,1,0:T(8,128)S(1)}, f32[10,24,640]{2,1,0:T(8,128)S(1)}, bf16[1280,128]{1,0:T(8,128)(2,1)S(1)}, f32[8,128]{1,0:T(8,128)S(1)}, f32[8,128]{1,0:T(8,128)S(1)}) custom-call(f32[8,128]{1,0:T(8,128)S(1)} %tail.4.refs_0_, f32[8,128]{1,0:T(8,128)S(1)} %collective-permute-done.6.refs_1_, f32[8,128]{1,0:T(8,128)S(1)} %collective-permute-done.7.refs_2_, ...), custom_call_target="tpu_custom_call" | custom-call | flops 2000000000 | bytes 1000000 | tf_op jit(solution)/shard_map/middle1/pallas_call | solution.py:443
  115.2 19.9 %all_to_all.34 = bf16[64,10,2,128]{3,2,1,0:T(2,128)(2,1)S(1)} all-to-all(bf16[64,10,2,128]{3,2,1,0:T(2,128)(2,1)S(1)} %bitcast.26), channel_id=1, replica_groups=mesh['z'=8,'y'=4,'c'=2,'x'=4] {'z','y','c'}, dimensions={0} | all-to-all | bytes 655360 | tf_op jit(solution)/shard_map/all_to_all | solution.py:354
  135.1 1.6 grid.5
  136.7 19.0 %all_to_all.35 = bf16[64,10,2,128]{3,2,1,0:T(2,128)(2,1)S(1)} all-to-all(bf16[64,10,2,128]{3,2,1,0:T(2,128)(2,1)S(1)} %bitcast.29), channel_id=1, replica_groups=mesh['z'=8,'y'=4,'c'=2,'x'=4] {'z','y','c'}, dimensions={0} | all-to-all | bytes 655360 | tf_op jit(solution)/shard_map/all_to_all | solution.py:354
  155.8 0.2 tail.5.refs_0_
  155.9 2.0 %collective-permute-start.11 = (f32[8,128]{1,0:T(8,128)S(1)}, f32[8,128]{1,0:T(8,128)S(1)}, u32[]{:S(2)}, u32[]{:S(2)}) collective-permute-start(f32[8,128]{1,0:T(8,128)S(1)} %tail.5.refs_0_), channel_id=1, source_target_pairs={{0,3},{1,2},{2,1},{3,0},{4,7},{5,6},{6,5},{7,4},{8,11},{9,10},{10,... | collective-permute-start | bytes 12296 | tf_op jit(solution)/shard_map/ppermute | solution.py:427
  158.0 0.5 collective-permute-start.10
  158.5 0.8 collective-permute-start.9
  159.3 3.2 %back.5.refs_4_ = f32[10,24,640]{2,1,0:T(8,128)S(1)} custom-call(s32[640]{0:T(1024)S(1)} %copy-done.2, bf16[1280,128]{1,0:T(8,128)(2,1)S(1)} %bitcast.25, bf16[10,640,640]{2,1,0:T(8,128)(2,1)S(1)} %bitcast.17), custom_call_target="tpu_custom_call" | custom-call | flops 8000000000 | bytes 1000000 | tf_op jit(solution)/shard_map/back/pallas_call | solution.py:428
  162.4 0.0 collective-permute-done.11.refs_3_
  162.5 0.0 collective-permute-done.10.refs_2_
  162.5 0.0 collective-permute-done.9.refs_1_
  162.5 1.5 last.1
  (1 shorter events, 0.0 us)
Async XLA Ops:
  0.6 9.3 %copy-start = (f32[10,2,1,12,640]{4,2,3,1,0:T(1,128)S(1)}, f32[10,2,1,12,640]{4,2,3,1,0:T(1,128)}, u32[]{:S(2)}) copy-start(f32[10,2,1,12,640]{4,2,3,1,0:T(1,128)} %param.4) | copy-start | bytes 1843204
  0.6 9.3 %slice-start = ((s8[8192000]{0:T(1024)(128)(4,1)}), s8[4194304]{0:T(1024)(128)(4,1)S(1)}, s32[]{:S(2)}) async-start(s8[8192000]{0:T(1024)(128)(4,1)} %bitcast.16), calls=%async_computation.6 | async-start | bytes 8388608
  0.7 11.5 %collective-permute-start.1 = (f32[10,1280]{1,0:T(8,128)}, f32[10,1280]{1,0:T(8,128)S(1)}, u32[]{:S(2)}, u32[]{:S(2)}) collective-permute-start(f32[10,1280]{1,0:T(8,128)} %refs_0_.1), channel_id=1, source_target_pairs={{0,8},{4,12},{8,0},{12,4},{16,24},{20,28},{24,16},{28,20},{1,9},{5... | collective-permute-start | bytes 153608 | tf_op jit(solution)/shard_map/ppermute | solution.py:406
  2.9 9.3 %collective-permute-start = (f32[10,1280]{1,0:T(8,128)}, f32[10,1280]{1,0:T(8,128)S(1)}, u32[]{:S(2)}, u32[]{:S(2)}) collective-permute-start(f32[10,1280]{1,0:T(8,128)} %refs_0_.1), channel_id=1, source_target_pairs={{0,4},{4,0},{8,12},{12,8},{16,20},{20,16},{24,28},{28,24},{1,5},{5... | collective-permute-start | bytes 153608 | tf_op jit(solution)/shard_map/ppermute | solution.py:406
  4.0 8.1 %collective-permute-start.2 = (f32[10,1280]{1,0:T(8,128)}, f32[10,1280]{1,0:T(8,128)S(1)}, u32[]{:S(2)}, u32[]{:S(2)}) collective-permute-start(f32[10,1280]{1,0:T(8,128)} %refs_0_.1), channel_id=1, source_target_pairs={{0,12},{4,8},{8,4},{12,0},{16,28},{20,24},{24,20},{28,16},{1,13},{... | collective-permute-start | bytes 153608 | tf_op jit(solution)/shard_map/ppermute | solution.py:406
  5.6 0.7 copy-start.1
  6.3 3.7 %slice-start.1 = ((s8[8192000]{0:T(1024)(128)(4,1)}), s8[3997696]{0:T(1024)(128)(4,1)S(1)}, s32[]{:S(2)}) async-start(s8[8192000]{0:T(1024)(128)(4,1)} %bitcast.16), calls=%async_computation.7 | async-start | bytes 7995392
  6.3 5.9 %copy-start.3 = (f32[10,1280]{1,0:T(8,128)S(1)}, f32[10,1280]{1,0:T(8,128)}, u32[]{:S(2)}) copy-start(f32[10,1280]{1,0:T(8,128)} %refs_0_.1) | copy-start | bytes 153604
  12.3 48.6 %copy-start.2 = (s32[640]{0:T(1024)S(1)}, s32[640]{0:T(1024)}, u32[]{:S(2)}) copy-start(s32[640]{0:T(1024)} %waves_ref.7) | copy-start | bytes 7684
  57.5 6.5 %collective-permute-start.5 = (f32[8,128]{1,0:T(8,128)S(1)}, f32[8,128]{1,0:T(8,128)S(1)}, u32[]{:S(2)}, u32[]{:S(2)}) collective-permute-start(f32[8,128]{1,0:T(8,128)S(1)} %tail.3.refs_0_), channel_id=1, source_target_pairs={{0,3},{1,2},{2,1},{3,0},{4,7},{5,6},{6,5},{7,4},{8,11},{9,10},{10,... | collective-permute-start | bytes 12296 | tf_op jit(solution)/shard_map/ppermute | solution.py:427
  60.1 4.0 %collective-permute-start.4 = (f32[8,128]{1,0:T(8,128)S(1)}, f32[8,128]{1,0:T(8,128)S(1)}, u32[]{:S(2)}, u32[]{:S(2)}) collective-permute-start(f32[8,128]{1,0:T(8,128)S(1)} %tail.3.refs_0_), channel_id=1, source_target_pairs={{0,2},{1,3},{2,0},{3,1},{4,6},{5,7},{6,4},{7,5},{8,10},{9,11},{10,... | collective-permute-start | bytes 12296 | tf_op jit(solution)/shard_map/ppermute | solution.py:427
  60.6 3.5 %collective-permute-start.3 = (f32[8,128]{1,0:T(8,128)S(1)}, f32[8,128]{1,0:T(8,128)S(1)}, u32[]{:S(2)}, u32[]{:S(2)}) collective-permute-start(f32[8,128]{1,0:T(8,128)S(1)} %tail.3.refs_0_), channel_id=1, source_target_pairs={{0,1},{1,0},{2,3},{3,2},{4,5},{5,4},{6,7},{7,6},{8,9},{9,8},{10,11... | collective-permute-start | bytes 12296 | tf_op jit(solution)/shard_map/ppermute | solution.py:427
  107.0 6.5 %collective-permute-start.8 = (f32[8,128]{1,0:T(8,128)S(1)}, f32[8,128]{1,0:T(8,128)S(1)}, u32[]{:S(2)}, u32[]{:S(2)}) collective-permute-start(f32[8,128]{1,0:T(8,128)S(1)} %tail.4.refs_0_), channel_id=1, source_target_pairs={{0,3},{1,2},{2,1},{3,0},{4,7},{5,6},{6,5},{7,4},{8,11},{9,10},{10,... | collective-permute-start | bytes 12296 | tf_op jit(solution)/shard_map/ppermute | solution.py:427
  109.0 4.5 %collective-permute-start.7 = (f32[8,128]{1,0:T(8,128)S(1)}, f32[8,128]{1,0:T(8,128)S(1)}, u32[]{:S(2)}, u32[]{:S(2)}) collective-permute-start(f32[8,128]{1,0:T(8,128)S(1)} %tail.4.refs_0_), channel_id=1, source_target_pairs={{0,2},{1,3},{2,0},{3,1},{4,6},{5,7},{6,4},{7,5},{8,10},{9,11},{10,... | collective-permute-start | bytes 12296 | tf_op jit(solution)/shard_map/ppermute | solution.py:427
  109.5 4.0 %collective-permute-start.6 = (f32[8,128]{1,0:T(8,128)S(1)}, f32[8,128]{1,0:T(8,128)S(1)}, u32[]{:S(2)}, u32[]{:S(2)}) collective-permute-start(f32[8,128]{1,0:T(8,128)S(1)} %tail.4.refs_0_), channel_id=1, source_target_pairs={{0,1},{1,0},{2,3},{3,2},{4,5},{5,4},{6,7},{7,6},{8,9},{9,8},{10,11... | collective-permute-start | bytes 12296 | tf_op jit(solution)/shard_map/ppermute | solution.py:427
  155.9 6.5 %collective-permute-start.11 = (f32[8,128]{1,0:T(8,128)S(1)}, f32[8,128]{1,0:T(8,128)S(1)}, u32[]{:S(2)}, u32[]{:S(2)}) collective-permute-start(f32[8,128]{1,0:T(8,128)S(1)} %tail.5.refs_0_), channel_id=1, source_target_pairs={{0,3},{1,2},{2,1},{3,0},{4,7},{5,6},{6,5},{7,4},{8,11},{9,10},{10,... | collective-permute-start | bytes 12296 | tf_op jit(solution)/shard_map/ppermute | solution.py:427
  158.0 4.5 %collective-permute-start.10 = (f32[8,128]{1,0:T(8,128)S(1)}, f32[8,128]{1,0:T(8,128)S(1)}, u32[]{:S(2)}, u32[]{:S(2)}) collective-permute-start(f32[8,128]{1,0:T(8,128)S(1)} %tail.5.refs_0_), channel_id=1, source_target_pairs={{0,2},{1,3},{2,0},{3,1},{4,6},{5,7},{6,4},{7,5},{8,10},{9,11},{10,... | collective-permute-start | bytes 12296 | tf_op jit(solution)/shard_map/ppermute | solution.py:427
  158.5 4.0 %collective-permute-start.9 = (f32[8,128]{1,0:T(8,128)S(1)}, f32[8,128]{1,0:T(8,128)S(1)}, u32[]{:S(2)}, u32[]{:S(2)}) collective-permute-start(f32[8,128]{1,0:T(8,128)S(1)} %tail.5.refs_0_), channel_id=1, source_target_pairs={{0,1},{1,0},{2,3},{3,2},{4,5},{5,4},{6,7},{7,6},{8,9},{9,8},{10,11... | collective-permute-start | bytes 12296 | tf_op jit(solution)/shard_map/ppermute | solution.py:427

commit v7 on v6

--- a/solution.py
+++ b/solution.py
@@ -272,7 +272,7 @@
             before, now = now, twice * now - before
         return carry
 
-    lax.fori_loop(0, waves_ref.shape[0] // rows, step, 0)
+    lax.fori_loop(0, waves_ref.shape[0] // rows, step, 0, unroll=5)
 
 
 def weight_kernel(*refs):

time: 165 us -> 164 us (level)
  no operation moved by 1% of the time
where the time goes in v7:
time: 164 us
  blocking collectives  122 us (74%)
  Pallas kernels  25.4 us (15%)
  starting transfers between devices  14.9 us (9%)
    all_to_all x6, blocking collectives, exchange(): return lax.all_to_all(packed, BAND, 0, 0, tiled=True).reshape(rows, LANES)  122 us
    ppermute x9, starting transfers between devices, reach(): lax.ppermute(sums, 'x', [(i, i ^ k) for i in range(XS)])  10 us
    pallas_call x3, Pallas kernels, reach(): call(functools.partial(back_kernel, slots, chunk_rows), 'back', [vec_shap...  9.53 us
    ppermute x3, starting transfers between devices, on_device(): near.append(lax.ppermute(obs_weight, ('y', 'c'), pairs))  4.92 us
    pallas_call x3, Pallas kernels, reach(): call(grid_kernel, 'grid', [payload_shape], [vmem] * 4, [pltpu.VMEM((LANES...  4.78 us
    pallas_call x1, Pallas kernels, on_device(): call(functools.partial(fourier_kernel, chunk_rows, slots, 1.0 / math.sqrt...  3.47 us
    pallas_call x2, Pallas kernels, on_device(): call(functools.partial(middle_kernel, stage, slots, chunk_rows), f'middle...  3.33 us
  transfers between devices with their start and end apart: 12, of which 0 were waited for; matrix products, arithmetic and copies ran while one was open for 0% of the time, Pallas kernels for 9%

profile of v7, /device:TPU:1, one launch (start us, length us, event | category | flops | bytes accessed | tf_op | source)
XLA Modules:
  0.0 164.0 jit_solution(18426414252078297831)
XLA Ops:
  0.6 0.0 copy-start
  0.6 0.0 slice-start
  0.7 2.2 %collective-permute-start.1 = (f32[10,1280]{1,0:T(8,128)}, f32[10,1280]{1,0:T(8,128)S(1)}, u32[]{:S(2)}, u32[]{:S(2)}) collective-permute-start(f32[10,1280]{1,0:T(8,128)} %refs_0_.1), channel_id=1, source_target_pairs={{0,8},{4,12},{8,0},{12,4},{16,24},{20,28},{24,16},{28,20},{1,9},{5... | collective-permute-start | bytes 153608 | tf_op jit(solution)/shard_map/ppermute | solution.py:406
  2.9 1.2 collective-permute-start
  4.0 1.5 collective-permute-start.2
  5.6 0.0 copy-start.1
  5.6 0.7 copy-done.1
  6.3 0.0 slice-start.1
  6.3 0.0 copy-start.3
  6.3 3.5 %fourier.1.table_ref = bf16[1280,1280]{1,0:T(8,128)(2,1)S(1)} custom-call(s32[5,128]{1,0:T(8,128)S(1)} %bitcast.34), custom_call_target="tpu_custom_call" | custom-call | flops 4000000000 | bytes 1000000 | tf_op jit(solution)/shard_map/fourier/pallas_call | solution.py:385
  9.7 0.0 copy-done
  9.7 0.0 slice-done
  9.8 0.0 slice-done.1
  9.8 2.2 %first.1 = (f32[10,24,640]{2,1,0:T(8,128)S(1)}, bf16[1280,128]{1,0:T(8,128)(2,1)S(1)}, f32[8,128]{1,0:T(8,128)S(1)}) custom-call(s32[640]{0:T(1024)S(1)} %copy-done.1, f32[1200,128]{1,0:T(8,128)S(1)} %bitcast.18, bf16[10,640,640]{2,1,0:T(8,128)(2,1)S(1)} %bitcast.17), custom_call_target="tpu_custom_call" | custom-call | flops 2000000000 | bytes 1000000 | tf_op jit(solution)/shard_map/first/pallas_call | solution.py:395
  12.0 0.0 collective-permute-done.1.refs_2_
  12.0 0.0 collective-permute-done.refs_1_
  12.0 0.0 collective-permute-done.2.refs_3_
  12.0 0.0 copy-done.3
  12.0 0.1 weight.1.weight_ref
  12.1 0.0 copy-start.2
  12.1 24.5 %all_to_all.30 = bf16[64,10,2,128]{3,2,1,0:T(2,128)(2,1)S(1)} all-to-all(bf16[64,10,2,128]{3,2,1,0:T(2,128)(2,1)S(1)} %bitcast.19), channel_id=1, replica_groups=mesh['z'=8,'y'=4,'c'=2,'x'=4] {'z','y','c'}, dimensions={0} | all-to-all | bytes 655360 | tf_op jit(solution)/shard_map/all_to_all | solution.py:354
  36.5 1.6 grid.3
  38.1 19.0 %all_to_all.31 = bf16[64,10,2,128]{3,2,1,0:T(2,128)(2,1)S(1)} all-to-all(bf16[64,10,2,128]{3,2,1,0:T(2,128)(2,1)S(1)} %bitcast.31), channel_id=1, replica_groups=mesh['z'=8,'y'=4,'c'=2,'x'=4] {'z','y','c'}, dimensions={0} | all-to-all | bytes 655360 | tf_op jit(solution)/shard_map/all_to_all | solution.py:354
  57.2 0.2 tail.3.refs_0_
  57.3 2.6 %collective-permute-start.5 = (f32[8,128]{1,0:T(8,128)S(1)}, f32[8,128]{1,0:T(8,128)S(1)}, u32[]{:S(2)}, u32[]{:S(2)}) collective-permute-start(f32[8,128]{1,0:T(8,128)S(1)} %tail.3.refs_0_), channel_id=1, source_target_pairs={{0,3},{1,2},{2,1},{3,0},{4,7},{5,6},{6,5},{7,4},{8,11},{9,10},{10,... | collective-permute-start | bytes 12296 | tf_op jit(solution)/shard_map/ppermute | solution.py:427
  59.9 0.5 collective-permute-start.4
  60.4 0.2 collective-permute-start.3
  60.7 0.0 copy-done.2
  60.7 3.2 %back.3.refs_5_ = f32[10,24,640]{2,1,0:T(8,128)S(1)} custom-call(s32[640]{0:T(1024)S(1)} %copy-done.2, bf16[1280,128]{1,0:T(8,128)(2,1)S(1)} %bitcast.21, bf16[10,640,640]{2,1,0:T(8,128)(2,1)S(1)} %bitcast.17), custom_call_target="tpu_custom_call" | custom-call | flops 8000000000 | bytes 1000000 | tf_op jit(solution)/shard_map/back/pallas_call | solution.py:428
  63.9 0.0 collective-permute-done.5.refs_3_
  63.9 0.0 collective-permute-done.4.refs_2_
  63.9 0.0 collective-permute-done.3.refs_1_
  63.9 1.6 middle0.1
  65.5 20.4 %all_to_all.32 = bf16[64,10,2,128]{3,2,1,0:T(2,128)(2,1)S(1)} all-to-all(bf16[64,10,2,128]{3,2,1,0:T(2,128)(2,1)S(1)} %bitcast.27), channel_id=1, replica_groups=mesh['z'=8,'y'=4,'c'=2,'x'=4] {'z','y','c'}, dimensions={0} | all-to-all | bytes 655360 | tf_op jit(solution)/shard_map/all_to_all | solution.py:354
  86.0 1.6 grid.4
  87.6 19.0 %all_to_all.33 = bf16[64,10,2,128]{3,2,1,0:T(2,128)(2,1)S(1)} all-to-all(bf16[64,10,2,128]{3,2,1,0:T(2,128)(2,1)S(1)} %bitcast.33), channel_id=1, replica_groups=mesh['z'=8,'y'=4,'c'=2,'x'=4] {'z','y','c'}, dimensions={0} | all-to-all | bytes 655360 | tf_op jit(solution)/shard_map/all_to_all | solution.py:354
  106.6 0.2 tail.4.refs_0_
  106.8 2.0 %collective-permute-start.8 = (f32[8,128]{1,0:T(8,128)S(1)}, f32[8,128]{1,0:T(8,128)S(1)}, u32[]{:S(2)}, u32[]{:S(2)}) collective-permute-start(f32[8,128]{1,0:T(8,128)S(1)} %tail.4.refs_0_), channel_id=1, source_target_pairs={{0,3},{1,2},{2,1},{3,0},{4,7},{5,6},{6,5},{7,4},{8,11},{9,10},{10,... | collective-permute-start | bytes 12296 | tf_op jit(solution)/shard_map/ppermute | solution.py:427
  108.8 0.5 collective-permute-start.7
  109.3 0.8 collective-permute-start.6
  110.1 3.2 %back.4.refs_5_ = f32[10,24,640]{2,1,0:T(8,128)S(1)} custom-call(s32[640]{0:T(1024)S(1)} %copy-done.2, bf16[1280,128]{1,0:T(8,128)(2,1)S(1)} %bitcast.23, bf16[10,640,640]{2,1,0:T(8,128)(2,1)S(1)} %bitcast.17), custom_call_target="tpu_custom_call" | custom-call | flops 8000000000 | bytes 1000000 | tf_op jit(solution)/shard_map/back/pallas_call | solution.py:428
  113.3 0.0 collective-permute-done.8.refs_3_
  113.3 0.0 collective-permute-done.7.refs_2_
  113.3 0.0 collective-permute-done.6.refs_1_
  113.3 1.7 %middle1.1 = (f32[10,24,640]{2,1,0:T(8,128)S(1)}, f32[10,24,640]{2,1,0:T(8,128)S(1)}, bf16[1280,128]{1,0:T(8,128)(2,1)S(1)}, f32[8,128]{1,0:T(8,128)S(1)}, f32[8,128]{1,0:T(8,128)S(1)}) custom-call(f32[8,128]{1,0:T(8,128)S(1)} %tail.4.refs_0_, f32[8,128]{1,0:T(8,128)S(1)} %collective-permute-done.6.refs_1_, f32[8,128]{1,0:T(8,128)S(1)} %collective-permute-done.7.refs_2_, ...), custom_call_target="tpu_custom_call" | custom-call | flops 2000000000 | bytes 1000000 | tf_op jit(solution)/shard_map/middle1/pallas_call | solution.py:443
  115.1 19.9 %all_to_all.34 = bf16[64,10,2,128]{3,2,1,0:T(2,128)(2,1)S(1)} all-to-all(bf16[64,10,2,128]{3,2,1,0:T(2,128)(2,1)S(1)} %bitcast.26), channel_id=1, replica_groups=mesh['z'=8,'y'=4,'c'=2,'x'=4] {'z','y','c'}, dimensions={0} | all-to-all | bytes 655360 | tf_op jit(solution)/shard_map/all_to_all | solution.py:354
  134.9 1.6 grid.5
  136.5 19.0 %all_to_all.35 = bf16[64,10,2,128]{3,2,1,0:T(2,128)(2,1)S(1)} all-to-all(bf16[64,10,2,128]{3,2,1,0:T(2,128)(2,1)S(1)} %bitcast.29), channel_id=1, replica_groups=mesh['z'=8,'y'=4,'c'=2,'x'=4] {'z','y','c'}, dimensions={0} | all-to-all | bytes 655360 | tf_op jit(solution)/shard_map/all_to_all | solution.py:354
  155.6 0.2 tail.5.refs_0_
  155.7 2.0 %collective-permute-start.11 = (f32[8,128]{1,0:T(8,128)S(1)}, f32[8,128]{1,0:T(8,128)S(1)}, u32[]{:S(2)}, u32[]{:S(2)}) collective-permute-start(f32[8,128]{1,0:T(8,128)S(1)} %tail.5.refs_0_), channel_id=1, source_target_pairs={{0,3},{1,2},{2,1},{3,0},{4,7},{5,6},{6,5},{7,4},{8,11},{9,10},{10,... | collective-permute-start | bytes 12296 | tf_op jit(solution)/shard_map/ppermute | solution.py:427
  157.8 0.5 collective-permute-start.10
  158.3 0.8 collective-permute-start.9
  159.1 3.2 %back.5.refs_4_ = f32[10,24,640]{2,1,0:T(8,128)S(1)} custom-call(s32[640]{0:T(1024)S(1)} %copy-done.2, bf16[1280,128]{1,0:T(8,128)(2,1)S(1)} %bitcast.25, bf16[10,640,640]{2,1,0:T(8,128)(2,1)S(1)} %bitcast.17), custom_call_target="tpu_custom_call" | custom-call | flops 8000000000 | bytes 1000000 | tf_op jit(solution)/shard_map/back/pallas_call | solution.py:428
  162.2 0.0 collective-permute-done.11.refs_3_
  162.3 0.0 collective-permute-done.10.refs_2_
  162.3 0.0 collective-permute-done.9.refs_1_
  162.3 1.5 last.1
  (1 shorter events, 0.0 us)
Async XLA Ops:
  0.6 9.1 %copy-start = (f32[10,2,1,12,640]{4,2,3,1,0:T(1,128)S(1)}, f32[10,2,1,12,640]{4,2,3,1,0:T(1,128)}, u32[]{:S(2)}) copy-start(f32[10,2,1,12,640]{4,2,3,1,0:T(1,128)} %param.4) | copy-start | bytes 1843204
  0.6 9.1 %slice-start = ((s8[8192000]{0:T(1024)(128)(4,1)}), s8[4194304]{0:T(1024)(128)(4,1)S(1)}, s32[]{:S(2)}) async-start(s8[8192000]{0:T(1024)(128)(4,1)} %bitcast.16), calls=%async_computation.6 | async-start | bytes 8388608
  0.7 11.3 %collective-permute-start.1 = (f32[10,1280]{1,0:T(8,128)}, f32[10,1280]{1,0:T(8,128)S(1)}, u32[]{:S(2)}, u32[]{:S(2)}) collective-permute-start(f32[10,1280]{1,0:T(8,128)} %refs_0_.1), channel_id=1, source_target_pairs={{0,8},{4,12},{8,0},{12,4},{16,24},{20,28},{24,16},{28,20},{1,9},{5... | collective-permute-start | bytes 153608 | tf_op jit(solution)/shard_map/ppermute | solution.py:406
  2.9 9.1 %collective-permute-start = (f32[10,1280]{1,0:T(8,128)}, f32[10,1280]{1,0:T(8,128)S(1)}, u32[]{:S(2)}, u32[]{:S(2)}) collective-permute-start(f32[10,1280]{1,0:T(8,128)} %refs_0_.1), channel_id=1, source_target_pairs={{0,4},{4,0},{8,12},{12,8},{16,20},{20,16},{24,28},{28,24},{1,5},{5... | collective-permute-start | bytes 153608 | tf_op jit(solution)/shard_map/ppermute | solution.py:406
  4.0 7.9 %collective-permute-start.2 = (f32[10,1280]{1,0:T(8,128)}, f32[10,1280]{1,0:T(8,128)S(1)}, u32[]{:S(2)}, u32[]{:S(2)}) collective-permute-start(f32[10,1280]{1,0:T(8,128)} %refs_0_.1), channel_id=1, source_target_pairs={{0,12},{4,8},{8,4},{12,0},{16,28},{20,24},{24,20},{28,16},{1,13},{... | collective-permute-start | bytes 153608 | tf_op jit(solution)/shard_map/ppermute | solution.py:406
  5.6 0.7 copy-start.1
  6.3 3.5 %slice-start.1 = ((s8[8192000]{0:T(1024)(128)(4,1)}), s8[3997696]{0:T(1024)(128)(4,1)S(1)}, s32[]{:S(2)}) async-start(s8[8192000]{0:T(1024)(128)(4,1)} %bitcast.16), calls=%async_computation.7 | async-start | bytes 7995392
  6.3 5.7 %copy-start.3 = (f32[10,1280]{1,0:T(8,128)S(1)}, f32[10,1280]{1,0:T(8,128)}, u32[]{:S(2)}) copy-start(f32[10,1280]{1,0:T(8,128)} %refs_0_.1) | copy-start | bytes 153604
  12.1 48.6 %copy-start.2 = (s32[640]{0:T(1024)S(1)}, s32[640]{0:T(1024)}, u32[]{:S(2)}) copy-start(s32[640]{0:T(1024)} %waves_ref.7) | copy-start | bytes 7684
  57.3 6.5 %collective-permute-start.5 = (f32[8,128]{1,0:T(8,128)S(1)}, f32[8,128]{1,0:T(8,128)S(1)}, u32[]{:S(2)}, u32[]{:S(2)}) collective-permute-start(f32[8,128]{1,0:T(8,128)S(1)} %tail.3.refs_0_), channel_id=1, source_target_pairs={{0,3},{1,2},{2,1},{3,0},{4,7},{5,6},{6,5},{7,4},{8,11},{9,10},{10,... | collective-permute-start | bytes 12296 | tf_op jit(solution)/shard_map/ppermute | solution.py:427
  59.9 4.0 %collective-permute-start.4 = (f32[8,128]{1,0:T(8,128)S(1)}, f32[8,128]{1,0:T(8,128)S(1)}, u32[]{:S(2)}, u32[]{:S(2)}) collective-permute-start(f32[8,128]{1,0:T(8,128)S(1)} %tail.3.refs_0_), channel_id=1, source_target_pairs={{0,2},{1,3},{2,0},{3,1},{4,6},{5,7},{6,4},{7,5},{8,10},{9,11},{10,... | collective-permute-start | bytes 12296 | tf_op jit(solution)/shard_map/ppermute | solution.py:427
  60.4 3.5 %collective-permute-start.3 = (f32[8,128]{1,0:T(8,128)S(1)}, f32[8,128]{1,0:T(8,128)S(1)}, u32[]{:S(2)}, u32[]{:S(2)}) collective-permute-start(f32[8,128]{1,0:T(8,128)S(1)} %tail.3.refs_0_), channel_id=1, source_target_pairs={{0,1},{1,0},{2,3},{3,2},{4,5},{5,4},{6,7},{7,6},{8,9},{9,8},{10,11... | collective-permute-start | bytes 12296 | tf_op jit(solution)/shard_map/ppermute | solution.py:427
  106.8 6.5 %collective-permute-start.8 = (f32[8,128]{1,0:T(8,128)S(1)}, f32[8,128]{1,0:T(8,128)S(1)}, u32[]{:S(2)}, u32[]{:S(2)}) collective-permute-start(f32[8,128]{1,0:T(8,128)S(1)} %tail.4.refs_0_), channel_id=1, source_target_pairs={{0,3},{1,2},{2,1},{3,0},{4,7},{5,6},{6,5},{7,4},{8,11},{9,10},{10,... | collective-permute-start | bytes 12296 | tf_op jit(solution)/shard_map/ppermute | solution.py:427
  108.8 4.5 %collective-permute-start.7 = (f32[8,128]{1,0:T(8,128)S(1)}, f32[8,128]{1,0:T(8,128)S(1)}, u32[]{:S(2)}, u32[]{:S(2)}) collective-permute-start(f32[8,128]{1,0:T(8,128)S(1)} %tail.4.refs_0_), channel_id=1, source_target_pairs={{0,2},{1,3},{2,0},{3,1},{4,6},{5,7},{6,4},{7,5},{8,10},{9,11},{10,... | collective-permute-start | bytes 12296 | tf_op jit(solution)/shard_map/ppermute | solution.py:427
  109.3 4.0 %collective-permute-start.6 = (f32[8,128]{1,0:T(8,128)S(1)}, f32[8,128]{1,0:T(8,128)S(1)}, u32[]{:S(2)}, u32[]{:S(2)}) collective-permute-start(f32[8,128]{1,0:T(8,128)S(1)} %tail.4.refs_0_), channel_id=1, source_target_pairs={{0,1},{1,0},{2,3},{3,2},{4,5},{5,4},{6,7},{7,6},{8,9},{9,8},{10,11... | collective-permute-start | bytes 12296 | tf_op jit(solution)/shard_map/ppermute | solution.py:427
  155.7 6.5 %collective-permute-start.11 = (f32[8,128]{1,0:T(8,128)S(1)}, f32[8,128]{1,0:T(8,128)S(1)}, u32[]{:S(2)}, u32[]{:S(2)}) collective-permute-start(f32[8,128]{1,0:T(8,128)S(1)} %tail.5.refs_0_), channel_id=1, source_target_pairs={{0,3},{1,2},{2,1},{3,0},{4,7},{5,6},{6,5},{7,4},{8,11},{9,10},{10,... | collective-permute-start | bytes 12296 | tf_op jit(solution)/shard_map/ppermute | solution.py:427
  157.8 4.5 %collective-permute-start.10 = (f32[8,128]{1,0:T(8,128)S(1)}, f32[8,128]{1,0:T(8,128)S(1)}, u32[]{:S(2)}, u32[]{:S(2)}) collective-permute-start(f32[8,128]{1,0:T(8,128)S(1)} %tail.5.refs_0_), channel_id=1, source_target_pairs={{0,2},{1,3},{2,0},{3,1},{4,6},{5,7},{6,4},{7,5},{8,10},{9,11},{10,... | collective-permute-start | bytes 12296 | tf_op jit(solution)/shard_map/ppermute | solution.py:427
  158.3 4.0 %collective-permute-start.9 = (f32[8,128]{1,0:T(8,128)S(1)}, f32[8,128]{1,0:T(8,128)S(1)}, u32[]{:S(2)}, u32[]{:S(2)}) collective-permute-start(f32[8,128]{1,0:T(8,128)S(1)} %tail.5.refs_0_), channel_id=1, source_target_pairs={{0,1},{1,0},{2,3},{3,2},{4,5},{5,4},{6,7},{7,6},{8,9},{9,8},{10,11... | collective-permute-start | bytes 12296 | tf_op jit(solution)/shard_map/ppermute | solution.py:427

commit v8 on v7

--- a/solution.py
+++ b/solution.py
@@ -308,7 +308,7 @@
 
 def grid_kernel(x_ref, table_ref, weight_ref, norm_ref, out_ref, turned_ref, wide_ref):
     count, lons = table_ref.shape
-    step = 256
+    step = 640
     turned_ref[...] = x_ref[...].T
     energy = jnp.zeros((SUB, step), F32)
     for first in range(0, lons, step):
@@ -350,7 +350,7 @@
 
 def exchange(payload, parts):
     rows = payload.shape[0]
-    packed = payload.reshape(parts, rows // parts // 2, 2, LANES)
+    packed = payload.reshape(parts, rows // parts // 4, 4, LANES)
     return lax.all_to_all(packed, BAND, 0, 0, tiled=True).reshape(rows, LANES)
 
 

time: 164 us -> 164 us (level)
  no operation moved by 1% of the time
where the time goes in v8:
time: 164 us
  blocking collectives  122 us (74%)
  Pallas kernels  25.4 us (15%)
  starting transfers between devices  14.9 us (9%)
    all_to_all x6, blocking collectives, exchange(): return lax.all_to_all(packed, BAND, 0, 0, tiled=True).reshape(rows, LANES)  122 us
    ppermute x9, starting transfers between devices, reach(): lax.ppermute(sums, 'x', [(i, i ^ k) for i in range(XS)])  10 us
    pallas_call x3, Pallas kernels, reach(): call(functools.partial(back_kernel, slots, chunk_rows), 'back', [vec_shap...  9.53 us
    ppermute x3, starting transfers between devices, on_device(): near.append(lax.ppermute(obs_weight, ('y', 'c'), pairs))  4.92 us
    pallas_call x3, Pallas kernels, reach(): call(grid_kernel, 'grid', [payload_shape], [vmem] * 4, [pltpu.VMEM((LANES...  4.78 us
    pallas_call x1, Pallas kernels, on_device(): call(functools.partial(fourier_kernel, chunk_rows, slots, 1.0 / math.sqrt...  3.47 us
    pallas_call x2, Pallas kernels, on_device(): call(functools.partial(middle_kernel, stage, slots, chunk_rows), f'middle...  3.33 us
  transfers between devices with their start and end apart: 12, of which 0 were waited for; matrix products, arithmetic and copies ran while one was open for 0% of the time, Pallas kernels for 9%

profile of v8, /device:TPU:1, one launch (start us, length us, event | category | flops | bytes accessed | tf_op | source)
XLA Modules:
  0.0 164.0 jit_solution(2915804994353056260)
XLA Ops:
  0.6 0.0 copy-start
  0.6 0.0 slice-start
  0.7 2.2 %collective-permute-start.1 = (f32[10,1280]{1,0:T(8,128)}, f32[10,1280]{1,0:T(8,128)S(1)}, u32[]{:S(2)}, u32[]{:S(2)}) collective-permute-start(f32[10,1280]{1,0:T(8,128)} %refs_0_.1), channel_id=1, source_target_pairs={{0,8},{4,12},{8,0},{12,4},{16,24},{20,28},{24,16},{28,20},{1,9},{5... | collective-permute-start | bytes 153608 | tf_op jit(solution)/shard_map/ppermute | solution.py:406
  2.9 1.2 collective-permute-start
  4.0 1.5 collective-permute-start.2
  5.6 0.0 copy-start.1
  5.6 0.7 copy-done.1
  6.3 0.0 slice-start.1
  6.3 0.0 copy-start.3
  6.3 3.5 %fourier.1.table_ref = bf16[1280,1280]{1,0:T(8,128)(2,1)S(1)} custom-call(s32[5,128]{1,0:T(8,128)S(1)} %bitcast.34), custom_call_target="tpu_custom_call" | custom-call | flops 4000000000 | bytes 1000000 | tf_op jit(solution)/shard_map/fourier/pallas_call | solution.py:385
  9.7 0.0 copy-done
  9.7 0.0 slice-done
  9.8 0.0 slice-done.1
  9.8 2.2 %first.1 = (f32[10,24,640]{2,1,0:T(8,128)S(1)}, bf16[1280,128]{1,0:T(8,128)(2,1)S(1)}, f32[8,128]{1,0:T(8,128)S(1)}) custom-call(s32[640]{0:T(1024)S(1)} %copy-done.1, f32[1200,128]{1,0:T(8,128)S(1)} %bitcast.18, bf16[10,640,640]{2,1,0:T(8,128)(2,1)S(1)} %bitcast.17), custom_call_target="tpu_custom_call" | custom-call | flops 2000000000 | bytes 1000000 | tf_op jit(solution)/shard_map/first/pallas_call | solution.py:395
  12.0 0.0 collective-permute-done.1.refs_2_
  12.0 0.0 collective-permute-done.refs_1_
  12.0 0.0 collective-permute-done.2.refs_3_
  12.0 0.0 copy-done.3
  12.0 0.1 weight.1.weight_ref
  12.1 0.0 copy-start.2
  12.1 24.5 %all_to_all.30 = bf16[64,5,4,128]{3,2,1,0:T(4,128)(2,1)S(1)} all-to-all(bf16[64,5,4,128]{3,2,1,0:T(4,128)(2,1)S(1)} %bitcast.19), channel_id=1, replica_groups=mesh['z'=8,'y'=4,'c'=2,'x'=4] {'z','y','c'}, dimensions={0} | all-to-all | bytes 655360 | tf_op jit(solution)/shard_map/all_to_all | solution.py:354
  36.5 1.6 grid.3
  38.1 19.0 %all_to_all.31 = bf16[64,5,4,128]{3,2,1,0:T(4,128)(2,1)S(1)} all-to-all(bf16[64,5,4,128]{3,2,1,0:T(4,128)(2,1)S(1)} %bitcast.31), channel_id=1, replica_groups=mesh['z'=8,'y'=4,'c'=2,'x'=4] {'z','y','c'}, dimensions={0} | all-to-all | bytes 655360 | tf_op jit(solution)/shard_map/all_to_all | solution.py:354
  57.2 0.2 tail.3.refs_0_
  57.3 2.6 %collective-permute-start.5 = (f32[8,128]{1,0:T(8,128)S(1)}, f32[8,128]{1,0:T(8,128)S(1)}, u32[]{:S(2)}, u32[]{:S(2)}) collective-permute-start(f32[8,128]{1,0:T(8,128)S(1)} %tail.3.refs_0_), channel_id=1, source_target_pairs={{0,3},{1,2},{2,1},{3,0},{4,7},{5,6},{6,5},{7,4},{8,11},{9,10},{10,... | collective-permute-start | bytes 12296 | tf_op jit(solution)/shard_map/ppermute | solution.py:427
  59.9 0.5 collective-permute-start.4
  60.4 0.2 collective-permute-start.3
  60.7 0.0 copy-done.2
  60.7 3.2 %back.3.refs_5_ = f32[10,24,640]{2,1,0:T(8,128)S(1)} custom-call(s32[640]{0:T(1024)S(1)} %copy-done.2, bf16[1280,128]{1,0:T(8,128)(2,1)S(1)} %bitcast.21, bf16[10,640,640]{2,1,0:T(8,128)(2,1)S(1)} %bitcast.17), custom_call_target="tpu_custom_call" | custom-call | flops 8000000000 | bytes 1000000 | tf_op jit(solution)/shard_map/back/pallas_call | solution.py:428
  63.9 0.0 collective-permute-done.5.refs_3_
  63.9 0.0 collective-permute-done.4.refs_2_
  63.9 0.0 collective-permute-done.3.refs_1_
  63.9 1.6 middle0.1
  65.5 20.4 %all_to_all.32 = bf16[64,5,4,128]{3,2,1,0:T(4,128)(2,1)S(1)} all-to-all(bf16[64,5,4,128]{3,2,1,0:T(4,128)(2,1)S(1)} %bitcast.27), channel_id=1, replica_groups=mesh['z'=8,'y'=4,'c'=2,'x'=4] {'z','y','c'}, dimensions={0} | all-to-all | bytes 655360 | tf_op jit(solution)/shard_map/all_to_all | solution.py:354
  86.0 1.6 grid.4
  87.5 19.0 %all_to_all.33 = bf16[64,5,4,128]{3,2,1,0:T(4,128)(2,1)S(1)} all-to-all(bf16[64,5,4,128]{3,2,1,0:T(4,128)(2,1)S(1)} %bitcast.33), channel_id=1, replica_groups=mesh['z'=8,'y'=4,'c'=2,'x'=4] {'z','y','c'}, dimensions={0} | all-to-all | bytes 655360 | tf_op jit(solution)/shard_map/all_to_all | solution.py:354
  106.6 0.2 tail.4.refs_0_
  106.8 2.0 %collective-permute-start.8 = (f32[8,128]{1,0:T(8,128)S(1)}, f32[8,128]{1,0:T(8,128)S(1)}, u32[]{:S(2)}, u32[]{:S(2)}) collective-permute-start(f32[8,128]{1,0:T(8,128)S(1)} %tail.4.refs_0_), channel_id=1, source_target_pairs={{0,3},{1,2},{2,1},{3,0},{4,7},{5,6},{6,5},{7,4},{8,11},{9,10},{10,... | collective-permute-start | bytes 12296 | tf_op jit(solution)/shard_map/ppermute | solution.py:427
  108.8 0.5 collective-permute-start.7
  109.3 0.8 collective-permute-start.6
  110.1 3.2 %back.4.refs_5_ = f32[10,24,640]{2,1,0:T(8,128)S(1)} custom-call(s32[640]{0:T(1024)S(1)} %copy-done.2, bf16[1280,128]{1,0:T(8,128)(2,1)S(1)} %bitcast.23, bf16[10,640,640]{2,1,0:T(8,128)(2,1)S(1)} %bitcast.17), custom_call_target="tpu_custom_call" | custom-call | flops 8000000000 | bytes 1000000 | tf_op jit(solution)/shard_map/back/pallas_call | solution.py:428
  113.3 0.0 collective-permute-done.8.refs_3_
  113.3 0.0 collective-permute-done.7.refs_2_
  113.3 0.0 collective-permute-done.6.refs_1_
  113.3 1.7 %middle1.1 = (f32[10,24,640]{2,1,0:T(8,128)S(1)}, f32[10,24,640]{2,1,0:T(8,128)S(1)}, bf16[1280,128]{1,0:T(8,128)(2,1)S(1)}, f32[8,128]{1,0:T(8,128)S(1)}, f32[8,128]{1,0:T(8,128)S(1)}) custom-call(f32[8,128]{1,0:T(8,128)S(1)} %tail.4.refs_0_, f32[8,128]{1,0:T(8,128)S(1)} %collective-permute-done.6.refs_1_, f32[8,128]{1,0:T(8,128)S(1)} %collective-permute-done.7.refs_2_, ...), custom_call_target="tpu_custom_call" | custom-call | flops 2000000000 | bytes 1000000 | tf_op jit(solution)/shard_map/middle1/pallas_call | solution.py:443
  115.0 19.9 %all_to_all.34 = bf16[64,5,4,128]{3,2,1,0:T(4,128)(2,1)S(1)} all-to-all(bf16[64,5,4,128]{3,2,1,0:T(4,128)(2,1)S(1)} %bitcast.26), channel_id=1, replica_groups=mesh['z'=8,'y'=4,'c'=2,'x'=4] {'z','y','c'}, dimensions={0} | all-to-all | bytes 655360 | tf_op jit(solution)/shard_map/all_to_all | solution.py:354
  134.9 1.6 grid.5
  136.5 19.0 %all_to_all.35 = bf16[64,5,4,128]{3,2,1,0:T(4,128)(2,1)S(1)} all-to-all(bf16[64,5,4,128]{3,2,1,0:T(4,128)(2,1)S(1)} %bitcast.29), channel_id=1, replica_groups=mesh['z'=8,'y'=4,'c'=2,'x'=4] {'z','y','c'}, dimensions={0} | all-to-all | bytes 655360 | tf_op jit(solution)/shard_map/all_to_all | solution.py:354
  155.6 0.2 tail.5.refs_0_
  155.7 2.0 %collective-permute-start.11 = (f32[8,128]{1,0:T(8,128)S(1)}, f32[8,128]{1,0:T(8,128)S(1)}, u32[]{:S(2)}, u32[]{:S(2)}) collective-permute-start(f32[8,128]{1,0:T(8,128)S(1)} %tail.5.refs_0_), channel_id=1, source_target_pairs={{0,3},{1,2},{2,1},{3,0},{4,7},{5,6},{6,5},{7,4},{8,11},{9,10},{10,... | collective-permute-start | bytes 12296 | tf_op jit(solution)/shard_map/ppermute | solution.py:427
  157.7 0.5 collective-permute-start.10
  158.3 0.8 collective-permute-start.9
  159.1 3.2 %back.5.refs_4_ = f32[10,24,640]{2,1,0:T(8,128)S(1)} custom-call(s32[640]{0:T(1024)S(1)} %copy-done.2, bf16[1280,128]{1,0:T(8,128)(2,1)S(1)} %bitcast.25, bf16[10,640,640]{2,1,0:T(8,128)(2,1)S(1)} %bitcast.17), custom_call_target="tpu_custom_call" | custom-call | flops 8000000000 | bytes 1000000 | tf_op jit(solution)/shard_map/back/pallas_call | solution.py:428
  162.2 0.0 collective-permute-done.11.refs_3_
  162.3 0.0 collective-permute-done.10.refs_2_
  162.3 0.0 collective-permute-done.9.refs_1_
  162.3 1.5 last.1
  (1 shorter events, 0.0 us)
Async XLA Ops:
  0.6 9.1 %copy-start = (f32[10,2,1,12,640]{4,2,3,1,0:T(1,128)S(1)}, f32[10,2,1,12,640]{4,2,3,1,0:T(1,128)}, u32[]{:S(2)}) copy-start(f32[10,2,1,12,640]{4,2,3,1,0:T(1,128)} %param.4) | copy-start | bytes 1843204
  0.6 9.1 %slice-start = ((s8[8192000]{0:T(1024)(128)(4,1)}), s8[4194304]{0:T(1024)(128)(4,1)S(1)}, s32[]{:S(2)}) async-start(s8[8192000]{0:T(1024)(128)(4,1)} %bitcast.16), calls=%async_computation.6 | async-start | bytes 8388608
  0.7 11.3 %collective-permute-start.1 = (f32[10,1280]{1,0:T(8,128)}, f32[10,1280]{1,0:T(8,128)S(1)}, u32[]{:S(2)}, u32[]{:S(2)}) collective-permute-start(f32[10,1280]{1,0:T(8,128)} %refs_0_.1), channel_id=1, source_target_pairs={{0,8},{4,12},{8,0},{12,4},{16,24},{20,28},{24,16},{28,20},{1,9},{5... | collective-permute-start | bytes 153608 | tf_op jit(solution)/shard_map/ppermute | solution.py:406
  2.9 9.1 %collective-permute-start = (f32[10,1280]{1,0:T(8,128)}, f32[10,1280]{1,0:T(8,128)S(1)}, u32[]{:S(2)}, u32[]{:S(2)}) collective-permute-start(f32[10,1280]{1,0:T(8,128)} %refs_0_.1), channel_id=1, source_target_pairs={{0,4},{4,0},{8,12},{12,8},{16,20},{20,16},{24,28},{28,24},{1,5},{5... | collective-permute-start | bytes 153608 | tf_op jit(solution)/shard_map/ppermute | solution.py:406
  4.0 7.9 %collective-permute-start.2 = (f32[10,1280]{1,0:T(8,128)}, f32[10,1280]{1,0:T(8,128)S(1)}, u32[]{:S(2)}, u32[]{:S(2)}) collective-permute-start(f32[10,1280]{1,0:T(8,128)} %refs_0_.1), channel_id=1, source_target_pairs={{0,12},{4,8},{8,4},{12,0},{16,28},{20,24},{24,20},{28,16},{1,13},{... | collective-permute-start | bytes 153608 | tf_op jit(solution)/shard_map/ppermute | solution.py:406
  5.6 0.7 copy-start.1
  6.3 3.5 %slice-start.1 = ((s8[8192000]{0:T(1024)(128)(4,1)}), s8[3997696]{0:T(1024)(128)(4,1)S(1)}, s32[]{:S(2)}) async-start(s8[8192000]{0:T(1024)(128)(4,1)} %bitcast.16), calls=%async_computation.7 | async-start | bytes 7995392
  6.3 5.7 %copy-start.3 = (f32[10,1280]{1,0:T(8,128)S(1)}, f32[10,1280]{1,0:T(8,128)}, u32[]{:S(2)}) copy-start(f32[10,1280]{1,0:T(8,128)} %refs_0_.1) | copy-start | bytes 153604
  12.1 48.6 %copy-start.2 = (s32[640]{0:T(1024)S(1)}, s32[640]{0:T(1024)}, u32[]{:S(2)}) copy-start(s32[640]{0:T(1024)} %waves_ref.7) | copy-start | bytes 7684
  57.3 6.5 %collective-permute-start.5 = (f32[8,128]{1,0:T(8,128)S(1)}, f32[8,128]{1,0:T(8,128)S(1)}, u32[]{:S(2)}, u32[]{:S(2)}) collective-permute-start(f32[8,128]{1,0:T(8,128)S(1)} %tail.3.refs_0_), channel_id=1, source_target_pairs={{0,3},{1,2},{2,1},{3,0},{4,7},{5,6},{6,5},{7,4},{8,11},{9,10},{10,... | collective-permute-start | bytes 12296 | tf_op jit(solution)/shard_map/ppermute | solution.py:427
  59.9 4.0 %collective-permute-start.4 = (f32[8,128]{1,0:T(8,128)S(1)}, f32[8,128]{1,0:T(8,128)S(1)}, u32[]{:S(2)}, u32[]{:S(2)}) collective-permute-start(f32[8,128]{1,0:T(8,128)S(1)} %tail.3.refs_0_), channel_id=1, source_target_pairs={{0,2},{1,3},{2,0},{3,1},{4,6},{5,7},{6,4},{7,5},{8,10},{9,11},{10,... | collective-permute-start | bytes 12296 | tf_op jit(solution)/shard_map/ppermute | solution.py:427
  60.4 3.5 %collective-permute-start.3 = (f32[8,128]{1,0:T(8,128)S(1)}, f32[8,128]{1,0:T(8,128)S(1)}, u32[]{:S(2)}, u32[]{:S(2)}) collective-permute-start(f32[8,128]{1,0:T(8,128)S(1)} %tail.3.refs_0_), channel_id=1, source_target_pairs={{0,1},{1,0},{2,3},{3,2},{4,5},{5,4},{6,7},{7,6},{8,9},{9,8},{10,11... | collective-permute-start | bytes 12296 | tf_op jit(solution)/shard_map/ppermute | solution.py:427
  106.8 6.5 %collective-permute-start.8 = (f32[8,128]{1,0:T(8,128)S(1)}, f32[8,128]{1,0:T(8,128)S(1)}, u32[]{:S(2)}, u32[]{:S(2)}) collective-permute-start(f32[8,128]{1,0:T(8,128)S(1)} %tail.4.refs_0_), channel_id=1, source_target_pairs={{0,3},{1,2},{2,1},{3,0},{4,7},{5,6},{6,5},{7,4},{8,11},{9,10},{10,... | collective-permute-start | bytes 12296 | tf_op jit(solution)/shard_map/ppermute | solution.py:427
  108.8 4.5 %collective-permute-start.7 = (f32[8,128]{1,0:T(8,128)S(1)}, f32[8,128]{1,0:T(8,128)S(1)}, u32[]{:S(2)}, u32[]{:S(2)}) collective-permute-start(f32[8,128]{1,0:T(8,128)S(1)} %tail.4.refs_0_), channel_id=1, source_target_pairs={{0,2},{1,3},{2,0},{3,1},{4,6},{5,7},{6,4},{7,5},{8,10},{9,11},{10,... | collective-permute-start | bytes 12296 | tf_op jit(solution)/shard_map/ppermute | solution.py:427
  109.3 4.0 %collective-permute-start.6 = (f32[8,128]{1,0:T(8,128)S(1)}, f32[8,128]{1,0:T(8,128)S(1)}, u32[]{:S(2)}, u32[]{:S(2)}) collective-permute-start(f32[8,128]{1,0:T(8,128)S(1)} %tail.4.refs_0_), channel_id=1, source_target_pairs={{0,1},{1,0},{2,3},{3,2},{4,5},{5,4},{6,7},{7,6},{8,9},{9,8},{10,11... | collective-permute-start | bytes 12296 | tf_op jit(solution)/shard_map/ppermute | solution.py:427
  155.7 6.5 %collective-permute-start.11 = (f32[8,128]{1,0:T(8,128)S(1)}, f32[8,128]{1,0:T(8,128)S(1)}, u32[]{:S(2)}, u32[]{:S(2)}) collective-permute-start(f32[8,128]{1,0:T(8,128)S(1)} %tail.5.refs_0_), channel_id=1, source_target_pairs={{0,3},{1,2},{2,1},{3,0},{4,7},{5,6},{6,5},{7,4},{8,11},{9,10},{10,... | collective-permute-start | bytes 12296 | tf_op jit(solution)/shard_map/ppermute | solution.py:427
  157.7 4.5 %collective-permute-start.10 = (f32[8,128]{1,0:T(8,128)S(1)}, f32[8,128]{1,0:T(8,128)S(1)}, u32[]{:S(2)}, u32[]{:S(2)}) collective-permute-start(f32[8,128]{1,0:T(8,128)S(1)} %tail.5.refs_0_), channel_id=1, source_target_pairs={{0,2},{1,3},{2,0},{3,1},{4,6},{5,7},{6,4},{7,5},{8,10},{9,11},{10,... | collective-permute-start | bytes 12296 | tf_op jit(solution)/shard_map/ppermute | solution.py:427
  158.3 4.0 %collective-permute-start.9 = (f32[8,128]{1,0:T(8,128)S(1)}, f32[8,128]{1,0:T(8,128)S(1)}, u32[]{:S(2)}, u32[]{:S(2)}) collective-permute-start(f32[8,128]{1,0:T(8,128)S(1)} %tail.5.refs_0_), channel_id=1, source_target_pairs={{0,1},{1,0},{2,3},{3,2},{4,5},{5,4},{6,7},{7,6},{8,9},{9,8},{10,11... | collective-permute-start | bytes 12296 | tf_op jit(solution)/shard_map/ppermute | solution.py:427
